TPU v7x, 16 devices: a 4x2x1 block of a 4x4x8 slice. The times are simulated.
16 devices in a mesh: dp: 2 (over y, z), ep: 8 (over x, core).
Axes of the slice: x: 4, y: 2, z: 1, core: 2. Of those that a mesh axis runs over, the one named last changes fastest.
The devices are a block of a 4x4x8 slice.
Arguments:
- tokens: bfloat16 [2048, 1536], P(('dp', 'ep')), parts along dimension 0
- expert_ids: int32 [2048, 8], P(('dp', 'ep')), parts along dimension 0
- gate_vals: float32 [2048, 8], P(('dp', 'ep')), parts along dimension 0
- w_gate: bfloat16 [40, 1536, 512], P('ep')
- w_up: bfloat16 [40, 1536, 512], P('ep')
- w_down: bfloat16 [40, 512, 1536], P('ep')
- grad_out: bfloat16 [2048, 1536], P(('dp', 'ep')), parts along dimension 0
Outputs:
- output 1: bfloat16 [2048, 1536], P(('dp', 'ep')), parts along dimension 0
- output 2: bfloat16 [2048, 1536], P(('dp', 'ep')), parts along dimension 0
- output 3: bfloat16 [80, 1536, 512], P(('dp', 'ep')), parts along dimension 0
- output 4: bfloat16 [80, 1536, 512], P(('dp', 'ep')), parts along dimension 0
- output 5: bfloat16 [80, 512, 1536], P(('dp', 'ep')), parts along dimension 0
There are 2 independent parts. A program takes and returns all parts, laid end to end along the dimension named above; an argument that names none is the same for every part.
All inputs are finite; a program needn't handle non-finite values.
Results may differ from a plain program's by a relative error of at most 0.00147.
Values are sent between devices in bfloat16 or wider.
A program may use at most 768 MiB of HBM per device.

v0:
```python
import jax
import jax.numpy as jnp
from jax import lax
from jax.sharding import PartitionSpec as P


def slot_positions(expert_ids, num_experts, capacity, hot_expert):
    flat_ids = expert_ids.reshape(-1)
    onehot = (flat_ids[:, None] == jnp.arange(num_experts)[None, :]).astype(jnp.int32)
    slot_rank = jnp.sum((jnp.cumsum(onehot, axis=0) - onehot) * onehot, axis=1)
    return jnp.where(flat_ids == hot_expert, num_experts * capacity + slot_rank, flat_ids * capacity + slot_rank)


def scatter_rows(row_vals, buf_pos, buf_rows):
    return jnp.zeros((buf_rows, row_vals.shape[-1]), row_vals.dtype).at[buf_pos].set(row_vals, unique_indices=True)


def expert_forward(in_rows, gate_w, up_w, down_w):
    act_a = jnp.einsum("secd,edf->secf", in_rows, gate_w, preferred_element_type=jnp.float32)
    act_b = jnp.einsum("secd,edf->secf", in_rows, up_w, preferred_element_type=jnp.float32)
    hidden = (act_a * jax.nn.sigmoid(act_a) * act_b).astype(jnp.bfloat16)
    expert_out = jnp.einsum("secf,efd->secd", hidden, down_w, preferred_element_type=jnp.float32).astype(jnp.bfloat16)
    return act_a, act_b, hidden, expert_out


def expert_backward(in_rows, saved_acts, d_out_rows, gate_w, up_w, down_w):
    act_a, act_b, hidden = saved_acts[0], saved_acts[1], saved_acts[2]
    d_hidden = jnp.einsum("secd,efd->secf", d_out_rows, down_w, preferred_element_type=jnp.float32)
    sig_a = jax.nn.sigmoid(act_a)
    d_act_a = (d_hidden * act_b * sig_a * (1.0 + act_a * (1.0 - sig_a))).astype(jnp.bfloat16)
    d_act_b = (d_hidden * act_a * sig_a).astype(jnp.bfloat16)
    d_in_rows = (jnp.einsum("secf,edf->secd", d_act_a, gate_w, preferred_element_type=jnp.float32) + jnp.einsum("secf,edf->secd", d_act_b, up_w, preferred_element_type=jnp.float32)).astype(jnp.bfloat16)
    grad_gate = jnp.einsum("secd,secf->edf", in_rows, d_act_a, preferred_element_type=jnp.float32)
    grad_up = jnp.einsum("secd,secf->edf", in_rows, d_act_b, preferred_element_type=jnp.float32)
    grad_down = jnp.einsum("secf,secd->efd", hidden, d_out_rows, preferred_element_type=jnp.float32)
    return d_in_rows, (grad_gate, grad_up, grad_down)


def solution(mesh):
    group_size = mesh.shape["ep"]
    num_chips = mesh.shape["dp"] * group_size
    tok_spec = P(("dp", "ep"), None)
    w_spec = P("ep", None, None)
    grad_spec = P(("dp", "ep"), None, None)

    def layer_fn(tokens, expert_ids, gate_vals, w_gate, w_up, w_down, grad_out):
        num_experts = w_gate.shape[0]
        tok_dev = tokens.shape[0] // num_chips
        top_k = expert_ids.shape[1]
        capacity = ((2 * tok_dev * top_k + 8 * num_experts - 1) // (8 * num_experts)) * 8
        hot_expert = num_experts // 2
        local_experts = num_experts // group_size
        owner_dev = hot_expert // local_experts
        hot_local = hot_expert % local_experts
        cold_rows = num_experts * capacity

        def device_fn(tok_rows, route_ids, route_gates, gate_w, up_w, down_w, dy_rows):
            row_width = tok_rows.shape[1]
            is_owner = lax.axis_index("ep") == owner_dev
            buf_pos = slot_positions(route_ids, num_experts, capacity, hot_expert)
            tok_rep = jnp.broadcast_to(tok_rows[:, None, :], (tok_dev, top_k, row_width)).reshape(tok_dev * top_k, row_width)
            d_rep = (route_gates[:, :, None] * dy_rows[:, None, :].astype(jnp.float32)).astype(jnp.bfloat16).reshape(tok_dev * top_k, row_width)
            send_x = scatter_rows(tok_rep, buf_pos, cold_rows + tok_dev)
            send_d = scatter_rows(d_rep, buf_pos, cold_rows + tok_dev)
            cold_shape = (group_size, local_experts, capacity, row_width)
            hot_gate = gate_w[hot_local:hot_local + 1]
            hot_up = up_w[hot_local:hot_local + 1]
            hot_down = down_w[hot_local:hot_local + 1]

            cold_x = lax.all_to_all(send_x[:cold_rows].reshape(cold_shape), "ep", 0, 0)
            hot_x = lax.all_gather(send_x[cold_rows:], "ep")[:, None]
            cold_acts = expert_forward(cold_x, gate_w, up_w, down_w)
            hot_acts = expert_forward(hot_x, hot_gate, hot_up, hot_down)
            cold_back = lax.all_to_all(cold_acts[3], "ep", 0, 0).reshape(cold_rows, row_width)
            hot_back = lax.all_to_all(hot_acts[3][:, 0], "ep", 0, 0)[owner_dev]
            y_rows = jnp.concatenate([cold_back, hot_back], axis=0)[buf_pos].reshape(tok_dev, top_k, row_width)
            moe_out = jnp.sum(route_gates[:, :, None] * y_rows.astype(jnp.float32), axis=1).astype(jnp.bfloat16)

            cold_d = lax.all_to_all(send_d[:cold_rows].reshape(cold_shape), "ep", 0, 0)
            hot_d = lax.all_gather(send_d[cold_rows:], "ep")[:, None]
            cold_dx, cold_grads = expert_backward(cold_x, cold_acts, cold_d, gate_w, up_w, down_w)
            hot_dx, hot_grads = expert_backward(hot_x, hot_acts, hot_d, hot_gate, hot_up, hot_down)
            cold_dx_back = lax.all_to_all(cold_dx, "ep", 0, 0).reshape(cold_rows, row_width)
            hot_dx_back = lax.all_to_all(hot_dx[:, 0], "ep", 0, 0)[owner_dev]
            dx_rows = jnp.concatenate([cold_dx_back, hot_dx_back], axis=0)[buf_pos].reshape(tok_dev, top_k, row_width)
            grad_tokens = jnp.sum(dx_rows.astype(jnp.float32), axis=1).astype(jnp.bfloat16)
            grad_list = [cold_g.at[hot_local].add(jnp.where(is_owner, hot_g[0], 0.0)).astype(jnp.bfloat16) for cold_g, hot_g in zip(cold_grads, hot_grads)]
            return moe_out, grad_tokens, grad_list[0], grad_list[1], grad_list[2]

        return jax.shard_map(device_fn, mesh=mesh, in_specs=(tok_spec, tok_spec, tok_spec, w_spec, w_spec, w_spec, tok_spec), out_specs=(tok_spec, tok_spec, grad_spec, grad_spec, grad_spec), check_vma=False)(tokens, expert_ids, gate_vals, w_gate, w_up, w_down, grad_out)

    return layer_fn
```

profile of v0, /device:TPU:112, one launch (start us, length us, event | category | flops | bytes accessed | tf_op | source)
XLA Modules:
  0.0 509.8 jit_solution(17229647247296511590)
XLA Ops:
  10.1 11.3 %reduce-window.6 = s32[40,8,128]{2,1,0:T(8,128)S(1)} reduce-window(s32[40,8,128]{2,1,0:T(8,128)S(1)} %fusion.91, s32[]{:T(128)} %constant.87.clone.1), window={size=1x1x128 pad=0_0x0_0x127_0}, to_apply=%region_0.0 | reduce-window | flops 5201920 | bytes 327684 | tf_op jit(solution)/shard_map/reduce-window | solution.py:90
  22.0 9.8 %scatter_custom_fusion = bf16[2368,1536]{1,0:T(8,128)(2,1)} fusion(s32[1024]{0:T(1024)S(1)} %bitcast.280, bf16[]{:T(256)} %constant.85.clone.1, bf16[128,1536]{1,0:T(8,128)(2,1)S(1)} %copy-done), kind=kCustom, calls=%fused_computation.52 | custom fusion | bytes 7667714 | tf_op jit(solution)/shard_map/scatter | solution.py:15
  31.8 1.8 slice.120
  33.9 10.4 %scatter_custom_fusion.1 = bf16[2368,1536]{1,0:T(8,128)(2,1)} fusion(s32[1024]{0:T(1024)S(1)} %bitcast.281, bf16[]{:T(256)} %constant.85.clone.1, f32[128,1536]{1,0:T(8,128)S(1)} %convert_element_type.87, f32[1024]{0:T(1024)S(1)} %mul.103), kind=kCustom, calls=%fused_computation.50 | custom fusion | flops 3145728 | bytes 8065026 | tf_op jit(solution)/shard_map/scatter | solution.py:15
  44.3 6.3 %slice.122 = bf16[2240,1536]{1,0:T(8,128)(2,1)} slice(bf16[2368,1536]{1,0:T(8,128)(2,1)} %scatter_custom_fusion.1), slice={[0:2240], [0:1536]} | slice | bytes 13762560 | tf_op jit(solution)/shard_map/slice | solution.py:79
  50.6 5.3 %all-to-all-start.3 = ((bf16[8,5,56,1536]{3,2,1,0:T(8,128)(2,1)}), bf16[8,5,56,1536]{3,2,1,0:T(8,128)(2,1)}, u32[]{:S(2)}, u32[]{:S(2)}) async-start(bf16[8,5,56,1536]{3,2,1,0:T(8,128)(2,1)} %bitcast.273), calls=%async_computation.3 | async-start | bytes 13762560 | tf_op jit(solution)/shard_map/all_to_all | solution.py:79
  56.0 1.8 slice.123
  57.8 6.3 %slice.119 = bf16[2240,1536]{1,0:T(8,128)(2,1)} slice(bf16[2368,1536]{1,0:T(8,128)(2,1)} %scatter_custom_fusion), slice={[0:2240], [0:1536]} | slice | bytes 13762560 | tf_op jit(solution)/shard_map/slice | solution.py:70
  64.1 82.9 %all-to-all-done.3 = bf16[8,5,56,1536]{3,2,1,0:T(8,128)(2,1)} async-done(((bf16[8,5,56,1536]{3,2,1,0:T(8,128)(2,1)}), bf16[8,5,56,1536]{3,2,1,0:T(8,128)(2,1)}, u32[]{:S(2)}, u32[]{:S(2)}) %all-to-all-start.3) | async-done | bytes 6881312 | tf_op jit(solution)/shard_map/all_to_all | solution.py:79
  147.0 5.0 all-to-all-start
  152.1 4.3 fusion.69
  156.4 4.5 fusion.73
  160.9 6.6 %fusion.59 = (bf16[8,1,128,512]{3,2,0,1:T(8,128)(2,1)}, bf16[8,1,128,512]{3,2,0,1:T(8,128)(2,1)S(1)}, bf16[8,1,128,512]{3,2,0,1:T(8,128)(2,1)S(1)}) fusion(f32[8,128,512]{2,1,0:T(8,128)} %fusion.73, f32[8,128,512]{2,1,0:T(8,128)S(1)} %fusion.69, bf16[8,128,1536]{2,1,0:T(8,128)(2,1)} %bitcast.276, bf16[5,512,1536]{2,1,0:T(8,128)(2,1)} %param.18), kind=kOutput, calls=%fused_computation.81 | convolution fusion | flops 1619001344 | bytes 12058624 | tf_op jit(solution)/shard_map/secd,efd->secf/dot_general | solution.py:28
  167.5 1.0 copy-done.8
  168.5 4.9 convolution_convert_fusion
  173.4 5.9 %fusion.71 = f32[8,128,1536]{2,1,0:T(8,128)} fusion(bf16[5,1536,512]{2,1,0:T(8,128)(2,1)} %param.16, bf16[8,1,128,512]{3,2,0,1:T(8,128)(2,1)S(1)} %get-tuple-element.45), kind=kOutput, calls=%fused_computation.97 | convolution fusion | flops 1610612736 | bytes 8912896 | tf_op jit(solution)/shard_map/secf,edf->secd/dot_general | solution.py:32
  179.3 50.9 %all-to-all-done = bf16[8,5,56,1536]{3,2,1,0:T(8,128)(2,1)} async-done(((bf16[8,5,56,1536]{3,2,1,0:T(8,128)(2,1)}), bf16[8,5,56,1536]{3,2,1,0:T(8,128)(2,1)}, u32[]{:S(2)}, u32[]{:S(2)}) %all-to-all-start) | async-done | bytes 6881312 | tf_op jit(solution)/shard_map/all_to_all | solution.py:70
  230.2 4.3 all-to-all-start.2
  234.5 7.2 %add_convert_fusion.1 = bf16[8,128,1536]{2,1,0:T(8,128)(2,1)} fusion(f32[8,128,1536]{2,1,0:T(8,128)} %fusion.71, bf16[5,1536,512]{2,1,0:T(8,128)(2,1)} %param.17, bf16[8,1,128,512]{3,2,0,1:T(8,128)(2,1)} %get-tuple-element.44), kind=kOutput, calls=%fused_computation.28 | convolution fusion | flops 1613758464 | bytes 12058624 | tf_op jit(solution)/shard_map/secf,edf->secd/dot_general | solution.py:32
  241.7 11.2 %fusion.2 = f32[5,8,56,512]{3,2,1,0:T(8,128)} fusion(bf16[5,1536,512]{2,1,0:T(8,128)(2,1)} %param.17, bf16[8,5,56,1536]{3,2,1,0:T(8,128)(2,1)} %all-to-all-done), kind=kOutput, calls=%fused_computation.7 | convolution fusion | flops 3523215360 | bytes 19333120 | tf_op jit(solution)/shard_map/secd,edf->secf/dot_general | solution.py:20
  252.9 8.4 %fusion.6 = f32[5,8,56,512]{3,2,1,0:T(8,128)} fusion(bf16[5,1536,512]{2,1,0:T(8,128)(2,1)S(1)} %bitcast.275, bf16[8,5,56,1536]{3,2,1,0:T(8,128)(2,1)} %all-to-all-done), kind=kOutput, calls=%fused_computation.11 | convolution fusion | flops 3523215360 | bytes 19333120 | tf_op jit(solution)/shard_map/secd,edf->secf/dot_general | solution.py:19
  261.3 11.4 %all-to-all-done.2 = bf16[8,128,1536]{2,1,0:T(8,128)(2,1)S(1)} async-done(((bf16[8,128,1536]{2,1,0:T(8,128)(2,1)}), bf16[8,128,1536]{2,1,0:T(8,128)(2,1)S(1)}, u32[]{:S(2)}, u32[]{:S(2)}) %all-to-all-start.2) | async-done | bytes 3145760 | tf_op jit(solution)/shard_map/all_to_all | solution.py:75
  272.7 4.6 all-to-all-start.5
  277.4 13.5 %fusion.25 = (bf16[8,5,56,512]{3,2,0,1:T(8,128)(2,1)}, bf16[8,5,56,512]{3,2,0,1:T(8,128)(2,1)}, bf16[8,5,56,512]{3,2,0,1:T(8,128)(2,1)}) fusion(f32[5,8,56,512]{3,2,1,0:T(8,128)} %fusion.2, f32[5,8,56,512]{3,2,1,0:T(8,128)} %fusion.6, bf16[5,512,1536]{2,1,0:T(8,128)(2,1)} %param.18, bf16[8,5,56,1536]{3,2,1,0:T(8,128)(2,1)} %all-to-all-done.3), kind=kOutput, calls=%fused_computation.37 | convolution fusion | flops 3541565440 | bytes 30801920 | tf_op jit(solution)/shard_map/secd,efd->secf/dot_general | solution.py:28
  290.9 7.7 %convert_bitcast_fusion = bf16[8,5,56,1536]{3,2,0,1:T(8,128)(2,1)S(1)} fusion(bf16[8,5,56,512]{3,2,0,1:T(8,128)(2,1)} %get-tuple-element.42, bf16[5,512,1536]{2,1,0:T(8,128)(2,1)} %param.18), kind=kOutput, calls=%fused_computation.23 | convolution fusion | flops 3526656000 | bytes 17039360 | tf_op jit(solution)/shard_map/secf,efd->secd/dot_general | solution.py:22
  298.6 3.4 copy.40
  302.0 13.6 %all-to-all-done.5 = bf16[8,128,1536]{2,1,0:T(8,128)(2,1)} async-done(((bf16[8,128,1536]{2,1,0:T(8,128)(2,1)}), bf16[8,128,1536]{2,1,0:T(8,128)(2,1)}, u32[]{:S(2)}, u32[]{:S(2)}) %all-to-all-start.5) | async-done | bytes 3145760 | tf_op jit(solution)/shard_map/all_to_all | solution.py:84
  315.6 5.2 %all-to-all-start.1 = ((bf16[8,5,56,1536]{3,2,1,0:T(8,128)(2,1)}), bf16[8,5,56,1536]{3,2,1,0:T(8,128)(2,1)}, u32[]{:S(2)}, u32[]{:S(2)}) async-start(bf16[8,5,56,1536]{3,2,1,0:T(8,128)(2,1)} %copy.40), calls=%async_computation.1 | async-start | bytes 13762560 | tf_op jit(solution)/shard_map/all_to_all | solution.py:74
  320.8 10.8 %convolution_bitcast_fusion = f32[5,512,1536]{2,1,0:T(8,128)} fusion(bf16[8,5,56,512]{3,2,0,1:T(8,128)(2,1)S(1)} %copy-done.18, bf16[8,5,56,1536]{3,2,1,0:T(8,128)(2,1)} %all-to-all-done.3), kind=kOutput, calls=%fused_computation.17 | convolution fusion | flops 3523215360 | bytes 24903680 | tf_op jit(solution)/shard_map/secf,secd->efd/dot_general | solution.py:35
  331.6 5.4 %fusion.44 = f32[5,512,1536]{2,1,0:T(8,128)} fusion(f32[5,512,1536]{2,1,0:T(8,128)} %convolution_bitcast_fusion, bf16[8,128,1536]{2,1,0:T(8,128)(2,1)S(1)} %bitcast.277, pred[]{:T(512)S(6)} %eq.55, bf16[8,1,128,512]{3,2,0,1:T(8,128)(2,1)S(1)} %copy-done.9), kind=kOutput, calls=%fused_computation.64 | convolution fusion | flops 1612185600 | bytes 10485761 | tf_op jit(solution)/shard_map/secf,secd->efd/dot_general | solution.py:35
  337.1 9.8 %convert_element_type.98 = bf16[5,512,1536]{2,1,0:T(8,128)(2,1)} convert(f32[5,512,1536]{2,1,0:T(8,128)} %fusion.44) | non-fusion elementwise | flops 3932160 | bytes 23592960 | tf_op jit(solution)/shard_map/convert_element_type | solution.py:87
  346.9 11.0 %fusion = f32[5,8,56,1536]{3,2,1,0:T(8,128)} fusion(bf16[8,5,56,512]{3,2,0,1:T(8,128)(2,1)S(1)} %copy-done.3, bf16[5,1536,512]{2,1,0:T(8,128)(2,1)} %param.17), kind=kOutput, calls=%fused_computation.5 | convolution fusion | flops 3523215360 | bytes 23920640 | tf_op jit(solution)/shard_map/secf,edf->secd/dot_general | solution.py:32
  357.9 9.9 %fusion.12 = bf16[8,5,56,1536]{3,2,0,1:T(8,128)(2,1)S(1)} fusion(f32[5,8,56,1536]{3,2,1,0:T(8,128)} %fusion, bf16[8,5,56,512]{3,2,0,1:T(8,128)(2,1)} %get-tuple-element.41, bf16[5,1536,512]{2,1,0:T(8,128)(2,1)} %param.16), kind=kOutput, calls=%fused_computation.22 | convolution fusion | flops 3530096640 | bytes 30801920 | tf_op jit(solution)/shard_map/secf,edf->secd/dot_general | solution.py:32
  367.8 3.4 copy.43
  371.2 27.8 %all-to-all-done.1 = bf16[8,5,56,1536]{3,2,1,0:T(8,128)(2,1)} async-done(((bf16[8,5,56,1536]{3,2,1,0:T(8,128)(2,1)}), bf16[8,5,56,1536]{3,2,1,0:T(8,128)(2,1)}, u32[]{:S(2)}, u32[]{:S(2)}) %all-to-all-start.1) | async-done | bytes 6881312 | tf_op jit(solution)/shard_map/all_to_all | solution.py:74
  399.0 5.3 %all-to-all-start.4 = ((bf16[8,5,56,1536]{3,2,1,0:T(8,128)(2,1)}), bf16[8,5,56,1536]{3,2,1,0:T(8,128)(2,1)}, u32[]{:S(2)}, u32[]{:S(2)}) async-start(bf16[8,5,56,1536]{3,2,1,0:T(8,128)(2,1)} %copy.43), calls=%async_computation.4 | async-start | bytes 13762560 | tf_op jit(solution)/shard_map/all_to_all | solution.py:83
  404.3 11.8 %convolution_bitcast_fusion.2 = f32[5,1536,512]{2,1,0:T(8,128)} fusion(bf16[8,5,56,1536]{3,2,1,0:T(8,128)(2,1)} %all-to-all-done, bf16[8,5,56,512]{3,2,0,1:T(8,128)(2,1)S(1)} %copy-done.6), kind=kOutput, calls=%fused_computation.19 | convolution fusion | flops 3523215360 | bytes 24903680 | tf_op jit(solution)/shard_map/secd,secf->edf/dot_general | solution.py:33
  416.1 5.4 %fusion.48 = f32[5,1536,512]{2,1,0:T(8,128)} fusion(f32[5,1536,512]{2,1,0:T(8,128)} %convolution_bitcast_fusion.2, bf16[8,128,1536]{2,1,0:T(8,128)(2,1)S(1)} %bitcast.286, pred[]{:T(512)S(6)} %eq.55, bf16[8,1,128,512]{3,2,0,1:T(8,128)(2,1)S(1)} %copy-done.17), kind=kOutput, calls=%fused_computation.68 | convolution fusion | flops 1612185600 | bytes 10485761 | tf_op jit(solution)/shard_map/secd,secf->edf/dot_general | solution.py:33
  421.5 9.8 %convert_element_type.96 = bf16[5,1536,512]{2,1,0:T(8,128)(2,1)} convert(f32[5,1536,512]{2,1,0:T(8,128)} %fusion.48) | non-fusion elementwise | flops 3932160 | bytes 23592960 | tf_op jit(solution)/shard_map/convert_element_type | solution.py:87
  431.4 12.0 %convolution_bitcast_fusion.1 = f32[5,1536,512]{2,1,0:T(8,128)} fusion(bf16[8,5,56,1536]{3,2,1,0:T(8,128)(2,1)} %all-to-all-done, bf16[8,5,56,512]{3,2,0,1:T(8,128)(2,1)S(1)} %copy-done.4), kind=kOutput, calls=%fused_computation.18 | convolution fusion | flops 3523215360 | bytes 24903680 | tf_op jit(solution)/shard_map/secd,secf->edf/dot_general | solution.py:34
  443.4 5.3 %fusion.46 = f32[5,1536,512]{2,1,0:T(8,128)} fusion(f32[5,1536,512]{2,1,0:T(8,128)} %convolution_bitcast_fusion.1, bf16[8,128,1536]{2,1,0:T(8,128)(2,1)S(1)} %bitcast.287, pred[]{:T(512)S(6)} %eq.55, bf16[8,1,128,512]{3,2,0,1:T(8,128)(2,1)S(1)} %copy-done.7), kind=kOutput, calls=%fused_computation.66 | convolution fusion | flops 1612185600 | bytes 10485761 | tf_op jit(solution)/shard_map/secd,secf->edf/dot_general | solution.py:34
  448.8 9.7 %convert_element_type.97 = bf16[5,1536,512]{2,1,0:T(8,128)(2,1)} convert(f32[5,1536,512]{2,1,0:T(8,128)} %fusion.46) | non-fusion elementwise | flops 3932160 | bytes 23592960 | tf_op jit(solution)/shard_map/convert_element_type | solution.py:87
  460.5 6.3 %pad_maximum_fusion = bf16[2368,1536]{1,0:T(8,128)(2,1)} fusion(bf16[128,1536]{1,0:T(8,128)(2,1)S(1)} %slice_bitcast_fusion.1, bf16[2240,1536]{1,0:T(8,128)(2,1)} %bitcast.15), kind=kLoop, calls=%fused_computation.20 | loop fusion | flops 14548992 | bytes 14548992 | tf_op jit(solution)/shard_map/concatenate | solution.py:76
  466.9 10.7 %gather_fusion = bf16[1024,1536]{1,0:T(8,128)(2,1)S(1)} fusion(bf16[2368,1536]{1,0:T(8,128)(2,1)} %pad_maximum_fusion, s32[1024]{0:T(1024)S(1)} %broadcast_clamp_fusion), kind=kCustom, calls=%fused_computation | custom fusion | bytes 6295552 | tf_op jit(solution)/shard_map/gather | solution.py:76
  477.5 4.4 fusion.13
  482.6 6.4 %pad_maximum_fusion.1 = bf16[2368,1536]{1,0:T(8,128)(2,1)} fusion(bf16[128,1536]{1,0:T(8,128)(2,1)S(1)} %slice_bitcast_fusion, bf16[2240,1536]{1,0:T(8,128)(2,1)} %bitcast.41), kind=kLoop, calls=%fused_computation.21 | loop fusion | flops 14548992 | bytes 14548992 | tf_op jit(solution)/shard_map/concatenate | solution.py:85
  488.9 10.7 %gather_fusion.1 = bf16[1024,1536]{1,0:T(8,128)(2,1)S(1)} fusion(bf16[2368,1536]{1,0:T(8,128)(2,1)} %pad_maximum_fusion.1, s32[1024]{0:T(1024)S(1)} %broadcast_clamp_fusion), kind=kCustom, calls=%fused_computation.1 | custom fusion | bytes 6295552 | tf_op jit(solution)/shard_map/gather | solution.py:85
  499.6 2.8 bitcast_reduce_fusion
  (73 shorter events, 6.6 us)
Async XLA Ops:
  7.2 14.8 %copy-start = (bf16[128,1536]{1,0:T(8,128)(2,1)S(1)}, bf16[128,1536]{1,0:T(8,128)(2,1)}, u32[]{:S(2)}) copy-start(bf16[128,1536]{1,0:T(8,128)(2,1)} %param.13) | copy-start | bytes 1179652
  7.2 144.8 %all-gather.5.cloned.1.call-start = ((), (), s32[]{:S(2)}) async-start(), calls=%async_computation.6 | async-start | bytes 3538944 | tf_op jit(solution)/shard_map/all_gather | solution.py:71
  21.9 11.8 %copy-start.12 = (f32[128,8]{0,1:T(8,128)S(1)}, f32[128,8]{0,1:T(8,128)}, u32[]{:S(2)}) copy-start(f32[128,8]{0,1:T(8,128)} %param.15) | copy-start | bytes 12292
  21.9 12.0 %copy-start.11 = (bf16[128,1536]{1,0:T(8,128)(2,1)S(1)}, bf16[128,1536]{1,0:T(8,128)(2,1)}, u32[]{:S(2)}) copy-start(bf16[128,1536]{1,0:T(8,128)(2,1)} %param.19) | copy-start | bytes 1179652
  33.7 10.6 %copy-start.10 = (f32[128,8]{1,0:T(8,128)}, f32[128,8]{1,0:T(8,128)S(1)}, u32[]{:S(2)}) copy-start(f32[128,8]{1,0:T(8,128)S(1)} %copy.31) | copy-start | bytes 12292
  50.6 96.4 %all-to-all-start.3 = ((bf16[8,5,56,1536]{3,2,1,0:T(8,128)(2,1)}), bf16[8,5,56,1536]{3,2,1,0:T(8,128)(2,1)}, u32[]{:S(2)}, u32[]{:S(2)}) async-start(bf16[8,5,56,1536]{3,2,1,0:T(8,128)(2,1)} %bitcast.273), calls=%async_computation.3 | async-start | bytes 13762560 | tf_op jit(solution)/shard_map/all_to_all | solution.py:79
  55.9 104.9 %all-gather.7.cloned.1.call-start = ((), (), s32[]{:S(2)}) async-start(), calls=%async_computation.7 | async-start | bytes 3538944 | tf_op jit(solution)/shard_map/all_gather | solution.py:80
  147.0 83.2 %all-to-all-start = ((bf16[8,5,56,1536]{3,2,1,0:T(8,128)(2,1)}), bf16[8,5,56,1536]{3,2,1,0:T(8,128)(2,1)}, u32[]{:S(2)}, u32[]{:S(2)}) async-start(bf16[8,5,56,1536]{3,2,1,0:T(8,128)(2,1)} %bitcast.272), calls=%async_computation | async-start | bytes 13762560 | tf_op jit(solution)/shard_map/all_to_all | solution.py:70
  152.0 4.3 copy-start.13
  167.5 1.0 copy-start.8
  167.5 5.9 %copy-start.16 = (bf16[8,1,128,512]{3,2,0,1:T(8,128)(2,1)}, bf16[8,1,128,512]{3,2,0,1:T(8,128)(2,1)S(1)}, u32[]{:S(2)}) copy-start(bf16[8,1,128,512]{3,2,0,1:T(8,128)(2,1)S(1)} %get-tuple-element.45) | copy-start | bytes 3145732
  230.2 42.5 %all-to-all-start.2 = ((bf16[8,128,1536]{2,1,0:T(8,128)(2,1)}), bf16[8,128,1536]{2,1,0:T(8,128)(2,1)S(1)}, u32[]{:S(2)}, u32[]{:S(2)}) async-start(bf16[8,128,1536]{2,1,0:T(8,128)(2,1)} %convolution_convert_fusion), calls=%async_computation.2 | async-start | bytes 6291456 | tf_op jit(solution)/shard_map/all_to_all | solution.py:75
  234.5 18.4 %slice-start = ((s8[7864320]{0:T(1024)(128)(4,1)}), s8[4194304]{0:T(1024)(128)(4,1)S(1)}, s32[]{:S(2)}) async-start(s8[7864320]{0:T(1024)(128)(4,1)} %bitcast.274), calls=%async_computation.8 | async-start | bytes 8388608
  241.7 11.2 %slice-start.1 = ((s8[7864320]{0:T(1024)(128)(4,1)}), s8[3670016]{0:T(1024)(128)(4,1)S(1)}, s32[]{:S(2)}) async-start(s8[7864320]{0:T(1024)(128)(4,1)} %bitcast.274), calls=%async_computation.9 | async-start | bytes 7340032
  272.7 18.2 %copy-start.2 = (bf16[8,128,1536]{2,1,0:T(8,128)(2,1)}, bf16[8,128,1536]{2,1,0:T(8,128)(2,1)S(1)}, u32[]{:S(2)}) copy-start(bf16[8,128,1536]{2,1,0:T(8,128)(2,1)S(1)} %all-to-all-done.2) | copy-start | bytes 9437188
  272.7 42.8 %all-to-all-start.5 = ((bf16[8,128,1536]{2,1,0:T(8,128)(2,1)}), bf16[8,128,1536]{2,1,0:T(8,128)(2,1)}, u32[]{:S(2)}, u32[]{:S(2)}) async-start(bf16[8,128,1536]{2,1,0:T(8,128)(2,1)} %add_convert_fusion.1), calls=%async_computation.5 | async-start | bytes 6291456 | tf_op jit(solution)/shard_map/all_to_all | solution.py:84
  302.0 18.8 %copy-start.18 = (bf16[8,5,56,512]{3,2,0,1:T(8,128)(2,1)S(1)}, bf16[8,5,56,512]{3,2,0,1:T(8,128)(2,1)}, u32[]{:S(2)}) copy-start(bf16[8,5,56,512]{3,2,0,1:T(8,128)(2,1)} %get-tuple-element.42) | copy-start | bytes 6881284
  315.6 83.4 %all-to-all-start.1 = ((bf16[8,5,56,1536]{3,2,1,0:T(8,128)(2,1)}), bf16[8,5,56,1536]{3,2,1,0:T(8,128)(2,1)}, u32[]{:S(2)}, u32[]{:S(2)}) async-start(bf16[8,5,56,1536]{3,2,1,0:T(8,128)(2,1)} %copy.40), calls=%async_computation.1 | async-start | bytes 13762560 | tf_op jit(solution)/shard_map/all_to_all | solution.py:74
  320.8 10.8 %copy-start.5 = (bf16[1024,1536]{1,0:T(8,128)(2,1)S(1)}, bf16[1024,1536]{1,0:T(8,128)(2,1)}, u32[]{:S(2)}) copy-start(bf16[1024,1536]{1,0:T(8,128)(2,1)} %all-gather.7.cloned.1.call-done) | copy-start | bytes 9437188
  320.8 10.8 %copy-start.9 = (bf16[8,1,128,512]{3,2,0,1:T(8,128)(2,1)S(1)}, bf16[8,1,128,512]{3,2,0,1:T(8,128)(2,1)}, u32[]{:S(2)}) copy-start(bf16[8,1,128,512]{3,2,0,1:T(8,128)(2,1)} %copy-done.8) | copy-start | bytes 3145732
  337.1 9.8 %copy-start.3 = (bf16[8,5,56,512]{3,2,0,1:T(8,128)(2,1)S(1)}, bf16[8,5,56,512]{3,2,0,1:T(8,128)(2,1)}, u32[]{:S(2)}) copy-start(bf16[8,5,56,512]{3,2,0,1:T(8,128)(2,1)} %get-tuple-element.43) | copy-start | bytes 6881284
  371.2 33.1 %copy-start.6 = (bf16[8,5,56,512]{3,2,0,1:T(8,128)(2,1)S(1)}, bf16[8,5,56,512]{3,2,0,1:T(8,128)(2,1)}, u32[]{:S(2)}) copy-start(bf16[8,5,56,512]{3,2,0,1:T(8,128)(2,1)} %get-tuple-element.41) | copy-start | bytes 6881284
  399.0 83.6 %all-to-all-start.4 = ((bf16[8,5,56,1536]{3,2,1,0:T(8,128)(2,1)}), bf16[8,5,56,1536]{3,2,1,0:T(8,128)(2,1)}, u32[]{:S(2)}, u32[]{:S(2)}) async-start(bf16[8,5,56,1536]{3,2,1,0:T(8,128)(2,1)} %copy.43), calls=%async_computation.4 | async-start | bytes 13762560 | tf_op jit(solution)/shard_map/all_to_all | solution.py:83
  404.3 11.8 %copy-start.14 = (bf16[1024,1536]{1,0:T(8,128)(2,1)S(1)}, bf16[1024,1536]{1,0:T(8,128)(2,1)}, u32[]{:S(2)}) copy-start(bf16[1024,1536]{1,0:T(8,128)(2,1)} %all-gather.5.cloned.1.call-done) | copy-start | bytes 9437188
  404.3 11.8 %copy-start.17 = (bf16[8,1,128,512]{3,2,0,1:T(8,128)(2,1)S(1)}, bf16[8,1,128,512]{3,2,0,1:T(8,128)(2,1)}, u32[]{:S(2)}) copy-start(bf16[8,1,128,512]{3,2,0,1:T(8,128)(2,1)} %copy-done.16) | copy-start | bytes 3145732
  421.5 9.9 %copy-start.4 = (bf16[8,5,56,512]{3,2,0,1:T(8,128)(2,1)S(1)}, bf16[8,5,56,512]{3,2,0,1:T(8,128)(2,1)}, u32[]{:S(2)}) copy-start(bf16[8,5,56,512]{3,2,0,1:T(8,128)(2,1)} %get-tuple-element.43) | copy-start | bytes 6881284
  431.4 12.0 %copy-start.7 = (bf16[8,1,128,512]{3,2,0,1:T(8,128)(2,1)S(1)}, bf16[8,1,128,512]{3,2,0,1:T(8,128)(2,1)}, u32[]{:S(2)}) copy-start(bf16[8,1,128,512]{3,2,0,1:T(8,128)(2,1)} %get-tuple-element.44) | copy-start | bytes 3145732
  431.4 12.0 %copy-start.15 = (bf16[1024,1536]{1,0:T(8,128)(2,1)S(1)}, bf16[1024,1536]{1,0:T(8,128)(2,1)}, u32[]{:S(2)}) copy-start(bf16[1024,1536]{1,0:T(8,128)(2,1)} %all-gather.5.cloned.1.call-done) | copy-start | bytes 9437188
  488.9 13.6 %copy-start.1 = (bf16[128,1536]{1,0:T(8,128)(2,1)S(1)}, bf16[128,1536]{1,0:T(8,128)(2,1)}, u32[]{:S(2)}) copy-start(bf16[128,1536]{1,0:T(8,128)(2,1)} %param.13) | copy-start | bytes 1179652
Sparse Core Ops, SparseCore 0:
  33.7 26.2 all-gather.4
  62.2 39.7 all-gather.6
where the time goes:
time: 519 us; the launch traced here: 510 us
  waiting for transfers between devices  187 us (36%)
  matrix products  146 us (28%)
  other arithmetic  72.7 us (14%)
  local copies, waits for them, and re-layouts  59.2 us (11%)
  starting transfers between devices  29.8 us (6%)
  between operations  14.9 us (3%)
    all_to_all x1, waiting for transfers between devices, device_fn(): cold_d = lax.all_to_all(send_d[:cold_rows].reshape(cold_shape), 'ep', 0, 0)  82.9 us
    all_to_all x1, waiting for transfers between devices, device_fn(): cold_x = lax.all_to_all(send_x[:cold_rows].reshape(cold_shape), 'ep', 0, 0)  50.9 us
    convert_element_type x3, other arithmetic, device_fn(): cold_g.at[hot_local].add(jnp.where(is_owner, hot_g[0], 0.0))  29.4 us
    all_to_all x1, waiting for transfers between devices, device_fn(): lax.all_to_all(cold_acts[3], 'ep', 0, 0).reshape(cold_rows, row_width)  27.8 us
    dot_general x2, matrix products, expert_backward(): jnp.einsum('secd,efd->secf', d_out_rows, down_w, preferred_element_type=j...  20.2 us
    dot_general x2, matrix products, expert_backward(): jnp.einsum('secf,edf->secd', d_act_b, up_w, preferred_element_type=jnp.fl...  18.2 us
    dot_general x2, matrix products, expert_backward(): jnp.einsum('secd,secf->edf', in_rows, d_act_b, preferred_element_type=jnp...  17.3 us
    dot_general x2, matrix products, expert_backward(): jnp.einsum('secd,secf->edf', in_rows, d_act_a, preferred_element_type=jnp...  17.2 us
  transfers between devices with their start and end apart: 8, of which 6 were waited for; matrix products, arithmetic and copies ran while one was open for 45% of the time, Pallas kernels for 0%

commit v1 on v0

v1 whole, which is shorter than its diff:
```python
import functools

import jax
import jax.numpy as jnp
from jax import lax
from jax.experimental import pallas as pl
from jax.experimental.pallas import tpu as pltpu
from jax.sharding import PartitionSpec as P

MESH = pl.DeviceIdType.MESH
F32 = jnp.float32
BF16 = jnp.bfloat16


def dot_nn(a, b):
    return lax.dot_general(a, b, (((1,), (0,)), ((), ())), preferred_element_type=F32)


def dot_nt(a, b):
    return lax.dot_general(a, b, (((1,), (1,)), ((), ())), preferred_element_type=F32)


def dot_tn(a, b):
    return lax.dot_general(a, b, (((0,), (0,)), ((), ())), preferred_element_type=F32)


def layer_kernel(cfg, x_hbm, dy_hbm, meta_ref, w1_hbm, w3_hbm, w2_hbm,
                 y_hbm, dx_hbm, xr_hbm, dr_hbm, ur_hbm, da_hbm, db_hbm, xe_hbm, de_hbm, ue_hbm, dae_hbm, dbe_hbm,
                 x_all, dy_all, meta_all, rt, gt, mc, ypart, dxpart, ybuf, dxbuf, yra, yrb, yfl, yfr, dxra, dxrb, dxfl, dxfr,
                 rows, urow, darow, dbrow, act1, act2, orow, w1, w3, w2, outb,
                 m_send, m_recv, ag_send, ag_recv, rs_send, rs_recv, w_sem, st_sem, io_sem):
    chips, tok, width, hid, n_loc, cap, owner = cfg
    group = 2 * chips
    cp = 2 * cap
    n_rows = chips * cp
    hot_rows = chips * 2 * tok
    hb_rows = hot_rows // 2
    half = tok // 2
    me = lax.axis_index("ep")
    c = me // 2
    k = lax.rem(me, 2)
    c_r = lax.rem(c + 1, chips)
    c_l = lax.rem(c + chips - 1, chips)
    c_o = lax.rem(c + 2, chips)
    right = 2 * c_r + k
    left = 2 * c_l + k
    partner = 2 * c + 1 - k
    is_owner = me == owner

    own_x = pltpu.make_async_copy(x_hbm, x_all.at[c, pl.ds(k * tok, tok)], io_sem.at[0])
    own_dy = pltpu.make_async_copy(dy_hbm, dy_all.at[c, pl.ds(k * tok, tok)], io_sem.at[1])
    own_x.start()
    own_dy.start()

    def w_copies(i):
        e = lax.rem(i, n_loc)
        s = lax.rem(i, 2)
        return (pltpu.make_async_copy(w1_hbm.at[e], w1.at[s], w_sem.at[0, s]),
                pltpu.make_async_copy(w3_hbm.at[e], w3.at[s], w_sem.at[1, s]),
                pltpu.make_async_copy(w2_hbm.at[e], w2.at[s], w_sem.at[2, s]))

    for cpy in w_copies(0):
        cpy.start()
    meta_all[me] = meta_ref[...]

    barrier = pltpu.get_barrier_semaphore()
    for d in range(1, group):
        pl.semaphore_signal(barrier, inc=1, device_id={"ep": lax.rem(me + d, group)}, device_id_type=MESH)
    pl.semaphore_wait(barrier, group - 1)

    def meta_copy(d):
        return pltpu.make_async_remote_copy(
            src_ref=meta_ref, dst_ref=meta_all.at[me], send_sem=m_send.at[d], recv_sem=m_recv.at[d],
            device_id={"ep": lax.rem(me + d, group)}, device_id_type=MESH)

    def ag(ref, t, i):
        chip, core, r0, n, dev = (
            (c, k, 0, half, right), (c, k, half, half, right), (c, k, half, half, left), (c, k, 0, half, left),
            (c, k, 0, tok, partner),
            (c_l, k, 0, half, right), (c_r, k, half, half, left),
            (c_l, k, 0, tok, partner), (c_r, k, 0, tok, partner),
            (c_o, k, 0, half, partner), (c_o, k, half, half, partner))[i]
        blk = ref.at[chip, pl.ds(core * tok + r0, n)]
        return pltpu.make_async_remote_copy(
            src_ref=blk, dst_ref=blk, send_sem=ag_send.at[t, i], recv_sem=ag_recv.at[t, i],
            device_id={"ep": dev}, device_id_type=MESH)

    own_x.wait()
    for d in range(1, group):
        meta_copy(d).start()
    for i in (0, 2, 1, 3, 4):
        ag(x_all, 0, i).start()
    own_dy.wait()

    @pl.loop(0, chips * 2 * tok // 64)
    def _(r):
        q = r // (2 * tok // 64)
        o = pl.multiple_of(lax.rem(r, 2 * tok // 64) * 64, 64)
        ypart[q, pl.ds(o, 64)] = jnp.zeros((64, width), F32)
        dxpart[q, pl.ds(o, 64)] = jnp.zeros((64, width), F32)

    for d in range(1, group):
        meta_copy(d).wait_recv()

    upper = (lax.broadcasted_iota(jnp.int32, (tok, tok), 0) < lax.broadcasted_iota(jnp.int32, (tok, tok), 1)).astype(F32).astype(BF16)
    row_id = lax.broadcasted_iota(jnp.int32, (8, tok), 0)
    for s in range(group):
        q, core = s // 2, s % 2
        ids = meta_all[s, 0:8, :]
        gates = meta_all[s, 8:16, :]
        mask_m = jnp.zeros((8, tok), F32)
        gate_m = jnp.zeros((8, tok), F32)
        for le in range(n_loc):
            eq = ids == (me * n_loc + le).astype(F32)
            hit = jnp.sum(jnp.where(eq, 1.0, 0.0), axis=0, keepdims=True)
            gv = jnp.sum(jnp.where(eq, gates, 0.0), axis=0, keepdims=True)
            mask_m = jnp.where(row_id == le, hit, mask_m)
            gate_m = jnp.where(row_id == le, gv, gate_m)
        rank = dot_nn(mask_m.astype(BF16), upper)
        pos = jnp.where(mask_m > 0.0, rank + float(cap * core), -1.0)
        rt[q, :, core * tok:(core + 1) * tok] = pos
        gt[q, :, core * tok:(core + 1) * tok] = gate_m
        both = jnp.concatenate([pos, gate_m, jnp.zeros((tok - 16, tok), F32)], axis=0)
        mc[q, core * tok:(core + 1) * tok, :] = jnp.transpose(both)

    ag(x_all, 0, 0).wait_recv()
    ag(x_all, 0, 5).start()
    ag(x_all, 0, 2).wait_recv()
    ag(x_all, 0, 6).start()
    for i in (0, 2, 1, 3, 4):
        ag(dy_all, 1, i).start()
    ag(x_all, 0, 1).wait_recv()
    ag(x_all, 0, 7).start()
    ag(x_all, 0, 3).wait_recv()
    ag(x_all, 0, 8).start()
    ag(x_all, 0, 4).wait_recv()
    ag(x_all, 0, 5).wait_recv()
    ag(x_all, 0, 9).start()
    ag(x_all, 0, 6).wait_recv()
    ag(x_all, 0, 10).start()
    for i in (7, 8, 9, 10):
        ag(x_all, 0, i).wait_recv()

    def pick_rows(q, e):
        hit = rt[q, pl.ds(e, 1), :] == lax.broadcasted_iota(jnp.int32, (cp, 2 * tok), 0).astype(F32)
        return hit

    def column(q, lane):
        m = mc[q]
        return jnp.sum(jnp.where(lax.broadcasted_iota(jnp.int32, (2 * tok, 128), 1) == lane, m, 0.0), axis=1, keepdims=True)

    def put_rows(q, e):
        hit = column(q, e) == lax.broadcasted_iota(jnp.int32, (2 * tok, cp), 1).astype(F32)
        return jnp.where(hit, 1.0, 0.0).astype(BF16)

    def forward(m, s, aoff):
        for j in range(hid // 256):
            cs = slice(j * 256, (j + 1) * 256)
            act1[pl.ds(aoff, m), cs] = dot_nn(rows[s, 0:m, :], w1[s, :, cs])
            act2[pl.ds(aoff, m), cs] = dot_nn(rows[s, 0:m, :], w3[s, :, cs])

        @pl.loop(0, m // 32)
        def _(r):
            o = pl.multiple_of(aoff + r * 32, 32)
            a = act1[pl.ds(o, 32), :]
            b = act2[pl.ds(o, 32), :]
            sg = jax.nn.sigmoid(a)
            ga = a * sg
            act1[pl.ds(o, 32), :] = b * (sg * (1.0 + a * (1.0 - sg)))
            act2[pl.ds(o, 32), :] = ga
            urow[s, pl.ds(pl.multiple_of(r * 32, 32), 32), :] = (ga * b).astype(BF16)

        for j in range(width // 256):
            cs = slice(j * 256, (j + 1) * 256)
            orow[0:m, cs] = dot_nn(urow[s, 0:m, :], w2[s, :, cs]).astype(BF16)

    def backward(m, s, aoff):
        for j in range(hid // 256):
            cs = slice(j * 256, (j + 1) * 256)
            du = dot_nt(rows[s, 0:m, :], w2[s, cs, :])
            darow[s, 0:m, cs] = (du * act1[pl.ds(aoff, m), cs]).astype(BF16)
            dbrow[s, 0:m, cs] = (du * act2[pl.ds(aoff, m), cs]).astype(BF16)
        for j in range(width // 256):
            cs = slice(j * 256, (j + 1) * 256)
            orow[0:m, cs] = (dot_nt(darow[s, 0:m, :], w1[s, cs, :]) + dot_nt(dbrow[s, 0:m, :], w3[s, cs, :])).astype(BF16)

    def act_off(e):
        return pl.multiple_of(jnp.where(e == 0, 0, hot_rows + (e - 1) * n_rows), 64)

    def st_fwd(e, s):
        return (pltpu.make_async_copy(rows.at[s, 0:n_rows], xr_hbm.at[e], st_sem.at[0, s]),
                pltpu.make_async_copy(urow.at[s, 0:n_rows], ur_hbm.at[e], st_sem.at[1, s]))

    def st_bwd(e, s):
        return (pltpu.make_async_copy(rows.at[s, 0:n_rows], dr_hbm.at[e], st_sem.at[0, s]),
                pltpu.make_async_copy(darow.at[s, 0:n_rows], da_hbm.at[e], st_sem.at[1, s]),
                pltpu.make_async_copy(dbrow.at[s, 0:n_rows], db_hbm.at[e], st_sem.at[2, s]))

    def hot_store(hb, pairs):
        rest = hb_rows - n_rows

        @pl.when(hb == 0)
        def _():
            cps = []
            for t, (src, main, extra) in enumerate(pairs):
                cps.append(pltpu.make_async_copy(src.at[0:n_rows], main.at[0], io_sem.at[2 + 2 * t]))
                cps.append(pltpu.make_async_copy(src.at[n_rows:hb_rows], extra.at[0:rest], io_sem.at[3 + 2 * t]))
            for cpy in cps:
                cpy.start()
            for cpy in cps:
                cpy.wait()

        @pl.when(hb == 1)
        def _():
            cps = [pltpu.make_async_copy(src.at[0:hb_rows], extra.at[rest:rest + hb_rows], io_sem.at[2 + 2 * t])
                   for t, (src, main, extra) in enumerate(pairs)]
            for cpy in cps:
                cpy.start()
            for cpy in cps:
                cpy.wait()

    @pl.loop(0, n_loc)
    def _(e):
        s = lax.rem(e, 2)
        hot = jnp.logical_and(is_owner, e == 0)
        for cpy in w_copies(e + 1):
            cpy.start()
        for cpy in w_copies(e):
            cpy.wait()

        @pl.when(e == 1)
        def _():
            ag(dy_all, 1, 0).wait_recv()
            ag(dy_all, 1, 5).start()
            ag(dy_all, 1, 2).wait_recv()
            ag(dy_all, 1, 6).start()

        @pl.when(e == 3)
        def _():
            ag(dy_all, 1, 1).wait_recv()
            ag(dy_all, 1, 7).start()
            ag(dy_all, 1, 3).wait_recv()
            ag(dy_all, 1, 8).start()

        @pl.when(jnp.logical_not(hot))
        def _():
            for q in range(chips):
                hit = jnp.where(pick_rows(q, e), 1.0, 0.0).astype(BF16)
                rows[s, q * cp:(q + 1) * cp, :] = dot_nn(hit, x_all[q]).astype(BF16)
            forward(n_rows, s, act_off(e))
            for q in range(chips):
                gate = column(q, e + 8)
                ypart[q] += gate * dot_nn(put_rows(q, e), orow[q * cp:(q + 1) * cp, :])

        @pl.when(hot)
        def _():
            @pl.loop(0, 2)
            def _(hb):
                for qq in range(chips // 2):
                    q = hb * (chips // 2) + qq
                    on = column(q, 0) >= 0.0
                    rows[0, qq * 2 * tok:(qq + 1) * 2 * tok, :] = jnp.where(on, x_all[q].astype(F32), 0.0).astype(BF16)
                forward(hb_rows, 0, pl.multiple_of(hb * hb_rows, 64))
                for qq in range(chips // 2):
                    q = hb * (chips // 2) + qq
                    ypart[q] += column(q, 8) * orow[qq * 2 * tok:(qq + 1) * 2 * tok, :].astype(F32)
                hot_store(hb, ((rows.at[0], xr_hbm, xe_hbm), (urow.at[0], ur_hbm, ue_hbm)))

        @pl.when(jnp.logical_and(e >= 1, jnp.logical_not(jnp.logical_and(is_owner, e == 1))))
        def _():
            for cpy in st_fwd(e - 1, 1 - s):
                cpy.wait()

        @pl.when(jnp.logical_not(hot))
        def _():
            for cpy in st_fwd(e, s):
                cpy.start()

    def rs(t, j):
        part, buf, ra, rb, fl, fr = ((ypart, ybuf, yra, yrb, yfl, yfr), (dxpart, dxbuf, dxra, dxrb, dxfl, dxfr))[t]
        o = k * tok
        if j < 4:
            q = (c_o, c_r, c_l, c)[j]
            src, dst, dev = part.at[q, pl.ds((1 - k) * tok, tok)], buf.at[q], partner
        else:
            src, dst, dev = (
                (part.at[c_o, pl.ds(o, half)], ra, right),
                (part.at[c_o, pl.ds(o + half, half)], rb, left),
                (part.at[c_r, pl.ds(o + half, half)], fl.at[half:tok], right),
                (part.at[c_l, pl.ds(o, half)], fr.at[0:half], left),
                (part.at[c_r, pl.ds(o, half)], fl.at[0:half], right),
                (part.at[c_l, pl.ds(o + half, half)], fr.at[half:tok], left))[j - 4]
        return pltpu.make_async_remote_copy(
            src_ref=src, dst_ref=dst, send_sem=rs_send.at[t, j], recv_sem=rs_recv.at[t, j],
            device_id={"ep": dev}, device_id_type=MESH)

    def add_rows(part, q, off, src, n):
        @pl.loop(0, n // 32)
        def _(r):
            o = pl.multiple_of(r * 32, 32)
            part[q, pl.ds(pl.multiple_of(off + r * 32, 32), 32)] += src[pl.ds(o, 32)]

    def rs_begin(t):
        part, buf = ((ypart, ybuf), (dxpart, dxbuf))[t]
        for j in range(4):
            rs(t, j).start()
        for j, q in enumerate((c_o, c_r, c_l, c)):
            rs(t, j).wait_recv()
            add_rows(part, q, k * tok, buf.at[q], tok)
            if j == 0:
                rs(t, 4).start()
                rs(t, 5).start()
            if j == 1:
                rs(t, 6).start()
            if j == 2:
                rs(t, 7).start()

    def rs_relay(t):
        part, ra, rb = ((ypart, yra, yrb), (dxpart, dxra, dxrb))[t]
        rs(t, 4).wait_recv()
        add_rows(part, c_r, k * tok, ra, half)
        rs(t, 8).start()
        rs(t, 5).wait_recv()
        add_rows(part, c_l, k * tok + half, rb, half)
        rs(t, 9).start()

    def rs_end(t):
        part, fl, fr, out = ((ypart, yfl, yfr, y_hbm), (dxpart, dxfl, dxfr, dx_hbm))[t]
        for j in (6, 7, 8, 9):
            rs(t, j).wait_recv()

        @pl.loop(0, tok // 32)
        def _(r):
            o = pl.multiple_of(r * 32, 32)
            total = part[c, pl.ds(pl.multiple_of(k * tok + r * 32, 32), 32)] + fl[pl.ds(o, 32)] + fr[pl.ds(o, 32)]
            outb[t, pl.ds(o, 32)] = total.astype(BF16)

        return pltpu.make_async_copy(outb.at[t], out, io_sem.at[t])

    rs_begin(0)
    ag(dy_all, 1, 4).wait_recv()
    ag(dy_all, 1, 5).wait_recv()
    ag(dy_all, 1, 9).start()
    ag(dy_all, 1, 6).wait_recv()
    ag(dy_all, 1, 10).start()
    for i in (7, 8, 9, 10):
        ag(dy_all, 1, i).wait_recv()
    for cpy in st_fwd(n_loc - 1, (n_loc - 1) % 2):
        cpy.wait()

    @pl.loop(0, n_loc)
    def _(e):
        s = lax.rem(e + n_loc, 2)
        hot = jnp.logical_and(is_owner, e == 0)

        @pl.when(e + 1 < n_loc)
        def _():
            for cpy in w_copies(e + n_loc + 1):
                cpy.start()

        for cpy in w_copies(e + n_loc):
            cpy.wait()

        @pl.when(e == 2)
        def _():
            rs_relay(0)

        @pl.when(jnp.logical_not(hot))
        def _():
            for q in range(chips):
                hit = pick_rows(q, e)
                gate = jnp.sum(jnp.where(hit, gt[q, pl.ds(e, 1), :], 0.0), axis=1, keepdims=True)
                got = dot_nn(jnp.where(hit, 1.0, 0.0).astype(BF16), dy_all[q])
                rows[s, q * cp:(q + 1) * cp, :] = (gate * got).astype(BF16)
            backward(n_rows, s, act_off(e))
            for q in range(chips):
                dxpart[q] += dot_nn(put_rows(q, e), orow[q * cp:(q + 1) * cp, :])

        @pl.when(hot)
        def _():
            @pl.loop(0, 2)
            def _(hb):
                for qq in range(chips // 2):
                    q = hb * (chips // 2) + qq
                    rows[s, qq * 2 * tok:(qq + 1) * 2 * tok, :] = (column(q, 8) * dy_all[q].astype(F32)).astype(BF16)
                backward(hb_rows, s, pl.multiple_of(hb * hb_rows, 64))
                for qq in range(chips // 2):
                    q = hb * (chips // 2) + qq
                    dxpart[q] += orow[qq * 2 * tok:(qq + 1) * 2 * tok, :].astype(F32)
                hot_store(hb, ((rows.at[s], dr_hbm, de_hbm), (darow.at[s], da_hbm, dae_hbm), (dbrow.at[s], db_hbm, dbe_hbm)))

        @pl.when(jnp.logical_and(e >= 1, jnp.logical_not(jnp.logical_and(is_owner, e == 1))))
        def _():
            for cpy in st_bwd(e - 1, 1 - s):
                cpy.wait()

        @pl.when(jnp.logical_not(hot))
        def _():
            for cpy in st_bwd(e, s):
                cpy.start()

    rs_begin(1)
    y_out = rs_end(0)
    y_out.start()
    rs_relay(1)
    dx_out = rs_end(1)
    dx_out.start()

    for cpy in st_bwd(n_loc - 1, (2 * n_loc - 1) % 2):
        cpy.wait()
    for d in range(1, group):
        meta_copy(d).wait_send()
    for i in range(11):
        ag(x_all, 0, i).wait_send()
        ag(dy_all, 1, i).wait_send()
    for j in range(10):
        rs(0, j).wait_send()
        rs(1, j).wait_send()
    y_out.wait()
    dx_out.wait()


def grad_kernel(owner, x_ref, d_ref, u_ref, da_ref, db_ref, xe, de, ue, dae, dbe, g1, g3, g2, xb, db_, ub, dab, dbb, sem):
    e = pl.program_id(0)
    hot = jnp.logical_and(lax.axis_index("ep") == owner, e == 0)

    @pl.when(jnp.logical_not(hot))
    def _():
        g1[0] = dot_tn(x_ref[0], da_ref[0]).astype(BF16)
        g3[0] = dot_tn(x_ref[0], db_ref[0]).astype(BF16)
        g2[0] = dot_tn(u_ref[0], d_ref[0]).astype(BF16)

    @pl.when(hot)
    def _():
        cps = [pltpu.make_async_copy(src, dst, sem.at[i]) for i, (src, dst) in enumerate(((xe, xb), (de, db_), (ue, ub), (dae, dab), (dbe, dbb)))]
        for cpy in cps:
            cpy.start()
        for cpy in cps:
            cpy.wait()
        g1[0] = (dot_tn(x_ref[0], da_ref[0]) + dot_tn(xb[...], dab[...])).astype(BF16)
        g3[0] = (dot_tn(x_ref[0], db_ref[0]) + dot_tn(xb[...], dbb[...])).astype(BF16)
        g2[0] = (dot_tn(u_ref[0], d_ref[0]) + dot_tn(ub[...], db_[...])).astype(BF16)


def solution(mesh):
    group = mesh.shape["ep"]
    num_dev = mesh.shape["dp"] * group
    tok_spec = P(("dp", "ep"), None)
    w_spec = P("ep", None, None)
    grad_spec = P(("dp", "ep"), None, None)

    def layer_fn(tokens, expert_ids, gate_vals, w_gate, w_up, w_down, grad_out):
        n_exp, width, hid = w_gate.shape
        tok = tokens.shape[0] // num_dev
        top_k = expert_ids.shape[1]
        cap = ((2 * tok * top_k + 8 * n_exp - 1) // (8 * n_exp)) * 8
        n_loc = n_exp // group
        hot = n_exp // 2
        owner = hot // n_loc
        chips = group // 2
        n_rows = chips * 2 * cap
        hot_rows = group * tok
        extra = hot_rows - n_rows
        cfg = (chips, tok, width, hid, n_loc, cap, owner)

        def device_fn(x, ids, gates, w1, w3, w2, dy):
            meta = jnp.concatenate([ids.T.astype(F32), gates.T], axis=0)
            any_spec = pl.BlockSpec(memory_space=pl.ANY)
            sds = jax.ShapeDtypeStruct
            hb = hot_rows // 2
            outs = pl.pallas_call(
                functools.partial(layer_kernel, cfg),
                out_shape=(
                    sds((tok, width), BF16), sds((tok, width), BF16),
                    sds((n_loc, n_rows, width), BF16), sds((n_loc, n_rows, width), BF16),
                    sds((n_loc, n_rows, hid), BF16), sds((n_loc, n_rows, hid), BF16), sds((n_loc, n_rows, hid), BF16),
                    sds((extra, width), BF16), sds((extra, width), BF16),
                    sds((extra, hid), BF16), sds((extra, hid), BF16), sds((extra, hid), BF16)),
                in_specs=[any_spec, any_spec, pl.BlockSpec(memory_space=pltpu.VMEM), any_spec, any_spec, any_spec],
                out_specs=[any_spec] * 12,
                scratch_shapes=[
                    pltpu.VMEM((chips, 2 * tok, width), BF16), pltpu.VMEM((chips, 2 * tok, width), BF16),
                    pltpu.VMEM((group, 16, tok), F32),
                    pltpu.VMEM((chips, 8, 2 * tok), F32), pltpu.VMEM((chips, 8, 2 * tok), F32),
                    pltpu.VMEM((chips, 2 * tok, 128), F32),
                    pltpu.VMEM((chips, 2 * tok, width), F32), pltpu.VMEM((chips, 2 * tok, width), F32),
                    pltpu.VMEM((chips, tok, width), F32), pltpu.VMEM((chips, tok, width), F32),
                    pltpu.VMEM((tok // 2, width), F32), pltpu.VMEM((tok // 2, width), F32),
                    pltpu.VMEM((tok, width), F32), pltpu.VMEM((tok, width), F32),
                    pltpu.VMEM((tok // 2, width), F32), pltpu.VMEM((tok // 2, width), F32),
                    pltpu.VMEM((tok, width), F32), pltpu.VMEM((tok, width), F32),
                    pltpu.VMEM((2, hb, width), BF16), pltpu.VMEM((2, hb, hid), BF16),
                    pltpu.VMEM((2, hb, hid), BF16), pltpu.VMEM((2, hb, hid), BF16),
                    pltpu.VMEM((hot_rows + (n_loc - 1) * n_rows, hid), F32), pltpu.VMEM((hot_rows + (n_loc - 1) * n_rows, hid), F32),
                    pltpu.VMEM((hb, width), BF16),
                    pltpu.VMEM((2, width, hid), BF16), pltpu.VMEM((2, width, hid), BF16), pltpu.VMEM((2, hid, width), BF16),
                    pltpu.VMEM((2, tok, width), BF16),
                    pltpu.SemaphoreType.DMA((group,)), pltpu.SemaphoreType.DMA((group,)),
                    pltpu.SemaphoreType.DMA((2, 11)), pltpu.SemaphoreType.DMA((2, 11)),
                    pltpu.SemaphoreType.DMA((2, 10)), pltpu.SemaphoreType.DMA((2, 10)),
                    pltpu.SemaphoreType.DMA((3, 2)), pltpu.SemaphoreType.DMA((3, 2)), pltpu.SemaphoreType.DMA((8,)),
                ],
                compiler_params=pltpu.CompilerParams(collective_id=0, has_side_effects=True, vmem_limit_bytes=67043328),
                name="moe_layer",
            )(x, dy, meta, w1, w3, w2)
            y, dx, xr, dr, ur, dar, dbr, xe, de, ue, dae, dbe = outs

            def blk(r, n):
                return pl.BlockSpec((1, r, n), lambda e: (e, 0, 0))

            g1, g3, g2 = pl.pallas_call(
                functools.partial(grad_kernel, owner),
                grid=(n_loc,),
                out_shape=(sds((n_loc, width, hid), BF16), sds((n_loc, width, hid), BF16), sds((n_loc, hid, width), BF16)),
                in_specs=[blk(n_rows, width), blk(n_rows, width), blk(n_rows, hid), blk(n_rows, hid), blk(n_rows, hid)] + [any_spec] * 5,
                out_specs=[blk(width, hid), blk(width, hid), blk(hid, width)],
                scratch_shapes=[pltpu.VMEM((extra, width), BF16), pltpu.VMEM((extra, width), BF16), pltpu.VMEM((extra, hid), BF16),
                                pltpu.VMEM((extra, hid), BF16), pltpu.VMEM((extra, hid), BF16), pltpu.SemaphoreType.DMA((5,))],
                compiler_params=pltpu.CompilerParams(vmem_limit_bytes=60 << 20),
                name="weight_grads",
            )(xr, dr, ur, dar, dbr, xe, de, ue, dae, dbe)
            return y, dx, g1, g3, g2

        return jax.shard_map(device_fn, mesh=mesh, in_specs=(tok_spec, tok_spec, tok_spec, w_spec, w_spec, w_spec, tok_spec),
                             out_specs=(tok_spec, tok_spec, grad_spec, grad_spec, grad_spec), check_vma=False)(
            tokens, expert_ids, gate_vals, w_gate, w_up, w_down, grad_out)

    return layer_fn
```

time: 519 us -> 133 us (0.26)
  the two profiles are of different devices: /device:TPU:112 before, /device:TPU:116 now
where the time goes in v1:
time: 133 us
  Pallas kernels  128 us (96%)
  other arithmetic  1.98 us (1%)
  local copies, waits for them, and re-layouts  1.5 us (1%)
    pallas_call x1, Pallas kernels, device_fn(): pl.pallas_call(functools.partial(layer_kernel, cfg), out_shape=(sds((tok,...  100 us
    pallas_call x1, Pallas kernels, device_fn(): pl.pallas_call(functools.partial(grad_kernel, owner), grid=(n_loc,), out_...  28 us

profile of v1, /device:TPU:116, one launch (start us, length us, event | category | flops | bytes accessed | tf_op | source)
XLA Modules:
  0.0 132.5 jit_solution(458794267488840155)
XLA Ops:
  0.6 0.7 convert_bitcast_fusion
  1.3 1.3 pad_maximum_fusion.meta_ref
  2.6 100.4 %moe_layer.1 = (bf16[128,1536]{1,0:T(8,128)(2,1)}, bf16[128,1536]{1,0:T(8,128)(2,1)}, bf16[5,448,1536]{2,1,0:T(8,128)(2,1)}, bf16[5,448,1536]{2,1,0:T(8,128)(2,1...) custom-call(bf16[128,1536]{1,0:T(8,128)(2,1)} %x_hbm.1, ...), custom_call_target="tpu_custom_call" | custom-call | tf_op jit(solution)/shard_map/moe_layer/pallas_call | solution.py:471
  103.0 0.0 copy-start.1
  103.0 0.0 copy-start
  103.0 28.0 %weight_grads.1 = (bf16[5,1536,512]{2,1,0:T(8,128)(2,1)}, bf16[5,1536,512]{2,1,0:T(8,128)(2,1)}, bf16[5,512,1536]{2,1,0:T(8,128)(2,1)}) custom-call(bf16[5,448,1536]{2,1,0:T(8,128)(2,1)} %get-tuple-element.22.x_ref, bf16[5,448,1536]{2,1,0:T(8,128)(2,1)} %get-tuple-element.23.d_ref, bf16[5,448,512]{2,1,0:T(8,128)(2,1)} %get-tuple-element.24.u_ref, ...), custom_call_target="tpu_custom_call" | custom-call | tf_op jit(solution)/shard_map/weight_grads/pallas_call | solution.py:511
  131.0 0.0 copy-done.1
  131.0 0.7 copy.14
  131.8 0.0 copy-done
  131.8 0.7 copy.15
Async XLA Ops:
  103.0 28.0 %copy-start.1 = (bf16[128,1536]{1,0:T(8,128)(2,1)S(1)}, bf16[128,1536]{1,0:T(8,128)(2,1)}, u32[]{:S(2)}) copy-start(bf16[128,1536]{1,0:T(8,128)(2,1)} %get-tuple-element.40) | copy-start | bytes 1179652
  103.0 28.8 %copy-start = (bf16[128,1536]{1,0:T(8,128)(2,1)S(1)}, bf16[128,1536]{1,0:T(8,128)(2,1)}, u32[]{:S(2)}) copy-start(bf16[128,1536]{1,0:T(8,128)(2,1)} %get-tuple-element.41) | copy-start | bytes 1179652

commit v2 on v1

--- a/solution.py
+++ b/solution.py
@@ -24,11 +24,11 @@
     return lax.dot_general(a, b, (((0,), (0,)), ((), ())), preferred_element_type=F32)
 
 
-def layer_kernel(cfg, x_hbm, dy_hbm, meta_ref, w1_hbm, w3_hbm, w2_hbm,
-                 y_hbm, dx_hbm, xr_hbm, dr_hbm, ur_hbm, da_hbm, db_hbm, xe_hbm, de_hbm, ue_hbm, dae_hbm, dbe_hbm,
-                 x_all, dy_all, meta_all, rt, gt, mc, ypart, dxpart, ybuf, dxbuf, yra, yrb, yfl, yfr, dxra, dxrb, dxfl, dxfr,
+def layer_kernel(cfg, x_hbm, dy_hbm, ids_ref, gates_ref, w1_hbm, w3_hbm, w2_hbm,
+                 y_hbm, soa_hbm, sob_hbm, sra_hbm, srb_hbm, sla_hbm, slb_hbm, sc_hbm, xr_hbm, dr_hbm, ur_hbm, da_hbm, db_hbm, xe_hbm, de_hbm, ue_hbm, dae_hbm, dbe_hbm,
+                 x_all, dy_all, ids_all, gates_all, rt, gt, mc, ypart, dxpart, ybuf, dxbuf, yra, yrb, yfl, yfr,
                  rows, urow, darow, dbrow, act1, act2, orow, w1, w3, w2, outb,
-                 m_send, m_recv, ag_send, ag_recv, rs_send, rs_recv, w_sem, st_sem, io_sem):
+                 m_send, m_recv, ag_send, ag_recv, rs_send, rs_recv, w_sem, st_sem, io_sem, so_sem):
     chips, tok, width, hid, n_loc, cap, owner = cfg
     group = 2 * chips
     cp = 2 * cap
@@ -61,17 +61,19 @@
 
     for cpy in w_copies(0):
         cpy.start()
-    meta_all[me] = meta_ref[...]
+    ids_all[me] = ids_ref[...]
+    gates_all[me] = gates_ref[...]
 
     barrier = pltpu.get_barrier_semaphore()
     for d in range(1, group):
         pl.semaphore_signal(barrier, inc=1, device_id={"ep": lax.rem(me + d, group)}, device_id_type=MESH)
     pl.semaphore_wait(barrier, group - 1)
 
-    def meta_copy(d):
-        return pltpu.make_async_remote_copy(
-            src_ref=meta_ref, dst_ref=meta_all.at[me], send_sem=m_send.at[d], recv_sem=m_recv.at[d],
+    def meta_copies(d):
+        return tuple(pltpu.make_async_remote_copy(
+            src_ref=src, dst_ref=dst.at[me], send_sem=m_send.at[i, d], recv_sem=m_recv.at[i, d],
             device_id={"ep": lax.rem(me + d, group)}, device_id_type=MESH)
+            for i, (src, dst) in enumerate(((ids_ref, ids_all), (gates_ref, gates_all))))
 
     def ag(ref, t, i):
         chip, core, r0, n, dev = (
@@ -87,7 +89,8 @@
 
     own_x.wait()
     for d in range(1, group):
-        meta_copy(d).start()
+        for cpy in meta_copies(d):
+            cpy.start()
     for i in (0, 2, 1, 3, 4):
         ag(x_all, 0, i).start()
     own_dy.wait()
@@ -100,18 +103,19 @@
         dxpart[q, pl.ds(o, 64)] = jnp.zeros((64, width), F32)
 
     for d in range(1, group):
-        meta_copy(d).wait_recv()
+        for cpy in meta_copies(d):
+            cpy.wait_recv()
 
     upper = (lax.broadcasted_iota(jnp.int32, (tok, tok), 0) < lax.broadcasted_iota(jnp.int32, (tok, tok), 1)).astype(F32).astype(BF16)
     row_id = lax.broadcasted_iota(jnp.int32, (8, tok), 0)
     for s in range(group):
         q, core = s // 2, s % 2
-        ids = meta_all[s, 0:8, :]
-        gates = meta_all[s, 8:16, :]
+        ids = ids_all[s]
+        gates = gates_all[s]
         mask_m = jnp.zeros((8, tok), F32)
         gate_m = jnp.zeros((8, tok), F32)
         for le in range(n_loc):
-            eq = ids == (me * n_loc + le).astype(F32)
+            eq = ids == me * n_loc + le
             hit = jnp.sum(jnp.where(eq, 1.0, 0.0), axis=0, keepdims=True)
             gv = jnp.sum(jnp.where(eq, gates, 0.0), axis=0, keepdims=True)
             mask_m = jnp.where(row_id == le, hit, mask_m)
@@ -277,19 +281,19 @@
                 cpy.start()
 
     def rs(t, j):
-        part, buf, ra, rb, fl, fr = ((ypart, ybuf, yra, yrb, yfl, yfr), (dxpart, dxbuf, dxra, dxrb, dxfl, dxfr))[t]
+        part, buf = ((ypart, ybuf), (dxpart, dxbuf))[t]
         o = k * tok
         if j < 4:
             q = (c_o, c_r, c_l, c)[j]
             src, dst, dev = part.at[q, pl.ds((1 - k) * tok, tok)], buf.at[q], partner
         else:
             src, dst, dev = (
-                (part.at[c_o, pl.ds(o, half)], ra, right),
-                (part.at[c_o, pl.ds(o + half, half)], rb, left),
-                (part.at[c_r, pl.ds(o + half, half)], fl.at[half:tok], right),
-                (part.at[c_l, pl.ds(o, half)], fr.at[0:half], left),
-                (part.at[c_r, pl.ds(o, half)], fl.at[0:half], right),
-                (part.at[c_l, pl.ds(o + half, half)], fr.at[half:tok], left))[j - 4]
+                (part.at[c_o, pl.ds(o, half)], yra, right),
+                (part.at[c_o, pl.ds(o + half, half)], yrb, left),
+                (part.at[c_r, pl.ds(o + half, half)], yfl.at[half:tok], right),
+                (part.at[c_l, pl.ds(o, half)], yfr.at[0:half], left),
+                (part.at[c_r, pl.ds(o, half)], yfl.at[0:half], right),
+                (part.at[c_l, pl.ds(o + half, half)], yfr.at[half:tok], left))[j - 4]
         return pltpu.make_async_remote_copy(
             src_ref=src, dst_ref=dst, send_sem=rs_send.at[t, j], recv_sem=rs_recv.at[t, j],
             device_id={"ep": dev}, device_id_type=MESH)
@@ -300,44 +304,49 @@
             o = pl.multiple_of(r * 32, 32)
             part[q, pl.ds(pl.multiple_of(off + r * 32, 32), 32)] += src[pl.ds(o, 32)]
 
-    def rs_begin(t):
-        part, buf = ((ypart, ybuf), (dxpart, dxbuf))[t]
+    def rs_begin_y():
         for j in range(4):
-            rs(t, j).start()
+            rs(0, j).start()
         for j, q in enumerate((c_o, c_r, c_l, c)):
-            rs(t, j).wait_recv()
-            add_rows(part, q, k * tok, buf.at[q], tok)
+            rs(0, j).wait_recv()
+            add_rows(ypart, q, k * tok, ybuf.at[q], tok)
             if j == 0:
-                rs(t, 4).start()
-                rs(t, 5).start()
+                rs(0, 4).start()
+                rs(0, 5).start()
             if j == 1:
-                rs(t, 6).start()
+                rs(0, 6).start()
             if j == 2:
-                rs(t, 7).start()
-
-    def rs_relay(t):
-        part, ra, rb = ((ypart, yra, yrb), (dxpart, dxra, dxrb))[t]
-        rs(t, 4).wait_recv()
-        add_rows(part, c_r, k * tok, ra, half)
-        rs(t, 8).start()
-        rs(t, 5).wait_recv()
-        add_rows(part, c_l, k * tok + half, rb, half)
-        rs(t, 9).start()
-
-    def rs_end(t):
-        part, fl, fr, out = ((ypart, yfl, yfr, y_hbm), (dxpart, dxfl, dxfr, dx_hbm))[t]
+                rs(0, 7).start()
+
+    def rs_relay_y():
+        rs(0, 4).wait_recv()
+        add_rows(ypart, c_r, k * tok, yra, half)
+        rs(0, 8).start()
+        rs(0, 5).wait_recv()
+        add_rows(ypart, c_l, k * tok + half, yrb, half)
+        rs(0, 9).start()
+
+    def rs_end_y():
         for j in (6, 7, 8, 9):
-            rs(t, j).wait_recv()
+            rs(0, j).wait_recv()
 
         @pl.loop(0, tok // 32)
         def _(r):
             o = pl.multiple_of(r * 32, 32)
-            total = part[c, pl.ds(pl.multiple_of(k * tok + r * 32, 32), 32)] + fl[pl.ds(o, 32)] + fr[pl.ds(o, 32)]
-            outb[t, pl.ds(o, 32)] = total.astype(BF16)
-
-        return pltpu.make_async_copy(outb.at[t], out, io_sem.at[t])
-
-    rs_begin(0)
+            total = ypart[c, pl.ds(pl.multiple_of(k * tok + r * 32, 32), 32)] + yfl[pl.ds(o, 32)] + yfr[pl.ds(o, 32)]
+            outb[pl.ds(o, 32)] = total.astype(BF16)
+
+        return pltpu.make_async_copy(outb, y_hbm, io_sem.at[0])
+
+    def chip_sums_out(j):
+        q = (c_o, c_r, c_l, c)[j]
+        if j == 3:
+            return (pltpu.make_async_copy(dxpart.at[q, pl.ds(k * tok, tok)], sc_hbm, so_sem.at[6]),)
+        lo, hi = ((soa_hbm, sob_hbm), (sra_hbm, srb_hbm), (sla_hbm, slb_hbm))[j]
+        return (pltpu.make_async_copy(dxpart.at[q, pl.ds(k * tok, half)], lo, so_sem.at[2 * j]),
+                pltpu.make_async_copy(dxpart.at[q, pl.ds(k * tok + half, half)], hi, so_sem.at[2 * j + 1]))
+
+    rs_begin_y()
     ag(dy_all, 1, 4).wait_recv()
     ag(dy_all, 1, 5).wait_recv()
     ag(dy_all, 1, 9).start()
@@ -361,9 +370,9 @@
         for cpy in w_copies(e + n_loc):
             cpy.wait()
 
-        @pl.when(e == 2)
-        def _():
-            rs_relay(0)
+        @pl.when(e == n_loc - 1)
+        def _():
+            rs_relay_y()
 
         @pl.when(jnp.logical_not(hot))
         def _():
@@ -399,36 +408,46 @@
             for cpy in st_bwd(e, s):
                 cpy.start()
 
-    rs_begin(1)
-    y_out = rs_end(0)
+    for j in range(4):
+        rs(1, j).start()
+    for j, q in enumerate((c_o, c_r, c_l, c)):
+        rs(1, j).wait_recv()
+        add_rows(dxpart, q, k * tok, dxbuf.at[q], tok)
+        for cpy in chip_sums_out(j):
+            cpy.start()
+    y_out = rs_end_y()
     y_out.start()
-    rs_relay(1)
-    dx_out = rs_end(1)
-    dx_out.start()
 
     for cpy in st_bwd(n_loc - 1, (2 * n_loc - 1) % 2):
         cpy.wait()
     for d in range(1, group):
-        meta_copy(d).wait_send()
+        for cpy in meta_copies(d):
+            cpy.wait_send()
     for i in range(11):
         ag(x_all, 0, i).wait_send()
         ag(dy_all, 1, i).wait_send()
     for j in range(10):
         rs(0, j).wait_send()
+    for j in range(4):
         rs(1, j).wait_send()
+        for cpy in chip_sums_out(j):
+            cpy.wait()
     y_out.wait()
-    dx_out.wait()
-
-
-def grad_kernel(owner, x_ref, d_ref, u_ref, da_ref, db_ref, xe, de, ue, dae, dbe, g1, g3, g2, xb, db_, ub, dab, dbb, sem):
+
+
+def expert_grads(x_ref, d_ref, u_ref, da_ref, db_ref, g1, g3, g2):
+    g1[0] = dot_tn(x_ref[0], da_ref[0]).astype(BF16)
+    g3[0] = dot_tn(x_ref[0], db_ref[0]).astype(BF16)
+    g2[0] = dot_tn(u_ref[0], d_ref[0]).astype(BF16)
+
+
+def first_grads_kernel(owner, x_ref, d_ref, u_ref, da_ref, db_ref, xe, de, ue, dae, dbe, g1, g3, g2, xb, db_, ub, dab, dbb, sem):
     e = pl.program_id(0)
     hot = jnp.logical_and(lax.axis_index("ep") == owner, e == 0)
 
     @pl.when(jnp.logical_not(hot))
     def _():
-        g1[0] = dot_tn(x_ref[0], da_ref[0]).astype(BF16)
-        g3[0] = dot_tn(x_ref[0], db_ref[0]).astype(BF16)
-        g2[0] = dot_tn(u_ref[0], d_ref[0]).astype(BF16)
+        expert_grads(x_ref, d_ref, u_ref, da_ref, db_ref, g1, g3, g2)
 
     @pl.when(hot)
     def _():
@@ -440,6 +459,11 @@
         g1[0] = (dot_tn(x_ref[0], da_ref[0]) + dot_tn(xb[...], dab[...])).astype(BF16)
         g3[0] = (dot_tn(x_ref[0], db_ref[0]) + dot_tn(xb[...], dbb[...])).astype(BF16)
         g2[0] = (dot_tn(u_ref[0], d_ref[0]) + dot_tn(ub[...], db_[...])).astype(BF16)
+
+
+def later_grads_kernel(x_ref, d_ref, u_ref, da_ref, db_ref, g1_in, g3_in, g2_in, g1, g3, g2):
+    del g1_in, g3_in, g2_in
+    expert_grads(x_ref, d_ref, u_ref, da_ref, db_ref, g1, g3, g2)
 
 
 def solution(mesh):
@@ -464,61 +488,94 @@
         cfg = (chips, tok, width, hid, n_loc, cap, owner)
 
         def device_fn(x, ids, gates, w1, w3, w2, dy):
-            meta = jnp.concatenate([ids.T.astype(F32), gates.T], axis=0)
             any_spec = pl.BlockSpec(memory_space=pl.ANY)
+            vmem_spec = pl.BlockSpec(memory_space=pltpu.VMEM)
             sds = jax.ShapeDtypeStruct
             hb = hot_rows // 2
+            half = tok // 2
+            act_rows = hot_rows + (n_loc - 1) * n_rows
             outs = pl.pallas_call(
                 functools.partial(layer_kernel, cfg),
                 out_shape=(
-                    sds((tok, width), BF16), sds((tok, width), BF16),
+                    sds((tok, width), BF16), *[sds((half, width), F32)] * 6, sds((tok, width), F32),
                     sds((n_loc, n_rows, width), BF16), sds((n_loc, n_rows, width), BF16),
                     sds((n_loc, n_rows, hid), BF16), sds((n_loc, n_rows, hid), BF16), sds((n_loc, n_rows, hid), BF16),
                     sds((extra, width), BF16), sds((extra, width), BF16),
                     sds((extra, hid), BF16), sds((extra, hid), BF16), sds((extra, hid), BF16)),
-                in_specs=[any_spec, any_spec, pl.BlockSpec(memory_space=pltpu.VMEM), any_spec, any_spec, any_spec],
-                out_specs=[any_spec] * 12,
+                in_specs=[any_spec, any_spec, vmem_spec, vmem_spec, any_spec, any_spec, any_spec],
+                out_specs=[any_spec] * 18,
                 scratch_shapes=[
                     pltpu.VMEM((chips, 2 * tok, width), BF16), pltpu.VMEM((chips, 2 * tok, width), BF16),
-                    pltpu.VMEM((group, 16, tok), F32),
+                    pltpu.VMEM((group, top_k, tok), jnp.int32), pltpu.VMEM((group, top_k, tok), F32),
                     pltpu.VMEM((chips, 8, 2 * tok), F32), pltpu.VMEM((chips, 8, 2 * tok), F32),
                     pltpu.VMEM((chips, 2 * tok, 128), F32),
                     pltpu.VMEM((chips, 2 * tok, width), F32), pltpu.VMEM((chips, 2 * tok, width), F32),
                     pltpu.VMEM((chips, tok, width), F32), pltpu.VMEM((chips, tok, width), F32),
-                    pltpu.VMEM((tok // 2, width), F32), pltpu.VMEM((tok // 2, width), F32),
-                    pltpu.VMEM((tok, width), F32), pltpu.VMEM((tok, width), F32),
-                    pltpu.VMEM((tok // 2, width), F32), pltpu.VMEM((tok // 2, width), F32),
+                    pltpu.VMEM((half, width), F32), pltpu.VMEM((half, width), F32),
                     pltpu.VMEM((tok, width), F32), pltpu.VMEM((tok, width), F32),
                     pltpu.VMEM((2, hb, width), BF16), pltpu.VMEM((2, hb, hid), BF16),
                     pltpu.VMEM((2, hb, hid), BF16), pltpu.VMEM((2, hb, hid), BF16),
-                    pltpu.VMEM((hot_rows + (n_loc - 1) * n_rows, hid), F32), pltpu.VMEM((hot_rows + (n_loc - 1) * n_rows, hid), F32),
+                    pltpu.VMEM((act_rows, hid), F32), pltpu.VMEM((act_rows, hid), F32),
                     pltpu.VMEM((hb, width), BF16),
                     pltpu.VMEM((2, width, hid), BF16), pltpu.VMEM((2, width, hid), BF16), pltpu.VMEM((2, hid, width), BF16),
-                    pltpu.VMEM((2, tok, width), BF16),
-                    pltpu.SemaphoreType.DMA((group,)), pltpu.SemaphoreType.DMA((group,)),
+                    pltpu.VMEM((tok, width), BF16),
+                    pltpu.SemaphoreType.DMA((2, group)), pltpu.SemaphoreType.DMA((2, group)),
                     pltpu.SemaphoreType.DMA((2, 11)), pltpu.SemaphoreType.DMA((2, 11)),
                     pltpu.SemaphoreType.DMA((2, 10)), pltpu.SemaphoreType.DMA((2, 10)),
                     pltpu.SemaphoreType.DMA((3, 2)), pltpu.SemaphoreType.DMA((3, 2)), pltpu.SemaphoreType.DMA((8,)),
+                    pltpu.SemaphoreType.DMA((7,)),
                 ],
                 compiler_params=pltpu.CompilerParams(collective_id=0, has_side_effects=True, vmem_limit_bytes=67043328),
                 name="moe_layer",
-            )(x, dy, meta, w1, w3, w2)
-            y, dx, xr, dr, ur, dar, dbr, xe, de, ue, dae, dbe = outs
-
-            def blk(r, n):
-                return pl.BlockSpec((1, r, n), lambda e: (e, 0, 0))
-
-            g1, g3, g2 = pl.pallas_call(
-                functools.partial(grad_kernel, owner),
-                grid=(n_loc,),
-                out_shape=(sds((n_loc, width, hid), BF16), sds((n_loc, width, hid), BF16), sds((n_loc, hid, width), BF16)),
-                in_specs=[blk(n_rows, width), blk(n_rows, width), blk(n_rows, hid), blk(n_rows, hid), blk(n_rows, hid)] + [any_spec] * 5,
-                out_specs=[blk(width, hid), blk(width, hid), blk(hid, width)],
+            )(x, dy, ids.T, gates.T, w1, w3, w2)
+            y, soa, sob, sra, srb, sla, slb, sc, xr, dr, ur, dar, dbr, xe, de, ue, dae, dbe = outs
+
+            to_right = [(i, (i + 2) % group) for i in range(group)]
+            to_left = [(i, (i + group - 2) % group) for i in range(group)]
+            ra = lax.ppermute(soa, "ep", to_right)
+            rb = lax.ppermute(sob, "ep", to_left)
+            fl_hi = lax.ppermute(srb, "ep", to_right)
+            fr_lo = lax.ppermute(sla, "ep", to_left)
+
+            n_first = (n_loc + 1) // 2
+            g_shapes = (sds((n_loc, width, hid), BF16), sds((n_loc, width, hid), BF16), sds((n_loc, hid, width), BF16))
+
+            def blk(r, n, first):
+                return pl.BlockSpec((1, r, n), lambda e: (e + first, 0, 0))
+
+            def row_specs(first):
+                return [blk(n_rows, width, first), blk(n_rows, width, first), blk(n_rows, hid, first), blk(n_rows, hid, first), blk(n_rows, hid, first)]
+
+            def out_blks(first):
+                return [blk(width, hid, first), blk(width, hid, first), blk(hid, width, first)]
+
+            def cost(n):
+                return pl.CostEstimate(flops=n * 6 * n_rows * width * hid, transcendentals=0,
+                                       bytes_accessed=n * 2 * (2 * n_rows * width + 3 * n_rows * hid + 3 * width * hid))
+
+            grads = pl.pallas_call(
+                functools.partial(first_grads_kernel, owner),
+                grid=(n_first,), out_shape=g_shapes,
+                in_specs=row_specs(0) + [any_spec] * 5, out_specs=out_blks(0),
                 scratch_shapes=[pltpu.VMEM((extra, width), BF16), pltpu.VMEM((extra, width), BF16), pltpu.VMEM((extra, hid), BF16),
                                 pltpu.VMEM((extra, hid), BF16), pltpu.VMEM((extra, hid), BF16), pltpu.SemaphoreType.DMA((5,))],
                 compiler_params=pltpu.CompilerParams(vmem_limit_bytes=60 << 20),
-                name="weight_grads",
+                cost_estimate=cost(n_first), name="first_grads",
             )(xr, dr, ur, dar, dbr, xe, de, ue, dae, dbe)
+
+            fl_lo = lax.ppermute(sra + ra, "ep", to_right)
+            fr_hi = lax.ppermute(slb + rb, "ep", to_left)
+            g1, g3, g2 = pl.pallas_call(
+                later_grads_kernel,
+                grid=(n_loc - n_first,), out_shape=g_shapes,
+                in_specs=row_specs(n_first) + [any_spec] * 3, out_specs=out_blks(n_first),
+                input_output_aliases={5: 0, 6: 1, 7: 2},
+                compiler_params=pltpu.CompilerParams(vmem_limit_bytes=60 << 20),
+                cost_estimate=cost(n_loc - n_first), name="later_grads",
+            )(xr, dr, ur, dar, dbr, *grads)
+            fl = jnp.concatenate([fl_lo, fl_hi], axis=0)
+            fr = jnp.concatenate([fr_lo, fr_hi], axis=0)
+            dx = (sc + fl + fr).astype(BF16)
             return y, dx, g1, g3, g2
 
         return jax.shard_map(device_fn, mesh=mesh, in_specs=(tok_spec, tok_spec, tok_spec, w_spec, w_spec, w_spec, tok_spec),

time: 133 us -> 120 us (0.902)
  the two profiles are of different devices: /device:TPU:116 before, /device:TPU:112 now
where the time goes in v2:
time: 120 us; the launch traced here: 119 us
  Pallas kernels  101 us (84%)
  starting transfers between devices  12.1 us (10%)
  waiting for transfers between devices  3.6 us (3%)
    pallas_call x1, Pallas kernels, device_fn(): pl.pallas_call(functools.partial(layer_kernel, cfg), out_shape=(sds((tok,...  77.5 us
    pallas_call x1, Pallas kernels, device_fn(): pl.pallas_call(functools.partial(first_grads_kernel, owner), grid=(n_firs...  14.3 us
    pallas_call x1, Pallas kernels, device_fn(): pl.pallas_call(later_grads_kernel, grid=(n_loc - n_first,), out_shape=g_s...  8.96 us
    ppermute x1, starting transfers between devices, device_fn(): ra = lax.ppermute(soa, 'ep', to_right)  5.17 us
    ppermute x1, waiting for transfers between devices, device_fn(): rb = lax.ppermute(sob, 'ep', to_left)  2.98 us
  transfers between devices with their start and end apart: 6, of which 2 were waited for; matrix products, arithmetic and copies ran while one was open for 0% of the time, Pallas kernels for 20%

profile of v2, /device:TPU:112, one launch (start us, length us, event | category | flops | bytes accessed | tf_op | source)
XLA Modules:
  0.0 118.8 jit_solution(14264344221258962432)
XLA Ops:
  0.6 77.5 %moe_layer.1 = (bf16[128,1536]{1,0:T(8,128)(2,1)}, f32[64,1536]{1,0:T(8,128)}, f32[64,1536]{1,0:T(8,128)}, f32[64,1536]{1,0:T(8,128)}, f32[64,1536]{1,0:T(8,128)...) custom-call(bf16[128,1536]{1,0:T(8,128)(2,1)} %x_hbm.1, ...), custom_call_target="tpu_custom_call" | custom-call | tf_op jit(solution)/shard_map/moe_layer/pallas_call | solution.py:497
  78.1 5.2 %collective-permute-start = (f32[64,1536]{1,0:T(8,128)}, f32[64,1536]{1,0:T(8,128)S(1)}, u32[]{:S(2)}, u32[]{:S(2)}) collective-permute-start(f32[64,1536]{1,0:T(8,128)} %get-tuple-element.32), channel_id=1, source_target_pairs={{0,2},{1,3},{2,4},{3,5},{4,6},{5,7},{6,0},{7,1},{8,10},{9,11},{10,... | collective-permute-start | bytes 1179656 | tf_op jit(solution)/shard_map/ppermute | solution.py:535
  83.3 2.4 %collective-permute-start.2 = (f32[64,1536]{1,0:T(8,128)}, f32[64,1536]{1,0:T(8,128)S(1)}, u32[]{:S(2)}, u32[]{:S(2)}) collective-permute-start(f32[64,1536]{1,0:T(8,128)} %get-tuple-element.33), channel_id=1, source_target_pairs={{0,2},{1,3},{2,4},{3,5},{4,6},{5,7},{6,0},{7,1},{8,10},{9,11},{10,... | collective-permute-start | bytes 1179656 | tf_op jit(solution)/shard_map/ppermute | solution.py:537
  85.6 0.9 collective-permute-start.3
  86.5 0.0 collective-permute-start.4
  86.5 0.0 copy-start.3
  86.5 0.0 copy-start.2
  86.5 14.3 %first_grads.1 = (bf16[5,1536,512]{2,1,0:T(8,128)(2,1)}, bf16[5,1536,512]{2,1,0:T(8,128)(2,1)}, bf16[5,512,1536]{2,1,0:T(8,128)(2,1)}) custom-call(bf16[5,448,1536]{2,1,0:T(8,128)(2,1)} %get-tuple-element.37.x_ref, bf16[5,448,1536]{2,1,0:T(8,128)(2,1)} %get-tuple-element.38.d_ref, bf16[5,448,512]{2,1,0:T(8,128)(2,1)} %get-tuple-element.39.u_ref, ...), custom_call_target="tpu_custom_call" | custom-call | flops 6341787648 | bytes 26542080 | tf_op jit(solution)/shard_map/first_grads/pallas_call | solution.py:556
  100.9 0.0 collective-permute-done
  100.9 0.0 copy-done.3
  100.9 2.1 %collective-permute-start.1 = (f32[64,1536]{1,0:T(8,128)S(1)}, f32[64,1536]{1,0:T(8,128)S(1)}, u32[]{:S(2)}, u32[]{:S(2)}) collective-permute-start(f32[64,1536]{1,0:T(8,128)S(1)} %add.12), channel_id=1, source_target_pairs={{0,2},{1,3},{2,4},{3,5},{4,6},{5,7},{6,0},{7,1},{8,10},{9,11},{10,... | collective-permute-start | bytes 1179656 | tf_op jit(solution)/shard_map/ppermute | solution.py:566
  103.0 3.0 %collective-permute-done.4 = f32[64,1536]{1,0:T(8,128)S(1)} collective-permute-done((f32[64,1536]{1,0:T(8,128)}, f32[64,1536]{1,0:T(8,128)S(1)}, u32[]{:S(2)}, u32[]{:S(2)}) %collective-permute-start.4) | collective-permute-done | bytes 393248 | tf_op jit(solution)/shard_map/ppermute | solution.py:536
  106.0 0.0 copy-done.2
  106.1 1.6 %collective-permute-start.5 = (f32[64,1536]{1,0:T(8,128)S(1)}, f32[64,1536]{1,0:T(8,128)S(1)}, u32[]{:S(2)}, u32[]{:S(2)}) collective-permute-start(f32[64,1536]{1,0:T(8,128)S(1)} %add.14), channel_id=1, source_target_pairs={{0,6},{1,7},{2,0},{3,1},{4,2},{5,3},{6,4},{7,5},{8,14},{9,15},{10,... | collective-permute-start | bytes 1179656 | tf_op jit(solution)/shard_map/ppermute | solution.py:567
  107.6 0.0 copy-start
  107.6 0.0 copy-start.1
  107.6 9.0 %later_grads.1 = (bf16[5,1536,512]{2,1,0:T(8,128)(2,1)}, bf16[5,1536,512]{2,1,0:T(8,128)(2,1)}, bf16[5,512,1536]{2,1,0:T(8,128)(2,1)}) custom-call(bf16[5,448,1536]{2,1,0:T(8,128)(2,1)} %get-tuple-element.37.x_ref, bf16[5,448,1536]{2,1,0:T(8,128)(2,1)} %get-tuple-element.38.d_ref, ...), custom_call_target="tpu_custom_call", output_to_operand_aliasing={{0}: (5, {}), {1}: (6, {}), {2}: (7, {})} | custom-call | flops 4227858432 | bytes 17694720 | tf_op jit(solution)/shard_map/later_grads/pallas_call | solution.py:568
  116.6 0.0 collective-permute-done.2
  116.6 0.0 collective-permute-done.3
  116.6 0.0 collective-permute-done.1
  116.6 0.6 collective-permute-done.5
  117.2 0.0 copy-done
  117.2 0.9 fusion.1
  118.1 0.0 copy-done.1
  118.1 0.7 copy.19
  (2 shorter events, 0.1 us)
Async XLA Ops:
  78.1 22.8 %collective-permute-start = (f32[64,1536]{1,0:T(8,128)}, f32[64,1536]{1,0:T(8,128)S(1)}, u32[]{:S(2)}, u32[]{:S(2)}) collective-permute-start(f32[64,1536]{1,0:T(8,128)} %get-tuple-element.32), channel_id=1, source_target_pairs={{0,2},{1,3},{2,4},{3,5},{4,6},{5,7},{6,0},{7,1},{8,10},{9,11},{10,... | collective-permute-start | bytes 1179656 | tf_op jit(solution)/shard_map/ppermute | solution.py:535
  83.3 33.3 %collective-permute-start.2 = (f32[64,1536]{1,0:T(8,128)}, f32[64,1536]{1,0:T(8,128)S(1)}, u32[]{:S(2)}, u32[]{:S(2)}) collective-permute-start(f32[64,1536]{1,0:T(8,128)} %get-tuple-element.33), channel_id=1, source_target_pairs={{0,2},{1,3},{2,4},{3,5},{4,6},{5,7},{6,0},{7,1},{8,10},{9,11},{10,... | collective-permute-start | bytes 1179656 | tf_op jit(solution)/shard_map/ppermute | solution.py:537
  85.6 31.0 %collective-permute-start.3 = (f32[64,1536]{1,0:T(8,128)}, f32[64,1536]{1,0:T(8,128)S(1)}, u32[]{:S(2)}, u32[]{:S(2)}) collective-permute-start(f32[64,1536]{1,0:T(8,128)} %get-tuple-element.34), channel_id=1, source_target_pairs={{0,6},{1,7},{2,0},{3,1},{4,2},{5,3},{6,4},{7,5},{8,14},{9,15},{10,... | collective-permute-start | bytes 1179656 | tf_op jit(solution)/shard_map/ppermute | solution.py:538
  86.5 19.5 %collective-permute-start.4 = (f32[64,1536]{1,0:T(8,128)}, f32[64,1536]{1,0:T(8,128)S(1)}, u32[]{:S(2)}, u32[]{:S(2)}) collective-permute-start(f32[64,1536]{1,0:T(8,128)} %get-tuple-element.36), channel_id=1, source_target_pairs={{0,6},{1,7},{2,0},{3,1},{4,2},{5,3},{6,4},{7,5},{8,14},{9,15},{10,... | collective-permute-start | bytes 1179656 | tf_op jit(solution)/shard_map/ppermute | solution.py:536
  86.5 14.3 %copy-start.3 = (f32[64,1536]{1,0:T(8,128)S(1)}, f32[64,1536]{1,0:T(8,128)}, u32[]{:S(2)}) copy-start(f32[64,1536]{1,0:T(8,128)} %get-tuple-element.31) | copy-start | bytes 1179652
  86.5 19.5 %copy-start.2 = (f32[64,1536]{1,0:T(8,128)S(1)}, f32[64,1536]{1,0:T(8,128)}, u32[]{:S(2)}) copy-start(f32[64,1536]{1,0:T(8,128)} %get-tuple-element.35) | copy-start | bytes 1179652
  100.9 15.7 %collective-permute-start.1 = (f32[64,1536]{1,0:T(8,128)S(1)}, f32[64,1536]{1,0:T(8,128)S(1)}, u32[]{:S(2)}, u32[]{:S(2)}) collective-permute-start(f32[64,1536]{1,0:T(8,128)S(1)} %add.12), channel_id=1, source_target_pairs={{0,2},{1,3},{2,4},{3,5},{4,6},{5,7},{6,0},{7,1},{8,10},{9,11},{10,... | collective-permute-start | bytes 1179656 | tf_op jit(solution)/shard_map/ppermute | solution.py:566
  106.1 11.2 %collective-permute-start.5 = (f32[64,1536]{1,0:T(8,128)S(1)}, f32[64,1536]{1,0:T(8,128)S(1)}, u32[]{:S(2)}, u32[]{:S(2)}) collective-permute-start(f32[64,1536]{1,0:T(8,128)S(1)} %add.14), channel_id=1, source_target_pairs={{0,6},{1,7},{2,0},{3,1},{4,2},{5,3},{6,4},{7,5},{8,14},{9,15},{10,... | collective-permute-start | bytes 1179656 | tf_op jit(solution)/shard_map/ppermute | solution.py:567
  107.6 9.6 %copy-start = (f32[128,1536]{1,0:T(8,128)S(1)}, f32[128,1536]{1,0:T(8,128)}, u32[]{:S(2)}) copy-start(f32[128,1536]{1,0:T(8,128)} %get-tuple-element.30) | copy-start | bytes 2359300
  107.6 10.5 %copy-start.1 = (bf16[128,1536]{1,0:T(8,128)(2,1)S(1)}, bf16[128,1536]{1,0:T(8,128)(2,1)}, u32[]{:S(2)}) copy-start(bf16[128,1536]{1,0:T(8,128)(2,1)} %get-tuple-element.58) | copy-start | bytes 1179652

commit v3 on v2

v3 whole, which is shorter than its diff:
```python
import functools

import jax
import jax.numpy as jnp
from jax import lax
from jax.experimental import pallas as pl
from jax.experimental.pallas import tpu as pltpu
from jax.sharding import PartitionSpec as P

MESH = pl.DeviceIdType.MESH
F32 = jnp.float32
BF16 = jnp.bfloat16


def dot_nn(a, b):
    return lax.dot_general(a, b, (((1,), (0,)), ((), ())), preferred_element_type=F32)


def dot_nt(a, b):
    return lax.dot_general(a, b, (((1,), (1,)), ((), ())), preferred_element_type=F32)


def dot_tn(a, b):
    return lax.dot_general(a, b, (((0,), (0,)), ((), ())), preferred_element_type=F32)


def layer_kernel(cfg, x_hbm, dy_hbm, ids_ref, gates_ref, w1_hbm, w3_hbm, w2_hbm,
                 y_hbm, soa_hbm, sob_hbm, sra_hbm, srb_hbm, sla_hbm, slb_hbm, sc_hbm, xr_hbm, dr_hbm, ur_hbm, da_hbm, db_hbm, xh_hbm, dh_hbm, uh_hbm, dah_hbm, dbh_hbm,
                 x_all, dy_all, ids_all, gates_all, rt, gt, mc, ypart, dxpart, cbuf, yra, yrb, yfl, yfr,
                 erows, hrows, urow, uhot, darow, dbrow, act1, act2, orow, pbuf, w1, w3, w2, outb,
                 m_send, m_recv, ag_send, ag_recv, rs_send, rs_recv, w_sem, st_sem, hst_sem, io_sem, so_sem, free_sem):
    chips, tok, width, hid, n_loc, cap, owner = cfg
    group = 2 * chips
    two = 2 * tok
    cp = 2 * cap
    n_rows = chips * cp
    hot_rows = chips * two
    half = tok // 2
    last = n_loc - 1
    me = lax.axis_index("ep")
    c = me // 2
    k = lax.rem(me, 2)
    c_r = lax.rem(c + 1, chips)
    c_l = lax.rem(c + chips - 1, chips)
    c_o = lax.rem(c + 2, chips)
    near = (c, c_l, c_r, c_o)
    right = 2 * c_r + k
    left = 2 * c_l + k
    partner = 2 * c + 1 - k
    is_owner = me == owner

    own_x = pltpu.make_async_copy(x_hbm, x_all.at[c, pl.ds(k * tok, tok)], io_sem.at[0])
    own_dy = pltpu.make_async_copy(dy_hbm, dy_all.at[c, pl.ds(k * tok, tok)], io_sem.at[1])
    own_x.start()
    own_dy.start()

    def w_copies(i):
        e = lax.rem(i, n_loc)
        s = lax.rem(i, 2)
        return (pltpu.make_async_copy(w1_hbm.at[e], w1.at[s], w_sem.at[0, s]),
                pltpu.make_async_copy(w3_hbm.at[e], w3.at[s], w_sem.at[1, s]),
                pltpu.make_async_copy(w2_hbm.at[e], w2.at[s], w_sem.at[2, s]))

    for cpy in w_copies(0):
        cpy.start()
    ids_all[me] = ids_ref[...]
    gates_all[me] = gates_ref[...]

    barrier = pltpu.get_barrier_semaphore()
    for d in range(1, group):
        pl.semaphore_signal(barrier, inc=1, device_id={"ep": lax.rem(me + d, group)}, device_id_type=MESH)
    pl.semaphore_wait(barrier, group - 1)

    def meta_copies(d):
        return tuple(pltpu.make_async_remote_copy(
            src_ref=src, dst_ref=dst.at[me], send_sem=m_send.at[i, d], recv_sem=m_recv.at[i, d],
            device_id={"ep": lax.rem(me + d, group)}, device_id_type=MESH)
            for i, (src, dst) in enumerate(((ids_ref, ids_all), (gates_ref, gates_all))))

    def ag(ref, t, i):
        chip, core, r0, n, dev = (
            (c, k, 0, half, right), (c, k, half, half, right), (c, k, half, half, left), (c, k, 0, half, left),
            (c, k, 0, tok, partner),
            (c_l, k, 0, half, right), (c_r, k, half, half, left),
            (c_l, k, 0, tok, partner), (c_r, k, 0, tok, partner),
            (c_o, k, 0, half, partner), (c_o, k, half, half, partner))[i]
        blk = ref.at[chip, pl.ds(core * tok + r0, n)]
        return pltpu.make_async_remote_copy(
            src_ref=blk, dst_ref=blk, send_sem=ag_send.at[t, i], recv_sem=ag_recv.at[t, i],
            device_id={"ep": dev}, device_id_type=MESH)

    own_x.wait()
    for d in range(1, group):
        for cpy in meta_copies(d):
            cpy.start()
    for i in (4, 0, 2, 1, 3):
        ag(x_all, 0, i).start()
    own_dy.wait()

    @pl.loop(0, chips * two // 64)
    def _(r):
        q = r // (two // 64)
        o = pl.multiple_of(lax.rem(r, two // 64) * 64, 64)
        ypart[q, pl.ds(o, 64)] = jnp.zeros((64, width), F32)
        dxpart[q, pl.ds(o, 64)] = jnp.zeros((64, width), F32)

    for d in range(1, group):
        for cpy in meta_copies(d):
            cpy.wait_recv()

    upper = (lax.broadcasted_iota(jnp.int32, (tok, tok), 0) < lax.broadcasted_iota(jnp.int32, (tok, tok), 1)).astype(F32).astype(BF16)
    row_id = lax.broadcasted_iota(jnp.int32, (8, tok), 0)
    for s in range(group):
        q, core = s // 2, s % 2
        ids = ids_all[s]
        gates = gates_all[s]
        mask_m = jnp.zeros((8, tok), F32)
        gate_m = jnp.zeros((8, tok), F32)
        for le in range(n_loc):
            eq = ids == me * n_loc + le
            hit = jnp.sum(jnp.where(eq, 1.0, 0.0), axis=0, keepdims=True)
            gv = jnp.sum(jnp.where(eq, gates, 0.0), axis=0, keepdims=True)
            mask_m = jnp.where(row_id == le, hit, mask_m)
            gate_m = jnp.where(row_id == le, gv, gate_m)
        rank = dot_nn(mask_m.astype(BF16), upper)
        pos = jnp.where(mask_m > 0.0, rank + float(cap * core), -1.0)
        rt[q, :, core * tok:(core + 1) * tok] = pos
        gt[q, :, core * tok:(core + 1) * tok] = gate_m
        both = jnp.concatenate([pos, gate_m, jnp.zeros((tok - 16, tok), F32)], axis=0)
        mc[q, core * tok:(core + 1) * tok, :] = jnp.transpose(both)

    def pick(p, q, src, scaled):
        for e in range(n_loc):
            hit = rt[q, e:e + 1, :] == lax.broadcasted_iota(jnp.int32, (cp, two), 0).astype(F32)
            pbuf[e * cp:(e + 1) * cp, :] = jnp.where(hit, 1.0, 0.0).astype(BF16)
        gates = [None] * n_loc
        if scaled:
            for e in range(n_loc):
                hit = rt[q, e:e + 1, :] == lax.broadcasted_iota(jnp.int32, (cp, two), 0).astype(F32)
                gates[e] = jnp.sum(jnp.where(hit, gt[q, e:e + 1, :], 0.0), axis=1, keepdims=True)
        for j in range(width // 256):
            cs = slice(j * 256, (j + 1) * 256)
            got = dot_nn(pbuf[...], src[q, :, cs])
            for e in range(n_loc):
                part = got[e * cp:(e + 1) * cp]
                erows[e, pl.ds(p * cp, cp), cs] = (gates[e] * part if scaled else part).astype(BF16)

    def column(q, lane):
        return jnp.sum(jnp.where(lax.broadcasted_iota(jnp.int32, (two, 128), 1) == lane, mc[q], 0.0), axis=1, keepdims=True)

    def put_rows(q, e):
        hit = column(q, e) == lax.broadcasted_iota(jnp.int32, (two, cp), 1).astype(F32)
        return jnp.where(hit, 1.0, 0.0).astype(BF16)

    def forward(m, src, dst, s, aoff):
        for j in range(hid // 256):
            cs = slice(j * 256, (j + 1) * 256)
            act1[pl.ds(aoff, m), cs] = dot_nn(src[...], w1[s, :, cs])
            act2[pl.ds(aoff, m), cs] = dot_nn(src[...], w3[s, :, cs])

        @pl.loop(0, m // 16)
        def _(r):
            o = pl.multiple_of(aoff + r * 16, 16)
            a = act1[pl.ds(o, 16), :]
            b = act2[pl.ds(o, 16), :]
            sg = jax.nn.sigmoid(a)
            ga = a * sg
            act1[pl.ds(o, 16), :] = b * (sg * (1.0 + a * (1.0 - sg)))
            act2[pl.ds(o, 16), :] = ga
            dst[pl.ds(pl.multiple_of(r * 16, 16), 16), :] = (ga * b).astype(BF16)

        for j in range(width // 256):
            cs = slice(j * 256, (j + 1) * 256)
            orow[0:m, cs] = dot_nn(dst[...], w2[s, :, cs]).astype(BF16)

    def backward(m, src, s, aoff):
        for j in range(hid // 256):
            cs = slice(j * 256, (j + 1) * 256)
            du = dot_nt(src[...], w2[s, cs, :])
            darow[s, 0:m, cs] = (du * act1[pl.ds(aoff, m), cs]).astype(BF16)
            dbrow[s, 0:m, cs] = (du * act2[pl.ds(aoff, m), cs]).astype(BF16)
        for j in range(width // 256):
            cs = slice(j * 256, (j + 1) * 256)
            orow[0:m, cs] = (dot_nt(darow[s, 0:m, :], w1[s, cs, :]) + dot_nt(dbrow[s, 0:m, :], w3[s, cs, :])).astype(BF16)

    def act_off(e):
        return pl.multiple_of(jnp.where(e == 0, 0, hot_rows + (e - 1) * n_rows), 64)

    def add_out(q, e, first):
        ypart[q] += column(q, e + 8) * dot_nn(put_rows(q, e), orow[first:first + cp, :])

    def hot_forward(p, q, s):
        on = column(q, 0) >= 0.0
        hrows[0:two, :] = jnp.where(on, x_all[q].astype(F32), 0.0).astype(BF16)
        xs = pltpu.make_async_copy(hrows.at[0:two], xh_hbm.at[pl.ds(p * two, two)], hst_sem.at[0])
        xs.start()
        o = pl.multiple_of(p * two, 64)
        forward(two, hrows.at[0:two], uhot.at[pl.ds(o, two)], s, o)
        ypart[q] += column(q, 8) * orow[0:two, :].astype(F32)
        xs.wait()

    def turn(i):
        for cpy in w_copies(i + 1):
            cpy.start()
        for cpy in w_copies(i):
            cpy.wait()

    ag(x_all, 0, 4).wait_recv()
    pick(0, c, x_all, False)

    @pl.loop(0, n_loc)
    def _(e):
        s = lax.rem(e, 2)
        hot = jnp.logical_and(is_owner, e == 0)
        turn(e)

        @pl.when(e == 3)
        def _():
            ag(x_all, 0, 0).wait_recv()
            ag(x_all, 0, 5).start()
            ag(x_all, 0, 2).wait_recv()
            ag(x_all, 0, 6).start()
            for i in (4, 0, 2, 1, 3):
                ag(dy_all, 1, i).start()

        @pl.when(jnp.logical_not(hot))
        def _():
            forward(cp, erows.at[e, 0:cp], urow.at[e, 0:cp], s, act_off(e))
            add_out(c, e, 0)

        @pl.when(hot)
        def _():
            hot_forward(0, c, s)

    def rs(t, j):
        part = (ypart, dxpart)[t]
        o = k * tok
        if j < 4:
            q = (c_o, c_r, c_l, c)[j]
            src, dst, dev = part.at[q, pl.ds((1 - k) * tok, tok)], cbuf.at[q], partner
        else:
            src, dst, dev = (
                (part.at[c_o, pl.ds(o, half)], yra, right),
                (part.at[c_o, pl.ds(o + half, half)], yrb, left),
                (part.at[c_r, pl.ds(o + half, half)], yfl.at[half:tok], right),
                (part.at[c_l, pl.ds(o, half)], yfr.at[0:half], left),
                (part.at[c_r, pl.ds(o, half)], yfl.at[0:half], right),
                (part.at[c_l, pl.ds(o + half, half)], yfr.at[half:tok], left))[j - 4]
        return pltpu.make_async_remote_copy(
            src_ref=src, dst_ref=dst, send_sem=rs_send.at[t, j], recv_sem=rs_recv.at[t, j],
            device_id={"ep": dev}, device_id_type=MESH)

    def add_rows(part, q, off, src, n):
        @pl.loop(0, n // 32)
        def _(r):
            o = pl.multiple_of(r * 32, 32)
            part[q, pl.ds(pl.multiple_of(off + r * 32, 32), 32)] += src[pl.ds(o, 32)]

    ag(x_all, 0, 1).wait_recv()
    ag(x_all, 0, 7).start()
    ag(x_all, 0, 3).wait_recv()
    ag(x_all, 0, 8).start()
    rs(0, 3).start()
    ag(x_all, 0, 7).wait_recv()
    pick(1, c_l, x_all, False)
    ag(x_all, 0, 8).wait_recv()
    pick(2, c_r, x_all, False)
    ag(x_all, 0, 5).wait_recv()
    ag(x_all, 0, 9).start()
    ag(x_all, 0, 6).wait_recv()
    ag(x_all, 0, 10).start()
    rs(0, 3).wait_recv()
    add_rows(ypart, c, k * tok, cbuf.at[c], tok)
    ag(x_all, 0, 9).wait_recv()
    ag(x_all, 0, 10).wait_recv()
    pick(3, c_o, x_all, False)

    def st_fwd(e):
        return (pltpu.make_async_copy(erows.at[e], xr_hbm.at[e], st_sem.at[0, e]),
                pltpu.make_async_copy(urow.at[e], ur_hbm.at[e], st_sem.at[1, e]))

    @pl.loop(0, n_loc)
    def _(e):
        s = lax.rem(e + n_loc, 2)
        hot = jnp.logical_and(is_owner, e == 0)
        turn(e + n_loc)

        @pl.when(e == 2)
        def _():
            ag(dy_all, 1, 0).wait_recv()
            ag(dy_all, 1, 5).start()
            ag(dy_all, 1, 2).wait_recv()
            ag(dy_all, 1, 6).start()

        @pl.when(jnp.logical_not(hot))
        def _():
            forward(n_rows - cp, erows.at[e, cp:n_rows], urow.at[e, cp:n_rows], s, pl.multiple_of(act_off(e) + cp, 16))
            for j, p in enumerate((3, 2, 1)):
                add_out(near[p], e, (p - 1) * cp)

                @pl.when(e == last)
                def _():
                    rs(0, j).start()

            for cpy in st_fwd(e):
                cpy.start()

        @pl.when(hot)
        def _():
            @pl.loop(1, chips)
            def _(p):
                q = jnp.where(p == 1, c_l, jnp.where(p == 2, c_r, c_o))
                hot_forward(p, q, s)

    for j, q in enumerate((c_o, c_r, c_l)):
        rs(0, j).wait_recv()
        add_rows(ypart, q, k * tok, cbuf.at[q], tok)
        if j == 0:
            rs(0, 4).start()
            rs(0, 5).start()
        else:
            rs(0, 5 + j).start()
    pl.semaphore_signal(free_sem, inc=1, device_id={"ep": partner}, device_id_type=MESH)

    ag(dy_all, 1, 4).wait_recv()
    ag(dy_all, 1, 1).wait_recv()
    ag(dy_all, 1, 7).start()
    ag(dy_all, 1, 3).wait_recv()
    ag(dy_all, 1, 8).start()
    ag(dy_all, 1, 5).wait_recv()
    ag(dy_all, 1, 9).start()
    ag(dy_all, 1, 6).wait_recv()
    ag(dy_all, 1, 10).start()
    for i in (7, 8, 9, 10):
        ag(dy_all, 1, i).wait_recv()

    @pl.loop(0, n_loc)
    def _(e):
        @pl.when(jnp.logical_not(jnp.logical_and(is_owner, e == 0)))
        def _():
            for cpy in st_fwd(e):
                cpy.wait()

    @pl.when(is_owner)
    def _():
        us = pltpu.make_async_copy(uhot, uh_hbm, hst_sem.at[0])
        us.start()
        us.wait()

    @pl.loop(0, chips)
    def _(p):
        q = jnp.where(p == 0, c, jnp.where(p == 1, c_l, jnp.where(p == 2, c_r, c_o)))
        pick(p, q, dy_all, True)

    def st_d(e):
        return pltpu.make_async_copy(erows.at[e], dr_hbm.at[e], st_sem.at[0, e])

    def st_ab(e, s):
        return (pltpu.make_async_copy(darow.at[s, 0:n_rows], da_hbm.at[e], st_sem.at[1, s]),
                pltpu.make_async_copy(dbrow.at[s, 0:n_rows], db_hbm.at[e], st_sem.at[1, 2 + s]))

    for e in range(n_loc):
        st_d(e).start()

    def rs_relay_y():
        rs(0, 4).wait_recv()
        add_rows(ypart, c_r, k * tok, yra, half)
        rs(0, 8).start()
        rs(0, 5).wait_recv()
        add_rows(ypart, c_l, k * tok + half, yrb, half)
        rs(0, 9).start()

    @pl.loop(0, n_loc)
    def _(e):
        s = lax.rem(e, 2)
        hot = jnp.logical_and(is_owner, e == 0)

        @pl.when(e < last)
        def _():
            for cpy in w_copies(e + 2 * n_loc + 1):
                cpy.start()

        for cpy in w_copies(e + 2 * n_loc):
            cpy.wait()

        @pl.when(e == last)
        def _():
            rs_relay_y()

        @pl.when(jnp.logical_not(hot))
        def _():
            backward(n_rows, erows.at[e], s, act_off(e))
            for p in range(chips):
                dxpart[near[p]] += dot_nn(put_rows(near[p], e), orow[p * cp:(p + 1) * cp, :])

        @pl.when(hot)
        def _():
            @pl.loop(0, chips // 2)
            def _(h):
                pair = (jnp.where(h == 0, c, c_r), jnp.where(h == 0, c_l, c_o))
                for i, q in enumerate(pair):
                    hrows[i * two:(i + 1) * two, :] = (column(q, 8) * dy_all[q].astype(F32)).astype(BF16)
                o = pl.multiple_of(h * 2 * two, 64)
                ds_ = pltpu.make_async_copy(hrows, dh_hbm.at[pl.ds(o, 2 * two)], hst_sem.at[0])
                ds_.start()
                backward(2 * two, hrows, s, o)
                sa = pltpu.make_async_copy(darow.at[s], dah_hbm.at[pl.ds(o, 2 * two)], hst_sem.at[1])
                sb = pltpu.make_async_copy(dbrow.at[s], dbh_hbm.at[pl.ds(o, 2 * two)], hst_sem.at[2])
                sa.start()
                sb.start()
                for i, q in enumerate(pair):
                    dxpart[q] += orow[i * two:(i + 1) * two, :].astype(F32)
                ds_.wait()
                sa.wait()
                sb.wait()

        @pl.when(jnp.logical_and(e >= 1, jnp.logical_not(jnp.logical_and(is_owner, e == 1))))
        def _():
            for cpy in st_ab(e - 1, 1 - s):
                cpy.wait()

        @pl.when(jnp.logical_not(hot))
        def _():
            for cpy in st_ab(e, s):
                cpy.start()

    def rs_end_y():
        for j in (6, 7, 8, 9):
            rs(0, j).wait_recv()

        @pl.loop(0, tok // 32)
        def _(r):
            o = pl.multiple_of(r * 32, 32)
            total = ypart[c, pl.ds(pl.multiple_of(k * tok + r * 32, 32), 32)] + yfl[pl.ds(o, 32)] + yfr[pl.ds(o, 32)]
            outb[pl.ds(o, 32)] = total.astype(BF16)

        return pltpu.make_async_copy(outb, y_hbm, io_sem.at[0])

    def chip_sums_out(j):
        q = (c_o, c_r, c_l, c)[j]
        if j == 3:
            return (pltpu.make_async_copy(dxpart.at[q, pl.ds(k * tok, tok)], sc_hbm, so_sem.at[6]),)
        lo, hi = ((soa_hbm, sob_hbm), (sra_hbm, srb_hbm), (sla_hbm, slb_hbm))[j]
        return (pltpu.make_async_copy(dxpart.at[q, pl.ds(k * tok, half)], lo, so_sem.at[2 * j]),
                pltpu.make_async_copy(dxpart.at[q, pl.ds(k * tok + half, half)], hi, so_sem.at[2 * j + 1]))

    pl.semaphore_wait(free_sem, 1)
    for j in range(4):
        rs(1, j).start()
    for j, q in enumerate((c_o, c_r, c_l, c)):
        rs(1, j).wait_recv()
        add_rows(dxpart, q, k * tok, cbuf.at[q], tok)
        for cpy in chip_sums_out(j):
            cpy.start()
    y_out = rs_end_y()
    y_out.start()

    for e in range(n_loc):
        st_d(e).wait()
    for cpy in st_ab(last, last % 2):
        cpy.wait()
    for d in range(1, group):
        for cpy in meta_copies(d):
            cpy.wait_send()
    for i in range(11):
        ag(x_all, 0, i).wait_send()
        ag(dy_all, 1, i).wait_send()
    for j in range(10):
        rs(0, j).wait_send()
    for j in range(4):
        rs(1, j).wait_send()
        for cpy in chip_sums_out(j):
            cpy.wait()
    y_out.wait()


def expert_grads(x_ref, d_ref, u_ref, da_ref, db_ref, g1, g3, g2):
    g1[0] = dot_tn(x_ref[0], da_ref[0]).astype(BF16)
    g3[0] = dot_tn(x_ref[0], db_ref[0]).astype(BF16)
    g2[0] = dot_tn(u_ref[0], d_ref[0]).astype(BF16)


def first_grads_kernel(owner, x_ref, d_ref, u_ref, da_ref, db_ref, xh, dh, uh, dah, dbh, g1, g3, g2, xb, dbuf, ub, dab, dbb, sem):
    i = pl.program_id(0)
    is_owner = lax.axis_index("ep") == owner
    hot = jnp.logical_and(is_owner, i == pl.num_programs(0) - 1)

    def copies():
        return [pltpu.make_async_copy(src, dst, sem.at[j]) for j, (src, dst) in enumerate(((xh, xb), (dah, dab), (dbh, dbb), (uh, ub), (dh, dbuf)))]

    @pl.when(jnp.logical_and(is_owner, i == 0))
    def _():
        for cpy in copies():
            cpy.start()

    @pl.when(jnp.logical_not(hot))
    def _():
        expert_grads(x_ref, d_ref, u_ref, da_ref, db_ref, g1, g3, g2)

    @pl.when(hot)
    def _():
        for cpy in copies():
            cpy.wait()
        g1[0] = dot_tn(xb[...], dab[...]).astype(BF16)
        g3[0] = dot_tn(xb[...], dbb[...]).astype(BF16)
        g2[0] = dot_tn(ub[...], dbuf[...]).astype(BF16)


def later_grads_kernel(x_ref, d_ref, u_ref, da_ref, db_ref, g1_in, g3_in, g2_in, g1, g3, g2):
    del g1_in, g3_in, g2_in
    expert_grads(x_ref, d_ref, u_ref, da_ref, db_ref, g1, g3, g2)


def solution(mesh):
    group = mesh.shape["ep"]
    num_dev = mesh.shape["dp"] * group
    tok_spec = P(("dp", "ep"), None)
    w_spec = P("ep", None, None)
    grad_spec = P(("dp", "ep"), None, None)

    def layer_fn(tokens, expert_ids, gate_vals, w_gate, w_up, w_down, grad_out):
        n_exp, width, hid = w_gate.shape
        tok = tokens.shape[0] // num_dev
        top_k = expert_ids.shape[1]
        cap = ((2 * tok * top_k + 8 * n_exp - 1) // (8 * n_exp)) * 8
        n_loc = n_exp // group
        hot = n_exp // 2
        owner = hot // n_loc
        chips = group // 2
        n_rows = chips * 2 * cap
        hot_rows = group * tok
        cfg = (chips, tok, width, hid, n_loc, cap, owner)

        def device_fn(x, ids, gates, w1, w3, w2, dy):
            any_spec = pl.BlockSpec(memory_space=pl.ANY)
            vmem_spec = pl.BlockSpec(memory_space=pltpu.VMEM)
            sds = jax.ShapeDtypeStruct
            hb = hot_rows // 2
            half = tok // 2
            act_rows = hot_rows + (n_loc - 1) * n_rows
            outs = pl.pallas_call(
                functools.partial(layer_kernel, cfg),
                out_shape=(
                    sds((tok, width), BF16), *[sds((half, width), F32)] * 6, sds((tok, width), F32),
                    sds((n_loc, n_rows, width), BF16), sds((n_loc, n_rows, width), BF16),
                    sds((n_loc, n_rows, hid), BF16), sds((n_loc, n_rows, hid), BF16), sds((n_loc, n_rows, hid), BF16),
                    sds((hot_rows, width), BF16), sds((hot_rows, width), BF16),
                    sds((hot_rows, hid), BF16), sds((hot_rows, hid), BF16), sds((hot_rows, hid), BF16)),
                in_specs=[any_spec, any_spec, vmem_spec, vmem_spec, any_spec, any_spec, any_spec],
                out_specs=[any_spec] * 18,
                scratch_shapes=[
                    pltpu.VMEM((chips, 2 * tok, width), BF16), pltpu.VMEM((chips, 2 * tok, width), BF16),
                    pltpu.VMEM((group, top_k, tok), jnp.int32), pltpu.VMEM((group, top_k, tok), F32),
                    pltpu.VMEM((chips, 8, 2 * tok), F32), pltpu.VMEM((chips, 8, 2 * tok), F32),
                    pltpu.VMEM((chips, 2 * tok, 128), F32),
                    pltpu.VMEM((chips, 2 * tok, width), F32), pltpu.VMEM((chips, 2 * tok, width), F32),
                    pltpu.VMEM((chips, tok, width), F32),
                    pltpu.VMEM((half, width), F32), pltpu.VMEM((half, width), F32),
                    pltpu.VMEM((tok, width), F32), pltpu.VMEM((tok, width), F32),
                    pltpu.VMEM((n_loc, n_rows, width), BF16), pltpu.VMEM((hb, width), BF16),
                    pltpu.VMEM((n_loc, n_rows, hid), BF16), pltpu.VMEM((hot_rows, hid), BF16),
                    pltpu.VMEM((2, hb, hid), BF16), pltpu.VMEM((2, hb, hid), BF16),
                    pltpu.VMEM((act_rows, hid), F32), pltpu.VMEM((act_rows, hid), F32),
                    pltpu.VMEM((hb, width), BF16), pltpu.VMEM((n_loc * 2 * cap, 2 * tok), BF16),
                    pltpu.VMEM((2, width, hid), BF16), pltpu.VMEM((2, width, hid), BF16), pltpu.VMEM((2, hid, width), BF16),
                    pltpu.VMEM((tok, width), BF16),
                    pltpu.SemaphoreType.DMA((2, group)), pltpu.SemaphoreType.DMA((2, group)),
                    pltpu.SemaphoreType.DMA((2, 11)), pltpu.SemaphoreType.DMA((2, 11)),
                    pltpu.SemaphoreType.DMA((2, 10)), pltpu.SemaphoreType.DMA((2, 10)),
                    pltpu.SemaphoreType.DMA((3, 2)), pltpu.SemaphoreType.DMA((2, n_loc)), pltpu.SemaphoreType.DMA((3,)),
                    pltpu.SemaphoreType.DMA((2,)), pltpu.SemaphoreType.DMA((7,)), pltpu.SemaphoreType.REGULAR,
                ],
                compiler_params=pltpu.CompilerParams(collective_id=0, has_side_effects=True, vmem_limit_bytes=67043328),
                name="moe_layer",
            )(x, dy, ids.T, gates.T, w1, w3, w2)
            y, soa, sob, sra, srb, sla, slb, sc, xr, dr, ur, dar, dbr, xh, dh, uh, dah, dbh = outs

            to_right = [(i, (i + 2) % group) for i in range(group)]
            to_left = [(i, (i + group - 2) % group) for i in range(group)]
            ra = lax.ppermute(soa, "ep", to_right)
            rb = lax.ppermute(sob, "ep", to_left)
            fl_hi = lax.ppermute(srb, "ep", to_right)
            fr_lo = lax.ppermute(sla, "ep", to_left)

            n_first = (n_loc + 1) // 2
            g_shapes = (sds((n_loc, width, hid), BF16), sds((n_loc, width, hid), BF16), sds((n_loc, hid, width), BF16))

            def blk(r, n, at):
                return pl.BlockSpec((1, r, n), lambda i: (at(i), 0, 0))

            def row_specs(at):
                return [blk(n_rows, width, at), blk(n_rows, width, at), blk(n_rows, hid, at), blk(n_rows, hid, at), blk(n_rows, hid, at)]

            def out_blks(at):
                return [blk(width, hid, at), blk(width, hid, at), blk(hid, width, at)]

            def cost(n):
                return pl.CostEstimate(flops=n * 6 * n_rows * width * hid, transcendentals=0,
                                       bytes_accessed=n * 2 * (2 * n_rows * width + 3 * n_rows * hid + 3 * width * hid))

            def first_at(i):
                return lax.rem(i + 1, n_first)

            def later_at(i):
                return i + n_first

            grads = pl.pallas_call(
                functools.partial(first_grads_kernel, owner),
                grid=(n_first,), out_shape=g_shapes,
                in_specs=row_specs(first_at) + [any_spec] * 5, out_specs=out_blks(first_at),
                scratch_shapes=[pltpu.VMEM((hot_rows, width), BF16), pltpu.VMEM((hot_rows, width), BF16), pltpu.VMEM((hot_rows, hid), BF16),
                                pltpu.VMEM((hot_rows, hid), BF16), pltpu.VMEM((hot_rows, hid), BF16), pltpu.SemaphoreType.DMA((5,))],
                compiler_params=pltpu.CompilerParams(vmem_limit_bytes=60 << 20),
                cost_estimate=cost(n_first), name="first_grads",
            )(xr, dr, ur, dar, dbr, xh, dh, uh, dah, dbh)

            fl_lo = lax.ppermute(sra + ra, "ep", to_right)
            fr_hi = lax.ppermute(slb + rb, "ep", to_left)
            g1, g3, g2 = pl.pallas_call(
                later_grads_kernel,
                grid=(n_loc - n_first,), out_shape=g_shapes,
                in_specs=row_specs(later_at) + [any_spec] * 3, out_specs=out_blks(later_at),
                input_output_aliases={5: 0, 6: 1, 7: 2},
                compiler_params=pltpu.CompilerParams(vmem_limit_bytes=60 << 20),
                cost_estimate=cost(n_loc - n_first), name="later_grads",
            )(xr, dr, ur, dar, dbr, *grads)
            fl = jnp.concatenate([fl_lo, fl_hi], axis=0)
            fr = jnp.concatenate([fr_lo, fr_hi], axis=0)
            dx = (sc + fl + fr).astype(BF16)
            return y, dx, g1, g3, g2

        return jax.shard_map(device_fn, mesh=mesh, in_specs=(tok_spec, tok_spec, tok_spec, w_spec, w_spec, w_spec, tok_spec),
                             out_specs=(tok_spec, tok_spec, grad_spec, grad_spec, grad_spec), check_vma=False)(
            tokens, expert_ids, gate_vals, w_gate, w_up, w_down, grad_out)

    return layer_fn
```

time: 120 us -> 118 us (0.983)
  starting transfers between devices: 12.1 us -> 10.8 us
    ppermute x1, starting transfers between devices: 5.17 us -> 3.94 us  [device_fn(): ra = lax.ppermute(soa, 'ep', to_right)]
where the time goes in v3:
time: 118 us
  Pallas kernels  101 us (86%)
  starting transfers between devices  10.8 us (9%)
  waiting for transfers between devices  3.27 us (3%)
    pallas_call x1, Pallas kernels, device_fn(): pl.pallas_call(functools.partial(layer_kernel, cfg), out_shape=(sds((tok,...  78 us
    pallas_call x1, Pallas kernels, device_fn(): pl.pallas_call(functools.partial(first_grads_kernel, owner), grid=(n_firs...  14.1 us
    pallas_call x1, Pallas kernels, device_fn(): pl.pallas_call(later_grads_kernel, grid=(n_loc - n_first,), out_shape=g_s...  8.96 us
    ppermute x1, starting transfers between devices, device_fn(): ra = lax.ppermute(soa, 'ep', to_right)  3.94 us
    ppermute x1, waiting for transfers between devices, device_fn(): rb = lax.ppermute(sob, 'ep', to_left)  2.66 us
  transfers between devices with their start and end apart: 6, of which 2 were waited for; matrix products, arithmetic and copies ran while one was open for 0% of the time, Pallas kernels for 20%

profile of v3, /device:TPU:112, one launch (start us, length us, event | category | flops | bytes accessed | tf_op | source)
XLA Modules:
  0.0 117.6 jit_solution(5322552987818989585)
XLA Ops:
  0.6 78.0 %moe_layer.1 = (bf16[128,1536]{1,0:T(8,128)(2,1)}, f32[64,1536]{1,0:T(8,128)}, f32[64,1536]{1,0:T(8,128)}, f32[64,1536]{1,0:T(8,128)}, f32[64,1536]{1,0:T(8,128)...) custom-call(bf16[128,1536]{1,0:T(8,128)(2,1)} %x_hbm.1, ...), custom_call_target="tpu_custom_call" | custom-call | tf_op jit(solution)/shard_map/moe_layer/pallas_call | solution.py:541
  78.6 3.9 %collective-permute-start = (f32[64,1536]{1,0:T(8,128)}, f32[64,1536]{1,0:T(8,128)S(1)}, u32[]{:S(2)}, u32[]{:S(2)}) collective-permute-start(f32[64,1536]{1,0:T(8,128)} %get-tuple-element.32), channel_id=1, source_target_pairs={{0,2},{1,3},{2,4},{3,5},{4,6},{5,7},{6,0},{7,1},{8,10},{9,11},{10,... | collective-permute-start | bytes 1179656 | tf_op jit(solution)/shard_map/ppermute | solution.py:580
  82.6 1.9 %collective-permute-start.2 = (f32[64,1536]{1,0:T(8,128)}, f32[64,1536]{1,0:T(8,128)S(1)}, u32[]{:S(2)}, u32[]{:S(2)}) collective-permute-start(f32[64,1536]{1,0:T(8,128)} %get-tuple-element.33), channel_id=1, source_target_pairs={{0,2},{1,3},{2,4},{3,5},{4,6},{5,7},{6,0},{7,1},{8,10},{9,11},{10,... | collective-permute-start | bytes 1179656 | tf_op jit(solution)/shard_map/ppermute | solution.py:582
  84.4 1.4 %collective-permute-start.3 = (f32[64,1536]{1,0:T(8,128)}, f32[64,1536]{1,0:T(8,128)S(1)}, u32[]{:S(2)}, u32[]{:S(2)}) collective-permute-start(f32[64,1536]{1,0:T(8,128)} %get-tuple-element.34), channel_id=1, source_target_pairs={{0,6},{1,7},{2,0},{3,1},{4,2},{5,3},{6,4},{7,5},{8,14},{9,15},{10,... | collective-permute-start | bytes 1179656 | tf_op jit(solution)/shard_map/ppermute | solution.py:583
  85.8 0.0 collective-permute-start.4
  85.8 0.0 copy-start.3
  85.8 0.0 copy-start.2
  85.8 14.1 %first_grads.1 = (bf16[5,1536,512]{2,1,0:T(8,128)(2,1)}, bf16[5,1536,512]{2,1,0:T(8,128)(2,1)}, bf16[5,512,1536]{2,1,0:T(8,128)(2,1)}) custom-call(bf16[5,448,1536]{2,1,0:T(8,128)(2,1)} %get-tuple-element.37.x_ref, bf16[5,448,1536]{2,1,0:T(8,128)(2,1)} %get-tuple-element.38.d_ref, bf16[5,448,512]{2,1,0:T(8,128)(2,1)} %get-tuple-element.39.u_ref, ...), custom_call_target="tpu_custom_call" | custom-call | flops 6341787648 | bytes 26542080 | tf_op jit(solution)/shard_map/first_grads/pallas_call | solution.py:607
  100.0 0.0 collective-permute-done
  100.0 0.0 copy-done.3
  100.1 2.1 %collective-permute-start.1 = (f32[64,1536]{1,0:T(8,128)S(1)}, f32[64,1536]{1,0:T(8,128)S(1)}, u32[]{:S(2)}, u32[]{:S(2)}) collective-permute-start(f32[64,1536]{1,0:T(8,128)S(1)} %add.12), channel_id=1, source_target_pairs={{0,2},{1,3},{2,4},{3,5},{4,6},{5,7},{6,0},{7,1},{8,10},{9,11},{10,... | collective-permute-start | bytes 1179656 | tf_op jit(solution)/shard_map/ppermute | solution.py:617
  102.1 2.7 %collective-permute-done.4 = f32[64,1536]{1,0:T(8,128)S(1)} collective-permute-done((f32[64,1536]{1,0:T(8,128)}, f32[64,1536]{1,0:T(8,128)S(1)}, u32[]{:S(2)}, u32[]{:S(2)}) %collective-permute-start.4) | collective-permute-done | bytes 393248 | tf_op jit(solution)/shard_map/ppermute | solution.py:581
  104.8 0.0 copy-done.2
  104.8 1.6 %collective-permute-start.5 = (f32[64,1536]{1,0:T(8,128)S(1)}, f32[64,1536]{1,0:T(8,128)S(1)}, u32[]{:S(2)}, u32[]{:S(2)}) collective-permute-start(f32[64,1536]{1,0:T(8,128)S(1)} %add.14), channel_id=1, source_target_pairs={{0,6},{1,7},{2,0},{3,1},{4,2},{5,3},{6,4},{7,5},{8,14},{9,15},{10,... | collective-permute-start | bytes 1179656 | tf_op jit(solution)/shard_map/ppermute | solution.py:618
  106.4 0.0 copy-start
  106.4 0.0 copy-start.1
  106.4 9.0 %later_grads.1 = (bf16[5,1536,512]{2,1,0:T(8,128)(2,1)}, bf16[5,1536,512]{2,1,0:T(8,128)(2,1)}, bf16[5,512,1536]{2,1,0:T(8,128)(2,1)}) custom-call(bf16[5,448,1536]{2,1,0:T(8,128)(2,1)} %get-tuple-element.37.x_ref, bf16[5,448,1536]{2,1,0:T(8,128)(2,1)} %get-tuple-element.38.d_ref, ...), custom_call_target="tpu_custom_call", output_to_operand_aliasing={{0}: (5, {}), {1}: (6, {}), {2}: (7, {})} | custom-call | flops 4227858432 | bytes 17694720 | tf_op jit(solution)/shard_map/later_grads/pallas_call | solution.py:619
  115.4 0.0 collective-permute-done.2
  115.4 0.0 collective-permute-done.3
  115.4 0.0 collective-permute-done.1
  115.4 0.6 collective-permute-done.5
  116.0 0.0 copy-done
  116.0 0.9 fusion.1
  116.9 0.0 copy-done.1
  116.9 0.7 copy.19
  (2 shorter events, 0.1 us)
Async XLA Ops:
  78.6 21.4 %collective-permute-start = (f32[64,1536]{1,0:T(8,128)}, f32[64,1536]{1,0:T(8,128)S(1)}, u32[]{:S(2)}, u32[]{:S(2)}) collective-permute-start(f32[64,1536]{1,0:T(8,128)} %get-tuple-element.32), channel_id=1, source_target_pairs={{0,2},{1,3},{2,4},{3,5},{4,6},{5,7},{6,0},{7,1},{8,10},{9,11},{10,... | collective-permute-start | bytes 1179656 | tf_op jit(solution)/shard_map/ppermute | solution.py:580
  82.6 32.8 %collective-permute-start.2 = (f32[64,1536]{1,0:T(8,128)}, f32[64,1536]{1,0:T(8,128)S(1)}, u32[]{:S(2)}, u32[]{:S(2)}) collective-permute-start(f32[64,1536]{1,0:T(8,128)} %get-tuple-element.33), channel_id=1, source_target_pairs={{0,2},{1,3},{2,4},{3,5},{4,6},{5,7},{6,0},{7,1},{8,10},{9,11},{10,... | collective-permute-start | bytes 1179656 | tf_op jit(solution)/shard_map/ppermute | solution.py:582
  84.4 31.0 %collective-permute-start.3 = (f32[64,1536]{1,0:T(8,128)}, f32[64,1536]{1,0:T(8,128)S(1)}, u32[]{:S(2)}, u32[]{:S(2)}) collective-permute-start(f32[64,1536]{1,0:T(8,128)} %get-tuple-element.34), channel_id=1, source_target_pairs={{0,6},{1,7},{2,0},{3,1},{4,2},{5,3},{6,4},{7,5},{8,14},{9,15},{10,... | collective-permute-start | bytes 1179656 | tf_op jit(solution)/shard_map/ppermute | solution.py:583
  85.8 19.0 %collective-permute-start.4 = (f32[64,1536]{1,0:T(8,128)}, f32[64,1536]{1,0:T(8,128)S(1)}, u32[]{:S(2)}, u32[]{:S(2)}) collective-permute-start(f32[64,1536]{1,0:T(8,128)} %get-tuple-element.36), channel_id=1, source_target_pairs={{0,6},{1,7},{2,0},{3,1},{4,2},{5,3},{6,4},{7,5},{8,14},{9,15},{10,... | collective-permute-start | bytes 1179656 | tf_op jit(solution)/shard_map/ppermute | solution.py:581
  85.8 14.2 %copy-start.3 = (f32[64,1536]{1,0:T(8,128)S(1)}, f32[64,1536]{1,0:T(8,128)}, u32[]{:S(2)}) copy-start(f32[64,1536]{1,0:T(8,128)} %get-tuple-element.31) | copy-start | bytes 1179652
  85.8 19.0 %copy-start.2 = (f32[64,1536]{1,0:T(8,128)S(1)}, f32[64,1536]{1,0:T(8,128)}, u32[]{:S(2)}) copy-start(f32[64,1536]{1,0:T(8,128)} %get-tuple-element.35) | copy-start | bytes 1179652
  100.1 15.3 %collective-permute-start.1 = (f32[64,1536]{1,0:T(8,128)S(1)}, f32[64,1536]{1,0:T(8,128)S(1)}, u32[]{:S(2)}, u32[]{:S(2)}) collective-permute-start(f32[64,1536]{1,0:T(8,128)S(1)} %add.12), channel_id=1, source_target_pairs={{0,2},{1,3},{2,4},{3,5},{4,6},{5,7},{6,0},{7,1},{8,10},{9,11},{10,... | collective-permute-start | bytes 1179656 | tf_op jit(solution)/shard_map/ppermute | solution.py:617
  104.8 11.2 %collective-permute-start.5 = (f32[64,1536]{1,0:T(8,128)S(1)}, f32[64,1536]{1,0:T(8,128)S(1)}, u32[]{:S(2)}, u32[]{:S(2)}) collective-permute-start(f32[64,1536]{1,0:T(8,128)S(1)} %add.14), channel_id=1, source_target_pairs={{0,6},{1,7},{2,0},{3,1},{4,2},{5,3},{6,4},{7,5},{8,14},{9,15},{10,... | collective-permute-start | bytes 1179656 | tf_op jit(solution)/shard_map/ppermute | solution.py:618
  106.4 9.6 %copy-start = (f32[128,1536]{1,0:T(8,128)S(1)}, f32[128,1536]{1,0:T(8,128)}, u32[]{:S(2)}) copy-start(f32[128,1536]{1,0:T(8,128)} %get-tuple-element.30) | copy-start | bytes 2359300
  106.4 10.5 %copy-start.1 = (bf16[128,1536]{1,0:T(8,128)(2,1)S(1)}, bf16[128,1536]{1,0:T(8,128)(2,1)}, u32[]{:S(2)}) copy-start(bf16[128,1536]{1,0:T(8,128)(2,1)} %get-tuple-element.58) | copy-start | bytes 1179652

commit v4 on v3

--- a/solution.py
+++ b/solution.py
@@ -25,7 +25,7 @@
 
 
 def layer_kernel(cfg, x_hbm, dy_hbm, ids_ref, gates_ref, w1_hbm, w3_hbm, w2_hbm,
-                 y_hbm, soa_hbm, sob_hbm, sra_hbm, srb_hbm, sla_hbm, slb_hbm, sc_hbm, xr_hbm, dr_hbm, ur_hbm, da_hbm, db_hbm, xh_hbm, dh_hbm, uh_hbm, dah_hbm, dbh_hbm,
+                 y_hbm, go_r, go_l, sr_hbm, sl_hbm, sc_hbm, xr_hbm, dr_hbm, ur_hbm, da_hbm, db_hbm, xh_hbm, dh_hbm, uh_hbm, dah_hbm, dbh_hbm,
                  x_all, dy_all, ids_all, gates_all, rt, gt, mc, ypart, dxpart, cbuf, yra, yrb, yfl, yfr,
                  erows, hrows, urow, uhot, darow, dbrow, act1, act2, orow, pbuf, w1, w3, w2, outb,
                  m_send, m_recv, ag_send, ag_recv, rs_send, rs_recv, w_sem, st_sem, hst_sem, io_sem, so_sem, free_sem):
@@ -155,25 +155,19 @@
     def forward(m, src, dst, s, aoff):
         for j in range(hid // 256):
             cs = slice(j * 256, (j + 1) * 256)
-            act1[pl.ds(aoff, m), cs] = dot_nn(src[...], w1[s, :, cs])
-            act2[pl.ds(aoff, m), cs] = dot_nn(src[...], w3[s, :, cs])
-
-        @pl.loop(0, m // 16)
-        def _(r):
-            o = pl.multiple_of(aoff + r * 16, 16)
-            a = act1[pl.ds(o, 16), :]
-            b = act2[pl.ds(o, 16), :]
+            a = dot_nn(src[...], w1[s, :, cs])
+            b = dot_nn(src[...], w3[s, :, cs])
             sg = jax.nn.sigmoid(a)
             ga = a * sg
-            act1[pl.ds(o, 16), :] = b * (sg * (1.0 + a * (1.0 - sg)))
-            act2[pl.ds(o, 16), :] = ga
-            dst[pl.ds(pl.multiple_of(r * 16, 16), 16), :] = (ga * b).astype(BF16)
+            act1[pl.ds(aoff, m), cs] = b * (sg * (1.0 + a * (1.0 - sg)))
+            act2[pl.ds(aoff, m), cs] = ga
+            dst[:, cs] = (ga * b).astype(BF16)
 
         for j in range(width // 256):
             cs = slice(j * 256, (j + 1) * 256)
             orow[0:m, cs] = dot_nn(dst[...], w2[s, :, cs]).astype(BF16)
 
-    def backward(m, src, s, aoff):
+    def backward(m, src, s, aoff, ooff):
         for j in range(hid // 256):
             cs = slice(j * 256, (j + 1) * 256)
             du = dot_nt(src[...], w2[s, cs, :])
@@ -181,22 +175,55 @@
             dbrow[s, 0:m, cs] = (du * act2[pl.ds(aoff, m), cs]).astype(BF16)
         for j in range(width // 256):
             cs = slice(j * 256, (j + 1) * 256)
-            orow[0:m, cs] = (dot_nt(darow[s, 0:m, :], w1[s, cs, :]) + dot_nt(dbrow[s, 0:m, :], w3[s, cs, :])).astype(BF16)
+            orow[pl.ds(ooff, m), cs] = (dot_nt(darow[s, 0:m, :], w1[s, cs, :]) + dot_nt(dbrow[s, 0:m, :], w3[s, cs, :])).astype(BF16)
 
     def act_off(e):
         return pl.multiple_of(jnp.where(e == 0, 0, hot_rows + (e - 1) * n_rows), 64)
 
     def add_out(q, e, first):
-        ypart[q] += column(q, e + 8) * dot_nn(put_rows(q, e), orow[first:first + cp, :])
+        gate = column(q, e + 8)
+        put = put_rows(q, e)
+        for j in range(width // 256):
+            cs = slice(j * 256, (j + 1) * 256)
+            ypart[q, :, cs] += gate * dot_nn(put, orow[first:first + cp, cs])
+
+    def add_dx_one(q, p, e):
+        put = put_rows(q, e)
+        for j in range(width // 256):
+            cs = slice(j * 256, (j + 1) * 256)
+            dxpart[q, :, cs] += dot_nn(put, orow[p * cp:(p + 1) * cp, cs])
+
+    def add_dx_two(q, p, e):
+        now, before = column(q, e), column(q, e - 1)
+        now = jnp.where(now >= 0.0, now + float(cp), -1.0)
+        lane = lax.broadcasted_iota(jnp.int32, (two, 2 * cp), 1).astype(F32)
+        put = jnp.where(jnp.logical_or(before == lane, now == lane), 1.0, 0.0).astype(BF16)
+        for j in range(width // 256):
+            cs = slice(j * 256, (j + 1) * 256)
+            both = jnp.concatenate([orow[2 * two + p * cp:2 * two + (p + 1) * cp, cs], orow[p * cp:(p + 1) * cp, cs]], axis=0)
+            dxpart[q, :, cs] += dot_nn(put, both)
+
+    def lane_of(q, r, n, lane):
+        m = mc[q, pl.ds(r, n), :]
+        return jnp.sum(jnp.where(lax.broadcasted_iota(jnp.int32, (n, 128), 1) == lane, m, 0.0), axis=1, keepdims=True)
 
     def hot_forward(p, q, s):
-        on = column(q, 0) >= 0.0
-        hrows[0:two, :] = jnp.where(on, x_all[q].astype(F32), 0.0).astype(BF16)
+        @pl.loop(0, two // 32)
+        def _(r):
+            o = pl.multiple_of(r * 32, 32)
+            on = lane_of(q, o, 32, 0) >= 0.0
+            hrows[pl.ds(o, 32), :] = jnp.where(on, x_all[q, pl.ds(o, 32), :].astype(F32), 0.0).astype(BF16)
+
         xs = pltpu.make_async_copy(hrows.at[0:two], xh_hbm.at[pl.ds(p * two, two)], hst_sem.at[0])
         xs.start()
         o = pl.multiple_of(p * two, 64)
         forward(two, hrows.at[0:two], uhot.at[pl.ds(o, two)], s, o)
-        ypart[q] += column(q, 8) * orow[0:two, :].astype(F32)
+
+        @pl.loop(0, two // 32)
+        def _(r):
+            i = pl.multiple_of(r * 32, 32)
+            ypart[q, pl.ds(i, 32), :] += lane_of(q, i, 32, 8) * orow[pl.ds(i, 32), :].astype(F32)
+
         xs.wait()
 
     def turn(i):
@@ -285,13 +312,21 @@
         hot = jnp.logical_and(is_owner, e == 0)
         turn(e + n_loc)
 
-        @pl.when(e == 2)
+        @pl.when(e == 1)
         def _():
             ag(dy_all, 1, 0).wait_recv()
             ag(dy_all, 1, 5).start()
             ag(dy_all, 1, 2).wait_recv()
             ag(dy_all, 1, 6).start()
 
+        @pl.when(e == 3)
+        def _():
+            ag(dy_all, 1, 4).wait_recv()
+            ag(dy_all, 1, 1).wait_recv()
+            ag(dy_all, 1, 7).start()
+            ag(dy_all, 1, 3).wait_recv()
+            ag(dy_all, 1, 8).start()
+
         @pl.when(jnp.logical_not(hot))
         def _():
             forward(n_rows - cp, erows.at[e, cp:n_rows], urow.at[e, cp:n_rows], s, pl.multiple_of(act_off(e) + cp, 16))
@@ -311,6 +346,13 @@
             def _(p):
                 q = jnp.where(p == 1, c_l, jnp.where(p == 2, c_r, c_o))
                 hot_forward(p, q, s)
+
+    @pl.loop(0, n_loc)
+    def _(e):
+        @pl.when(jnp.logical_not(jnp.logical_and(is_owner, e == 0)))
+        def _():
+            for cpy in st_fwd(e):
+                cpy.wait()
 
     for j, q in enumerate((c_o, c_r, c_l)):
         rs(0, j).wait_recv()
@@ -318,34 +360,22 @@
         if j == 0:
             rs(0, 4).start()
             rs(0, 5).start()
+            ag(dy_all, 1, 5).wait_recv()
+            ag(dy_all, 1, 9).start()
+            ag(dy_all, 1, 6).wait_recv()
+            ag(dy_all, 1, 10).start()
         else:
             rs(0, 5 + j).start()
     pl.semaphore_signal(free_sem, inc=1, device_id={"ep": partner}, device_id_type=MESH)
-
-    ag(dy_all, 1, 4).wait_recv()
-    ag(dy_all, 1, 1).wait_recv()
-    ag(dy_all, 1, 7).start()
-    ag(dy_all, 1, 3).wait_recv()
-    ag(dy_all, 1, 8).start()
-    ag(dy_all, 1, 5).wait_recv()
-    ag(dy_all, 1, 9).start()
-    ag(dy_all, 1, 6).wait_recv()
-    ag(dy_all, 1, 10).start()
-    for i in (7, 8, 9, 10):
-        ag(dy_all, 1, i).wait_recv()
-
-    @pl.loop(0, n_loc)
-    def _(e):
-        @pl.when(jnp.logical_not(jnp.logical_and(is_owner, e == 0)))
-        def _():
-            for cpy in st_fwd(e):
-                cpy.wait()
 
     @pl.when(is_owner)
     def _():
         us = pltpu.make_async_copy(uhot, uh_hbm, hst_sem.at[0])
         us.start()
         us.wait()
+
+    for i in (7, 8, 9, 10):
+        ag(dy_all, 1, i).wait_recv()
 
     @pl.loop(0, chips)
     def _(p):
@@ -383,15 +413,31 @@
         for cpy in w_copies(e + 2 * n_loc):
             cpy.wait()
 
-        @pl.when(e == last)
+        @pl.when(e == last - 1)
         def _():
             rs_relay_y()
 
         @pl.when(jnp.logical_not(hot))
         def _():
-            backward(n_rows, erows.at[e], s, act_off(e))
-            for p in range(chips):
-                dxpart[near[p]] += dot_nn(put_rows(near[p], e), orow[p * cp:(p + 1) * cp, :])
+            backward(n_rows, erows.at[e], s, act_off(e), pl.multiple_of(s * 2 * two, 64))
+
+            @pl.when(e == 0)
+            def _():
+                for p in range(chips):
+                    add_dx_one(near[p], p, e)
+
+            @pl.when(e == last)
+            def _():
+                pl.semaphore_wait(free_sem, 1)
+
+            @pl.when(jnp.logical_and(e > 0, s == 0))
+            def _():
+                for j, p in enumerate((3, 2, 1, 0)):
+                    add_dx_two(near[p], p, e)
+
+                    @pl.when(e == last)
+                    def _():
+                        rs(1, j).start()
 
         @pl.when(hot)
         def _():
@@ -399,17 +445,26 @@
             def _(h):
                 pair = (jnp.where(h == 0, c, c_r), jnp.where(h == 0, c_l, c_o))
                 for i, q in enumerate(pair):
-                    hrows[i * two:(i + 1) * two, :] = (column(q, 8) * dy_all[q].astype(F32)).astype(BF16)
+                    @pl.loop(0, two // 32)
+                    def _(r):
+                        at = pl.multiple_of(r * 32, 32)
+                        got = dy_all[q, pl.ds(at, 32), :].astype(F32)
+                        hrows[pl.ds(pl.multiple_of(i * two + r * 32, 32), 32), :] = (lane_of(q, at, 32, 8) * got).astype(BF16)
+
                 o = pl.multiple_of(h * 2 * two, 64)
                 ds_ = pltpu.make_async_copy(hrows, dh_hbm.at[pl.ds(o, 2 * two)], hst_sem.at[0])
                 ds_.start()
-                backward(2 * two, hrows, s, o)
+                backward(2 * two, hrows, s, o, 0)
                 sa = pltpu.make_async_copy(darow.at[s], dah_hbm.at[pl.ds(o, 2 * two)], hst_sem.at[1])
                 sb = pltpu.make_async_copy(dbrow.at[s], dbh_hbm.at[pl.ds(o, 2 * two)], hst_sem.at[2])
                 sa.start()
                 sb.start()
                 for i, q in enumerate(pair):
-                    dxpart[q] += orow[i * two:(i + 1) * two, :].astype(F32)
+                    @pl.loop(0, two // 32)
+                    def _(r):
+                        at = pl.multiple_of(r * 32, 32)
+                        dxpart[q, pl.ds(at, 32), :] += orow[pl.ds(pl.multiple_of(i * two + r * 32, 32), 32), :].astype(F32)
+
                 ds_.wait()
                 sa.wait()
                 sb.wait()
@@ -438,15 +493,13 @@
 
     def chip_sums_out(j):
         q = (c_o, c_r, c_l, c)[j]
+        lo = dxpart.at[q, pl.ds(k * tok, half)]
+        hi = dxpart.at[q, pl.ds(k * tok + half, half)]
         if j == 3:
             return (pltpu.make_async_copy(dxpart.at[q, pl.ds(k * tok, tok)], sc_hbm, so_sem.at[6]),)
-        lo, hi = ((soa_hbm, sob_hbm), (sra_hbm, srb_hbm), (sla_hbm, slb_hbm))[j]
-        return (pltpu.make_async_copy(dxpart.at[q, pl.ds(k * tok, half)], lo, so_sem.at[2 * j]),
-                pltpu.make_async_copy(dxpart.at[q, pl.ds(k * tok + half, half)], hi, so_sem.at[2 * j + 1]))
-
-    pl.semaphore_wait(free_sem, 1)
-    for j in range(4):
-        rs(1, j).start()
+        to_lo, to_hi = ((go_r.at[0:half], go_l.at[0:half]), (sr_hbm, go_r.at[half:tok]), (go_l.at[half:tok], sl_hbm))[j]
+        return (pltpu.make_async_copy(lo, to_lo, so_sem.at[2 * j]), pltpu.make_async_copy(hi, to_hi, so_sem.at[2 * j + 1]))
+
     for j, q in enumerate((c_o, c_r, c_l, c)):
         rs(1, j).wait_recv()
         add_rows(dxpart, q, k * tok, cbuf.at[q], tok)
@@ -480,8 +533,9 @@
     g2[0] = dot_tn(u_ref[0], d_ref[0]).astype(BF16)
 
 
-def first_grads_kernel(owner, x_ref, d_ref, u_ref, da_ref, db_ref, xh, dh, uh, dah, dbh, g1, g3, g2, xb, dbuf, ub, dab, dbb, sem):
+def first_grads_kernel(owner, x_ref, d_ref, u_ref, da_ref, db_ref, xh, dh, uh, dah, dbh, y_ref, g1, g3, g2, y_out, xb, dbuf, ub, dab, dbb, sem):
     i = pl.program_id(0)
+    y_out[...] = y_ref[...]
     is_owner = lax.axis_index("ep") == owner
     hot = jnp.logical_and(is_owner, i == pl.num_programs(0) - 1)
 
@@ -541,13 +595,13 @@
             outs = pl.pallas_call(
                 functools.partial(layer_kernel, cfg),
                 out_shape=(
-                    sds((tok, width), BF16), *[sds((half, width), F32)] * 6, sds((tok, width), F32),
+                    sds((tok, width), BF16), *[sds((tok, width), F32)] * 2, *[sds((half, width), F32)] * 2, sds((tok, width), F32),
                     sds((n_loc, n_rows, width), BF16), sds((n_loc, n_rows, width), BF16),
                     sds((n_loc, n_rows, hid), BF16), sds((n_loc, n_rows, hid), BF16), sds((n_loc, n_rows, hid), BF16),
                     sds((hot_rows, width), BF16), sds((hot_rows, width), BF16),
                     sds((hot_rows, hid), BF16), sds((hot_rows, hid), BF16), sds((hot_rows, hid), BF16)),
                 in_specs=[any_spec, any_spec, vmem_spec, vmem_spec, any_spec, any_spec, any_spec],
-                out_specs=[any_spec] * 18,
+                out_specs=[any_spec] * 16,
                 scratch_shapes=[
                     pltpu.VMEM((chips, 2 * tok, width), BF16), pltpu.VMEM((chips, 2 * tok, width), BF16),
                     pltpu.VMEM((group, top_k, tok), jnp.int32), pltpu.VMEM((group, top_k, tok), F32),
@@ -561,7 +615,7 @@
                     pltpu.VMEM((n_loc, n_rows, hid), BF16), pltpu.VMEM((hot_rows, hid), BF16),
                     pltpu.VMEM((2, hb, hid), BF16), pltpu.VMEM((2, hb, hid), BF16),
                     pltpu.VMEM((act_rows, hid), F32), pltpu.VMEM((act_rows, hid), F32),
-                    pltpu.VMEM((hb, width), BF16), pltpu.VMEM((n_loc * 2 * cap, 2 * tok), BF16),
+                    pltpu.VMEM((hb + n_rows, width), BF16), pltpu.VMEM((n_loc * 2 * cap, 2 * tok), BF16),
                     pltpu.VMEM((2, width, hid), BF16), pltpu.VMEM((2, width, hid), BF16), pltpu.VMEM((2, hid, width), BF16),
                     pltpu.VMEM((tok, width), BF16),
                     pltpu.SemaphoreType.DMA((2, group)), pltpu.SemaphoreType.DMA((2, group)),
@@ -573,14 +627,12 @@
                 compiler_params=pltpu.CompilerParams(collective_id=0, has_side_effects=True, vmem_limit_bytes=67043328),
                 name="moe_layer",
             )(x, dy, ids.T, gates.T, w1, w3, w2)
-            y, soa, sob, sra, srb, sla, slb, sc, xr, dr, ur, dar, dbr, xh, dh, uh, dah, dbh = outs
+            y, go_r, go_l, sr, sl, sc, xr, dr, ur, dar, dbr, xh, dh, uh, dah, dbh = outs
 
             to_right = [(i, (i + 2) % group) for i in range(group)]
             to_left = [(i, (i + group - 2) % group) for i in range(group)]
-            ra = lax.ppermute(soa, "ep", to_right)
-            rb = lax.ppermute(sob, "ep", to_left)
-            fl_hi = lax.ppermute(srb, "ep", to_right)
-            fr_lo = lax.ppermute(sla, "ep", to_left)
+            from_l = lax.ppermute(go_r, "ep", to_right)
+            from_r = lax.ppermute(go_l, "ep", to_left)
 
             n_first = (n_loc + 1) // 2
             g_shapes = (sds((n_loc, width, hid), BF16), sds((n_loc, width, hid), BF16), sds((n_loc, hid, width), BF16))
@@ -604,18 +656,19 @@
             def later_at(i):
                 return i + n_first
 
-            grads = pl.pallas_call(
+            y_spec = pl.BlockSpec((tok, width), lambda i: (0, 0))
+            *grads, y = pl.pallas_call(
                 functools.partial(first_grads_kernel, owner),
-                grid=(n_first,), out_shape=g_shapes,
-                in_specs=row_specs(first_at) + [any_spec] * 5, out_specs=out_blks(first_at),
+                grid=(n_first,), out_shape=g_shapes + (sds((tok, width), BF16),),
+                in_specs=row_specs(first_at) + [any_spec] * 5 + [y_spec], out_specs=out_blks(first_at) + [y_spec],
                 scratch_shapes=[pltpu.VMEM((hot_rows, width), BF16), pltpu.VMEM((hot_rows, width), BF16), pltpu.VMEM((hot_rows, hid), BF16),
                                 pltpu.VMEM((hot_rows, hid), BF16), pltpu.VMEM((hot_rows, hid), BF16), pltpu.SemaphoreType.DMA((5,))],
                 compiler_params=pltpu.CompilerParams(vmem_limit_bytes=60 << 20),
                 cost_estimate=cost(n_first), name="first_grads",
-            )(xr, dr, ur, dar, dbr, xh, dh, uh, dah, dbh)
-
-            fl_lo = lax.ppermute(sra + ra, "ep", to_right)
-            fr_hi = lax.ppermute(slb + rb, "ep", to_left)
+            )(xr, dr, ur, dar, dbr, xh, dh, uh, dah, dbh, y)
+
+            fl_lo = lax.ppermute(sr + from_l[:half], "ep", to_right)
+            fr_hi = lax.ppermute(sl + from_r[:half], "ep", to_left)
             g1, g3, g2 = pl.pallas_call(
                 later_grads_kernel,
                 grid=(n_loc - n_first,), out_shape=g_shapes,
@@ -624,8 +677,8 @@
                 compiler_params=pltpu.CompilerParams(vmem_limit_bytes=60 << 20),
                 cost_estimate=cost(n_loc - n_first), name="later_grads",
             )(xr, dr, ur, dar, dbr, *grads)
-            fl = jnp.concatenate([fl_lo, fl_hi], axis=0)
-            fr = jnp.concatenate([fr_lo, fr_hi], axis=0)
+            fl = jnp.concatenate([fl_lo, from_l[half:]], axis=0)
+            fr = jnp.concatenate([from_r[half:], fr_hi], axis=0)
             dx = (sc + fl + fr).astype(BF16)
             return y, dx, g1, g3, g2
 

time: 118 us -> 111 us (0.941)
  Pallas kernels: 101 us -> 95.2 us
    pallas_call x1, Pallas kernels: 78 us -> 71.2 us  [device_fn(): pl.pallas_call(functools.partial(layer_kernel, cfg), out_shape=(sds((tok,...]
    ppermute x6 -> x4, waiting for transfers between devices: 3.27 us -> 2.56 us  [the longest x1 1.44 us: device_fn(): fr_hi = lax.ppermute(sl + from_r[:half], 'ep', to_left)]
    ppermute x6 -> x4, starting transfers between devices: 10.8 us -> 11.4 us  [the longest x1 5.3 us: device_fn(): from_l = lax.ppermute(go_r, 'ep', to_right)]
  transfers between devices with their start and end apart: 6 -> 4, of which waited for: 2 -> 3; matrix products, arithmetic and copies ran while one was open for 0% -> 0% of each run, Pallas kernels for 20% -> 22%
where the time goes in v4:
time: 111 us
  Pallas kernels  95.2 us (86%)
  starting transfers between devices  11.4 us (10%)
  waiting for transfers between devices  2.56 us (2%)
    pallas_call x1, Pallas kernels, device_fn(): pl.pallas_call(functools.partial(layer_kernel, cfg), out_shape=(sds((tok,...  71.2 us
    pallas_call x1, Pallas kernels, device_fn(): pl.pallas_call(functools.partial(first_grads_kernel, owner), grid=(n_firs...  15.1 us
    pallas_call x1, Pallas kernels, device_fn(): pl.pallas_call(later_grads_kernel, grid=(n_loc - n_first,), out_shape=g_s...  8.93 us
    ppermute x1, starting transfers between devices, device_fn(): from_l = lax.ppermute(go_r, 'ep', to_right)  5.3 us
    ppermute x1, starting transfers between devices, device_fn(): fl_lo = lax.ppermute(sr + from_l[:half], 'ep', to_right)  4.8 us
  transfers between devices with their start and end apart: 4, of which 3 were waited for; matrix products, arithmetic and copies ran while one was open for 0% of the time, Pallas kernels for 22%

profile of v4, /device:TPU:112, one launch (start us, length us, event | category | flops | bytes accessed | tf_op | source)
XLA Modules:
  0.0 110.9 jit_solution(12011417700619174944)
XLA Ops:
  0.6 71.2 %moe_layer.1 = (bf16[128,1536]{1,0:T(8,128)(2,1)}, f32[128,1536]{1,0:T(8,128)}, f32[128,1536]{1,0:T(8,128)}, f32[64,1536]{1,0:T(8,128)}, f32[64,1536]{1,0:T(8,12...) custom-call(bf16[128,1536]{1,0:T(8,128)(2,1)} %x_hbm.1, ...), custom_call_target="tpu_custom_call" | custom-call | tf_op jit(solution)/shard_map/moe_layer/pallas_call | solution.py:595
  71.8 5.3 %collective-permute-start = (f32[128,1536]{1,0:T(8,128)}, f32[128,1536]{1,0:T(8,128)S(1)}, u32[]{:S(2)}, u32[]{:S(2)}) collective-permute-start(f32[128,1536]{1,0:T(8,128)} %get-tuple-element.42), channel_id=1, source_target_pairs={{0,2},{1,3},{2,4},{3,5},{4,6},{5,7},{6,0},{7,1},{8,10},{9,11},{10,... | collective-permute-start | bytes 2359304 | tf_op jit(solution)/shard_map/ppermute | solution.py:634
  77.1 0.6 collective-permute-start.2
  77.8 0.0 copy-start.2
  77.8 0.0 copy-start.1
  77.8 15.1 %first_grads.1 = (bf16[5,1536,512]{2,1,0:T(8,128)(2,1)}, bf16[5,1536,512]{2,1,0:T(8,128)(2,1)}, bf16[5,512,1536]{2,1,0:T(8,128)(2,1)}, bf16[128,1536]{1,0:T(8,128)(2,1)}) custom-call(bf16[5,448,1536]{2,1,0:T(8,128)(2,1)} %get-tuple-element.28.x_ref, bf16[5,448,1536]{2,1,0:T(8,128)(2,1)} %get-tuple-element.29.d_ref, ...), custom_call_target="tpu_custom_call" | custom-call | flops 6341787648 | bytes 26542080 | tf_op jit(solution)/shard_map/first_grads/pallas_call | solution.py:660
  92.9 0.0 collective-permute-done
  92.9 0.0 copy-done.2
  92.9 0.1 slice_add_fusion.1
  93.0 4.8 %collective-permute-start.1 = (f32[64,1536]{1,0:T(8,128)S(1)}, f32[64,1536]{1,0:T(8,128)S(1)}, u32[]{:S(2)}, u32[]{:S(2)}) collective-permute-start(f32[64,1536]{1,0:T(8,128)S(1)} %get-tuple-element.53), channel_id=1, source_target_pairs={{0,2},{1,3},{2,4},{3,5},{4,6},{5,7},{6,0},{7,1},{8,10},{9,11},{10,... | collective-permute-start | bytes 1179656 | tf_op jit(solution)/shard_map/ppermute | solution.py:670
  97.8 0.3 collective-permute-done.2
  98.1 0.0 copy-done.1
  98.1 0.1 fusion.2
  98.2 0.6 collective-permute-start.3
  98.8 0.0 copy-start
  98.8 8.9 %later_grads.1 = (bf16[5,1536,512]{2,1,0:T(8,128)(2,1)}, bf16[5,1536,512]{2,1,0:T(8,128)(2,1)}, bf16[5,512,1536]{2,1,0:T(8,128)(2,1)}) custom-call(bf16[5,448,1536]{2,1,0:T(8,128)(2,1)} %get-tuple-element.28.x_ref, bf16[5,448,1536]{2,1,0:T(8,128)(2,1)} %get-tuple-element.29.d_ref, ...), custom_call_target="tpu_custom_call", output_to_operand_aliasing={{0}: (5, {}), {1}: (6, {}), {2}: (7, {})} | custom-call | flops 4227858432 | bytes 17694720 | tf_op jit(solution)/shard_map/later_grads/pallas_call | solution.py:672
  107.7 0.8 collective-permute-done.1
  108.5 1.4 %collective-permute-done.3 = f32[64,1536]{1,0:T(8,128)S(1)} collective-permute-done((f32[64,1536]{1,0:T(8,128)S(1)}, f32[64,1536]{1,0:T(8,128)S(1)}, u32[]{:S(2)}, u32[]{:S(2)}) %collective-permute-start.3) | collective-permute-done | bytes 393248 | tf_op jit(solution)/shard_map/ppermute | solution.py:671
  110.0 0.0 copy-done
  110.0 0.9 fusion.1
Async XLA Ops:
  71.8 21.1 %collective-permute-start = (f32[128,1536]{1,0:T(8,128)}, f32[128,1536]{1,0:T(8,128)S(1)}, u32[]{:S(2)}, u32[]{:S(2)}) collective-permute-start(f32[128,1536]{1,0:T(8,128)} %get-tuple-element.42), channel_id=1, source_target_pairs={{0,2},{1,3},{2,4},{3,5},{4,6},{5,7},{6,0},{7,1},{8,10},{9,11},{10,... | collective-permute-start | bytes 2359304 | tf_op jit(solution)/shard_map/ppermute | solution.py:634
  77.1 21.0 %collective-permute-start.2 = (f32[128,1536]{1,0:T(8,128)}, f32[128,1536]{1,0:T(8,128)S(1)}, u32[]{:S(2)}, u32[]{:S(2)}) collective-permute-start(f32[128,1536]{1,0:T(8,128)} %get-tuple-element.43), channel_id=1, source_target_pairs={{0,6},{1,7},{2,0},{3,1},{4,2},{5,3},{6,4},{7,5},{8,14},{9,15},{10,... | collective-permute-start | bytes 2359304 | tf_op jit(solution)/shard_map/ppermute | solution.py:635
  77.8 15.1 %copy-start.2 = (f32[64,1536]{1,0:T(8,128)S(1)}, f32[64,1536]{1,0:T(8,128)}, u32[]{:S(2)}) copy-start(f32[64,1536]{1,0:T(8,128)} %get-tuple-element.41) | copy-start | bytes 1179652
  77.8 20.4 %copy-start.1 = (f32[64,1536]{1,0:T(8,128)S(1)}, f32[64,1536]{1,0:T(8,128)}, u32[]{:S(2)}) copy-start(f32[64,1536]{1,0:T(8,128)} %get-tuple-element.44) | copy-start | bytes 1179652
  93.0 15.6 %collective-permute-start.1 = (f32[64,1536]{1,0:T(8,128)S(1)}, f32[64,1536]{1,0:T(8,128)S(1)}, u32[]{:S(2)}, u32[]{:S(2)}) collective-permute-start(f32[64,1536]{1,0:T(8,128)S(1)} %get-tuple-element.53), channel_id=1, source_target_pairs={{0,2},{1,3},{2,4},{3,5},{4,6},{5,7},{6,0},{7,1},{8,10},{9,11},{10,... | collective-permute-start | bytes 1179656 | tf_op jit(solution)/shard_map/ppermute | solution.py:670
  98.2 11.8 %collective-permute-start.3 = (f32[64,1536]{1,0:T(8,128)S(1)}, f32[64,1536]{1,0:T(8,128)S(1)}, u32[]{:S(2)}, u32[]{:S(2)}) collective-permute-start(f32[64,1536]{1,0:T(8,128)S(1)} %get-tuple-element.52), channel_id=1, source_target_pairs={{0,6},{1,7},{2,0},{3,1},{4,2},{5,3},{6,4},{7,5},{8,14},{9,15},{10,... | collective-permute-start | bytes 1179656 | tf_op jit(solution)/shard_map/ppermute | solution.py:671
  98.8 11.2 %copy-start = (f32[128,1536]{1,0:T(8,128)S(1)}, f32[128,1536]{1,0:T(8,128)}, u32[]{:S(2)}) copy-start(f32[128,1536]{1,0:T(8,128)} %get-tuple-element.40) | copy-start | bytes 2359300

commit v5 on v4

--- a/solution.py
+++ b/solution.py
@@ -54,15 +54,15 @@
     own_x.start()
     own_dy.start()
 
-    def w_copies(i):
-        e = lax.rem(i, n_loc)
-        s = lax.rem(i, 2)
+    def w_copies(e):
+        s = lax.rem(e, 2)
         return (pltpu.make_async_copy(w1_hbm.at[e], w1.at[s], w_sem.at[0, s]),
                 pltpu.make_async_copy(w3_hbm.at[e], w3.at[s], w_sem.at[1, s]),
                 pltpu.make_async_copy(w2_hbm.at[e], w2.at[s], w_sem.at[2, s]))
 
-    for cpy in w_copies(0):
-        cpy.start()
+    for e in (last, last - 1):
+        for cpy in w_copies(e):
+            cpy.start()
     ids_all[me] = ids_ref[...]
     gates_all[me] = gates_ref[...]
 
@@ -152,22 +152,26 @@
         hit = column(q, e) == lax.broadcasted_iota(jnp.int32, (two, cp), 1).astype(F32)
         return jnp.where(hit, 1.0, 0.0).astype(BF16)
 
-    def forward(m, src, dst, s, aoff):
+    def forward(m, src, dst, s, aoff, on, emit):
         for j in range(hid // 256):
             cs = slice(j * 256, (j + 1) * 256)
             a = dot_nn(src[...], w1[s, :, cs])
             b = dot_nn(src[...], w3[s, :, cs])
             sg = jax.nn.sigmoid(a)
             ga = a * sg
-            act1[pl.ds(aoff, m), cs] = b * (sg * (1.0 + a * (1.0 - sg)))
+            fa = b * (sg * (1.0 + a * (1.0 - sg)))
+            u = ga * b
+            if on is not None:
+                fa, ga, u = jnp.where(on, fa, 0.0), jnp.where(on, ga, 0.0), jnp.where(on, u, 0.0)
+            act1[pl.ds(aoff, m), cs] = fa
             act2[pl.ds(aoff, m), cs] = ga
-            dst[:, cs] = (ga * b).astype(BF16)
+            dst[:, cs] = u.astype(BF16)
 
         for j in range(width // 256):
             cs = slice(j * 256, (j + 1) * 256)
-            orow[0:m, cs] = dot_nn(dst[...], w2[s, :, cs]).astype(BF16)
-
-    def backward(m, src, s, aoff, ooff):
+            emit(cs, dot_nn(dst[...], w2[s, :, cs]).astype(BF16))
+
+    def backward(m, src, s, aoff, emit):
         for j in range(hid // 256):
             cs = slice(j * 256, (j + 1) * 256)
             du = dot_nt(src[...], w2[s, cs, :])
@@ -175,7 +179,7 @@
             dbrow[s, 0:m, cs] = (du * act2[pl.ds(aoff, m), cs]).astype(BF16)
         for j in range(width // 256):
             cs = slice(j * 256, (j + 1) * 256)
-            orow[pl.ds(ooff, m), cs] = (dot_nt(darow[s, 0:m, :], w1[s, cs, :]) + dot_nt(dbrow[s, 0:m, :], w3[s, cs, :])).astype(BF16)
+            emit(cs, (dot_nt(darow[s, 0:m, :], w1[s, cs, :]) + dot_nt(dbrow[s, 0:m, :], w3[s, cs, :])).astype(BF16))
 
     def act_off(e):
         return pl.multiple_of(jnp.where(e == 0, 0, hot_rows + (e - 1) * n_rows), 64)
@@ -208,56 +212,30 @@
         return jnp.sum(jnp.where(lax.broadcasted_iota(jnp.int32, (n, 128), 1) == lane, m, 0.0), axis=1, keepdims=True)
 
     def hot_forward(p, q, s):
-        @pl.loop(0, two // 32)
-        def _(r):
-            o = pl.multiple_of(r * 32, 32)
-            on = lane_of(q, o, 32, 0) >= 0.0
-            hrows[pl.ds(o, 32), :] = jnp.where(on, x_all[q, pl.ds(o, 32), :].astype(F32), 0.0).astype(BF16)
-
-        xs = pltpu.make_async_copy(hrows.at[0:two], xh_hbm.at[pl.ds(p * two, two)], hst_sem.at[0])
-        xs.start()
         o = pl.multiple_of(p * two, 64)
-        forward(two, hrows.at[0:two], uhot.at[pl.ds(o, two)], s, o)
-
-        @pl.loop(0, two // 32)
-        def _(r):
-            i = pl.multiple_of(r * 32, 32)
-            ypart[q, pl.ds(i, 32), :] += lane_of(q, i, 32, 8) * orow[pl.ds(i, 32), :].astype(F32)
-
-        xs.wait()
-
-    def turn(i):
-        for cpy in w_copies(i + 1):
-            cpy.start()
-        for cpy in w_copies(i):
-            cpy.wait()
-
-    ag(x_all, 0, 4).wait_recv()
-    pick(0, c, x_all, False)
-
-    @pl.loop(0, n_loc)
-    def _(e):
-        s = lax.rem(e, 2)
-        hot = jnp.logical_and(is_owner, e == 0)
-        turn(e)
-
-        @pl.when(e == 3)
-        def _():
-            ag(x_all, 0, 0).wait_recv()
-            ag(x_all, 0, 5).start()
-            ag(x_all, 0, 2).wait_recv()
-            ag(x_all, 0, 6).start()
-            for i in (4, 0, 2, 1, 3):
-                ag(dy_all, 1, i).start()
-
-        @pl.when(jnp.logical_not(hot))
-        def _():
-            forward(cp, erows.at[e, 0:cp], urow.at[e, 0:cp], s, act_off(e))
-            add_out(c, e, 0)
-
-        @pl.when(hot)
-        def _():
-            hot_forward(0, c, s)
+        gate = column(q, 8)
+
+        def emit(cs, out):
+            ypart[q, :, cs] += gate * out.astype(F32)
+
+        forward(two, x_all.at[q], uhot.at[pl.ds(o, two)], s, o, column(q, 0) >= 0.0, emit)
+
+    def cold_forward(e, s, r0, r1):
+        def emit(cs, out):
+            orow[0:r1 - r0, cs] = out
+
+        forward(r1 - r0, erows.at[e, r0:r1], urow.at[e, r0:r1], s, pl.multiple_of(act_off(e) + r0, 16), None, emit)
+
+    def turn(i, e, step, first):
+        @pl.when(jnp.logical_and(i >= 1, i < last))
+        def _():
+            for cpy in w_copies(e + step):
+                cpy.start()
+
+        @pl.when(i >= (0 if first else 2))
+        def _():
+            for cpy in w_copies(e):
+                cpy.wait()
 
     def rs(t, j):
         part = (ypart, dxpart)[t]
@@ -283,6 +261,34 @@
             o = pl.multiple_of(r * 32, 32)
             part[q, pl.ds(pl.multiple_of(off + r * 32, 32), 32)] += src[pl.ds(o, 32)]
 
+    ag(x_all, 0, 4).wait_recv()
+    pick(0, c, x_all, False)
+
+    @pl.loop(0, n_loc)
+    def _(i):
+        e = last - i
+        s = lax.rem(e, 2)
+        hot = jnp.logical_and(is_owner, e == 0)
+        turn(i, e, -1, True)
+
+        @pl.when(i == 3)
+        def _():
+            ag(x_all, 0, 0).wait_recv()
+            ag(x_all, 0, 5).start()
+            ag(x_all, 0, 2).wait_recv()
+            ag(x_all, 0, 6).start()
+            for n in (4, 0, 2, 1, 3):
+                ag(dy_all, 1, n).start()
+
+        @pl.when(jnp.logical_not(hot))
+        def _():
+            cold_forward(e, s, 0, cp)
+            add_out(c, e, 0)
+
+        @pl.when(hot)
+        def _():
+            hot_forward(0, c, s)
+
     ag(x_all, 0, 1).wait_recv()
     ag(x_all, 0, 7).start()
     ag(x_all, 0, 3).wait_recv()
@@ -292,10 +298,43 @@
     pick(1, c_l, x_all, False)
     ag(x_all, 0, 8).wait_recv()
     pick(2, c_r, x_all, False)
-    ag(x_all, 0, 5).wait_recv()
-    ag(x_all, 0, 9).start()
-    ag(x_all, 0, 6).wait_recv()
-    ag(x_all, 0, 10).start()
+
+    @pl.loop(0, n_loc)
+    def _(e):
+        s = lax.rem(e, 2)
+        hot = jnp.logical_and(is_owner, e == 0)
+        turn(e, e, 1, False)
+
+        @pl.when(e == 2)
+        def _():
+            ag(x_all, 0, 5).wait_recv()
+            ag(x_all, 0, 9).start()
+            ag(x_all, 0, 6).wait_recv()
+            ag(x_all, 0, 10).start()
+
+        @pl.when(e == last)
+        def _():
+            ag(dy_all, 1, 0).wait_recv()
+            ag(dy_all, 1, 5).start()
+            ag(dy_all, 1, 2).wait_recv()
+            ag(dy_all, 1, 6).start()
+
+        @pl.when(jnp.logical_not(hot))
+        def _():
+            cold_forward(e, s, cp, 3 * cp)
+            for j, p in ((1, 2), (2, 1)):
+                add_out(near[p], e, (p - 1) * cp)
+
+                @pl.when(e == last)
+                def _():
+                    rs(0, j).start()
+
+        @pl.when(hot)
+        def _():
+            @pl.loop(1, 3)
+            def _(p):
+                hot_forward(p, jnp.where(p == 1, c_l, c_r), s)
+
     rs(0, 3).wait_recv()
     add_rows(ypart, c, k * tok, cbuf.at[c], tok)
     ag(x_all, 0, 9).wait_recv()
@@ -306,20 +345,25 @@
         return (pltpu.make_async_copy(erows.at[e], xr_hbm.at[e], st_sem.at[0, e]),
                 pltpu.make_async_copy(urow.at[e], ur_hbm.at[e], st_sem.at[1, e]))
 
+    def st_hot():
+        return [pltpu.make_async_copy(uhot, uh_hbm, hst_sem.at[0])] + [
+            pltpu.make_async_copy(x_all.at[q], xh_hbm.at[p * two:(p + 1) * two], hst_sem.at[1 + p]) for p, q in enumerate(near)]
+
     @pl.loop(0, n_loc)
-    def _(e):
-        s = lax.rem(e + n_loc, 2)
+    def _(i):
+        e = last - i
+        s = lax.rem(e, 2)
         hot = jnp.logical_and(is_owner, e == 0)
-        turn(e + n_loc)
-
-        @pl.when(e == 1)
-        def _():
-            ag(dy_all, 1, 0).wait_recv()
-            ag(dy_all, 1, 5).start()
-            ag(dy_all, 1, 2).wait_recv()
-            ag(dy_all, 1, 6).start()
-
-        @pl.when(e == 3)
+        turn(i, e, -1, False)
+
+        @pl.when(i == 1)
+        def _():
+            for j, q in ((1, c_r), (2, c_l)):
+                rs(0, j).wait_recv()
+                add_rows(ypart, q, k * tok, cbuf.at[q], tok)
+                rs(0, 5 + j).start()
+
+        @pl.when(i == 3)
         def _():
             ag(dy_all, 1, 4).wait_recv()
             ag(dy_all, 1, 1).wait_recv()
@@ -329,23 +373,18 @@
 
         @pl.when(jnp.logical_not(hot))
         def _():
-            forward(n_rows - cp, erows.at[e, cp:n_rows], urow.at[e, cp:n_rows], s, pl.multiple_of(act_off(e) + cp, 16))
-            for j, p in enumerate((3, 2, 1)):
-                add_out(near[p], e, (p - 1) * cp)
-
-                @pl.when(e == last)
-                def _():
-                    rs(0, j).start()
-
+            cold_forward(e, s, 3 * cp, n_rows)
+            add_out(c_o, e, 0)
             for cpy in st_fwd(e):
                 cpy.start()
 
         @pl.when(hot)
         def _():
-            @pl.loop(1, chips)
-            def _(p):
-                q = jnp.where(p == 1, c_l, jnp.where(p == 2, c_r, c_o))
-                hot_forward(p, q, s)
+            hot_forward(3, c_o, s)
+            for cpy in st_hot():
+                cpy.start()
+
+    rs(0, 0).start()
 
     @pl.loop(0, n_loc)
     def _(e):
@@ -354,33 +393,28 @@
             for cpy in st_fwd(e):
                 cpy.wait()
 
-    for j, q in enumerate((c_o, c_r, c_l)):
-        rs(0, j).wait_recv()
-        add_rows(ypart, q, k * tok, cbuf.at[q], tok)
-        if j == 0:
-            rs(0, 4).start()
-            rs(0, 5).start()
-            ag(dy_all, 1, 5).wait_recv()
-            ag(dy_all, 1, 9).start()
-            ag(dy_all, 1, 6).wait_recv()
-            ag(dy_all, 1, 10).start()
-        else:
-            rs(0, 5 + j).start()
+    pick(0, c, dy_all, True)
+    rs(0, 0).wait_recv()
+    add_rows(ypart, c_o, k * tok, cbuf.at[c_o], tok)
+    rs(0, 4).start()
+    rs(0, 5).start()
     pl.semaphore_signal(free_sem, inc=1, device_id={"ep": partner}, device_id_type=MESH)
+    ag(dy_all, 1, 7).wait_recv()
+    pick(1, c_l, dy_all, True)
+    ag(dy_all, 1, 5).wait_recv()
+    ag(dy_all, 1, 9).start()
+    ag(dy_all, 1, 6).wait_recv()
+    ag(dy_all, 1, 10).start()
+    ag(dy_all, 1, 8).wait_recv()
+    pick(2, c_r, dy_all, True)
+    ag(dy_all, 1, 9).wait_recv()
+    ag(dy_all, 1, 10).wait_recv()
+    pick(3, c_o, dy_all, True)
 
     @pl.when(is_owner)
     def _():
-        us = pltpu.make_async_copy(uhot, uh_hbm, hst_sem.at[0])
-        us.start()
-        us.wait()
-
-    for i in (7, 8, 9, 10):
-        ag(dy_all, 1, i).wait_recv()
-
-    @pl.loop(0, chips)
-    def _(p):
-        q = jnp.where(p == 0, c, jnp.where(p == 1, c_l, jnp.where(p == 2, c_r, c_o)))
-        pick(p, q, dy_all, True)
+        for cpy in st_hot():
+            cpy.wait()
 
     def st_d(e):
         return pltpu.make_async_copy(erows.at[e], dr_hbm.at[e], st_sem.at[0, e])
@@ -405,21 +439,20 @@
         s = lax.rem(e, 2)
         hot = jnp.logical_and(is_owner, e == 0)
 
-        @pl.when(e < last)
-        def _():
-            for cpy in w_copies(e + 2 * n_loc + 1):
-                cpy.start()
-
-        for cpy in w_copies(e + 2 * n_loc):
-            cpy.wait()
-
-        @pl.when(e == last - 1)
-        def _():
-            rs_relay_y()
+        turn(e, e, 1, False)
 
         @pl.when(jnp.logical_not(hot))
         def _():
-            backward(n_rows, erows.at[e], s, act_off(e), pl.multiple_of(s * 2 * two, 64))
+            ooff = pl.multiple_of(s * 2 * two, 64)
+
+            def emit(cs, out):
+                orow[pl.ds(ooff, n_rows), cs] = out
+
+            backward(n_rows, erows.at[e], s, act_off(e), emit)
+
+            @pl.when(e == last - 1)
+            def _():
+                rs_relay_y()
 
             @pl.when(e == 0)
             def _():
@@ -444,28 +477,27 @@
             @pl.loop(0, chips // 2)
             def _(h):
                 pair = (jnp.where(h == 0, c, c_r), jnp.where(h == 0, c_l, c_o))
-                for i, q in enumerate(pair):
-                    @pl.loop(0, two // 32)
+                for n, q in enumerate(pair):
+                    @pl.loop(0, two // 64)
                     def _(r):
-                        at = pl.multiple_of(r * 32, 32)
-                        got = dy_all[q, pl.ds(at, 32), :].astype(F32)
-                        hrows[pl.ds(pl.multiple_of(i * two + r * 32, 32), 32), :] = (lane_of(q, at, 32, 8) * got).astype(BF16)
+                        at = pl.multiple_of(r * 64, 64)
+                        got = dy_all[q, pl.ds(at, 64), :].astype(F32)
+                        hrows[pl.ds(pl.multiple_of(n * two + r * 64, 64), 64), :] = (lane_of(q, at, 64, 8) * got).astype(BF16)
 
                 o = pl.multiple_of(h * 2 * two, 64)
-                ds_ = pltpu.make_async_copy(hrows, dh_hbm.at[pl.ds(o, 2 * two)], hst_sem.at[0])
-                ds_.start()
-                backward(2 * two, hrows, s, o, 0)
+                sd = pltpu.make_async_copy(hrows, dh_hbm.at[pl.ds(o, 2 * two)], hst_sem.at[0])
+                sd.start()
+
+                def emit(cs, out):
+                    for n, q in enumerate(pair):
+                        dxpart[q, :, cs] += out[n * two:(n + 1) * two].astype(F32)
+
+                backward(2 * two, hrows, s, o, emit)
                 sa = pltpu.make_async_copy(darow.at[s], dah_hbm.at[pl.ds(o, 2 * two)], hst_sem.at[1])
                 sb = pltpu.make_async_copy(dbrow.at[s], dbh_hbm.at[pl.ds(o, 2 * two)], hst_sem.at[2])
                 sa.start()
                 sb.start()
-                for i, q in enumerate(pair):
-                    @pl.loop(0, two // 32)
-                    def _(r):
-                        at = pl.multiple_of(r * 32, 32)
-                        dxpart[q, pl.ds(at, 32), :] += orow[pl.ds(pl.multiple_of(i * two + r * 32, 32), 32), :].astype(F32)
-
-                ds_.wait()
+                sd.wait()
                 sa.wait()
                 sb.wait()
 
@@ -621,7 +653,7 @@
                     pltpu.SemaphoreType.DMA((2, group)), pltpu.SemaphoreType.DMA((2, group)),
                     pltpu.SemaphoreType.DMA((2, 11)), pltpu.SemaphoreType.DMA((2, 11)),
                     pltpu.SemaphoreType.DMA((2, 10)), pltpu.SemaphoreType.DMA((2, 10)),
-                    pltpu.SemaphoreType.DMA((3, 2)), pltpu.SemaphoreType.DMA((2, n_loc)), pltpu.SemaphoreType.DMA((3,)),
+                    pltpu.SemaphoreType.DMA((3, 2)), pltpu.SemaphoreType.DMA((2, n_loc)), pltpu.SemaphoreType.DMA((5,)),
                     pltpu.SemaphoreType.DMA((2,)), pltpu.SemaphoreType.DMA((7,)), pltpu.SemaphoreType.REGULAR,
                 ],
                 compiler_params=pltpu.CompilerParams(collective_id=0, has_side_effects=True, vmem_limit_bytes=67043328),

time: 111 us -> 109 us (0.982)
  starting transfers between devices: 11.4 us -> 8.77 us
    ppermute x1, starting transfers between devices: 4.8 us -> 3.19 us  [device_fn(): fl_lo = lax.ppermute(sr + from_l[:half], 'ep', to_right)]
  transfers between devices with their start and end apart: 4 -> 4, of which waited for: 3 -> 4; matrix products, arithmetic and copies ran while one was open for 0% -> 0% of each run, Pallas kernels for 22% -> 22%
where the time goes in v5:
time: 109 us
  Pallas kernels  95.8 us (88%)
  starting transfers between devices  8.77 us (8%)
  waiting for transfers between devices  2.99 us (3%)
    pallas_call x1, Pallas kernels, device_fn(): pl.pallas_call(functools.partial(layer_kernel, cfg), out_shape=(sds((tok,...  71.7 us
    pallas_call x1, Pallas kernels, device_fn(): pl.pallas_call(functools.partial(first_grads_kernel, owner), grid=(n_firs...  15.1 us
    pallas_call x1, Pallas kernels, device_fn(): pl.pallas_call(later_grads_kernel, grid=(n_loc - n_first,), out_shape=g_s...  8.93 us
    ppermute x1, starting transfers between devices, device_fn(): from_l = lax.ppermute(go_r, 'ep', to_right)  4.47 us
    ppermute x1, starting transfers between devices, device_fn(): fl_lo = lax.ppermute(sr + from_l[:half], 'ep', to_right)  3.19 us
  transfers between devices with their start and end apart: 4, of which 4 were waited for; matrix products, arithmetic and copies ran while one was open for 0% of the time, Pallas kernels for 22%

profile of v5, /device:TPU:112, one launch (start us, length us, event | category | flops | bytes accessed | tf_op | source)
XLA Modules:
  0.0 109.2 jit_solution(13268191328364166529)
XLA Ops:
  0.6 71.7 %moe_layer.1 = (bf16[128,1536]{1,0:T(8,128)(2,1)}, f32[128,1536]{1,0:T(8,128)}, f32[128,1536]{1,0:T(8,128)}, f32[64,1536]{1,0:T(8,128)}, f32[64,1536]{1,0:T(8,12...) custom-call(bf16[128,1536]{1,0:T(8,128)(2,1)} %x_hbm.1, ...), custom_call_target="tpu_custom_call" | custom-call | tf_op jit(solution)/shard_map/moe_layer/pallas_call | solution.py:627
  72.4 4.5 %collective-permute-start = (f32[128,1536]{1,0:T(8,128)}, f32[128,1536]{1,0:T(8,128)S(1)}, u32[]{:S(2)}, u32[]{:S(2)}) collective-permute-start(f32[128,1536]{1,0:T(8,128)} %get-tuple-element.42), channel_id=1, source_target_pairs={{0,2},{1,3},{2,4},{3,5},{4,6},{5,7},{6,0},{7,1},{8,10},{9,11},{10,... | collective-permute-start | bytes 2359304 | tf_op jit(solution)/shard_map/ppermute | solution.py:666
  76.9 0.6 collective-permute-start.2
  77.5 0.0 copy-start.2
  77.5 0.0 copy-start.1
  77.5 15.1 %first_grads.1 = (bf16[5,1536,512]{2,1,0:T(8,128)(2,1)}, bf16[5,1536,512]{2,1,0:T(8,128)(2,1)}, bf16[5,512,1536]{2,1,0:T(8,128)(2,1)}, bf16[128,1536]{1,0:T(8,128)(2,1)}) custom-call(bf16[5,448,1536]{2,1,0:T(8,128)(2,1)} %get-tuple-element.28.x_ref, bf16[5,448,1536]{2,1,0:T(8,128)(2,1)} %get-tuple-element.29.d_ref, ...), custom_call_target="tpu_custom_call" | custom-call | flops 6341787648 | bytes 26542080 | tf_op jit(solution)/shard_map/first_grads/pallas_call | solution.py:692
  92.6 0.2 collective-permute-done
  92.8 0.0 copy-done.2
  92.8 0.1 slice_add_fusion.1
  92.9 3.2 %collective-permute-start.1 = (f32[64,1536]{1,0:T(8,128)S(1)}, f32[64,1536]{1,0:T(8,128)S(1)}, u32[]{:S(2)}, u32[]{:S(2)}) collective-permute-start(f32[64,1536]{1,0:T(8,128)S(1)} %get-tuple-element.53), channel_id=1, source_target_pairs={{0,2},{1,3},{2,4},{3,5},{4,6},{5,7},{6,0},{7,1},{8,10},{9,11},{10,... | collective-permute-start | bytes 1179656 | tf_op jit(solution)/shard_map/ppermute | solution.py:702
  96.1 1.0 collective-permute-done.2
  97.1 0.0 copy-done.1
  97.1 0.1 fusion.2
  97.2 0.5 collective-permute-start.3
  97.6 0.0 copy-start
  97.6 8.9 %later_grads.1 = (bf16[5,1536,512]{2,1,0:T(8,128)(2,1)}, bf16[5,1536,512]{2,1,0:T(8,128)(2,1)}, bf16[5,512,1536]{2,1,0:T(8,128)(2,1)}) custom-call(bf16[5,448,1536]{2,1,0:T(8,128)(2,1)} %get-tuple-element.28.x_ref, bf16[5,448,1536]{2,1,0:T(8,128)(2,1)} %get-tuple-element.29.d_ref, ...), custom_call_target="tpu_custom_call", output_to_operand_aliasing={{0}: (5, {}), {1}: (6, {}), {2}: (7, {})} | custom-call | flops 4227858432 | bytes 17694720 | tf_op jit(solution)/shard_map/later_grads/pallas_call | solution.py:704
  106.6 0.5 collective-permute-done.1
  107.1 1.3 %collective-permute-done.3 = f32[64,1536]{1,0:T(8,128)S(1)} collective-permute-done((f32[64,1536]{1,0:T(8,128)S(1)}, f32[64,1536]{1,0:T(8,128)S(1)}, u32[]{:S(2)}, u32[]{:S(2)}) %collective-permute-start.3) | collective-permute-done | bytes 393248 | tf_op jit(solution)/shard_map/ppermute | solution.py:703
  108.4 0.0 copy-done
  108.4 0.9 fusion.1
Async XLA Ops:
  72.4 20.4 %collective-permute-start = (f32[128,1536]{1,0:T(8,128)}, f32[128,1536]{1,0:T(8,128)S(1)}, u32[]{:S(2)}, u32[]{:S(2)}) collective-permute-start(f32[128,1536]{1,0:T(8,128)} %get-tuple-element.42), channel_id=1, source_target_pairs={{0,2},{1,3},{2,4},{3,5},{4,6},{5,7},{6,0},{7,1},{8,10},{9,11},{10,... | collective-permute-start | bytes 2359304 | tf_op jit(solution)/shard_map/ppermute | solution.py:666
  76.9 20.2 %collective-permute-start.2 = (f32[128,1536]{1,0:T(8,128)}, f32[128,1536]{1,0:T(8,128)S(1)}, u32[]{:S(2)}, u32[]{:S(2)}) collective-permute-start(f32[128,1536]{1,0:T(8,128)} %get-tuple-element.43), channel_id=1, source_target_pairs={{0,6},{1,7},{2,0},{3,1},{4,2},{5,3},{6,4},{7,5},{8,14},{9,15},{10,... | collective-permute-start | bytes 2359304 | tf_op jit(solution)/shard_map/ppermute | solution.py:667
  77.5 15.3 %copy-start.2 = (f32[64,1536]{1,0:T(8,128)S(1)}, f32[64,1536]{1,0:T(8,128)}, u32[]{:S(2)}) copy-start(f32[64,1536]{1,0:T(8,128)} %get-tuple-element.41) | copy-start | bytes 1179652
  77.5 19.6 %copy-start.1 = (f32[64,1536]{1,0:T(8,128)S(1)}, f32[64,1536]{1,0:T(8,128)}, u32[]{:S(2)}) copy-start(f32[64,1536]{1,0:T(8,128)} %get-tuple-element.44) | copy-start | bytes 1179652
  92.9 14.2 %collective-permute-start.1 = (f32[64,1536]{1,0:T(8,128)S(1)}, f32[64,1536]{1,0:T(8,128)S(1)}, u32[]{:S(2)}, u32[]{:S(2)}) collective-permute-start(f32[64,1536]{1,0:T(8,128)S(1)} %get-tuple-element.53), channel_id=1, source_target_pairs={{0,2},{1,3},{2,4},{3,5},{4,6},{5,7},{6,0},{7,1},{8,10},{9,11},{10,... | collective-permute-start | bytes 1179656 | tf_op jit(solution)/shard_map/ppermute | solution.py:702
  97.2 11.2 %collective-permute-start.3 = (f32[64,1536]{1,0:T(8,128)S(1)}, f32[64,1536]{1,0:T(8,128)S(1)}, u32[]{:S(2)}, u32[]{:S(2)}) collective-permute-start(f32[64,1536]{1,0:T(8,128)S(1)} %get-tuple-element.52), channel_id=1, source_target_pairs={{0,6},{1,7},{2,0},{3,1},{4,2},{5,3},{6,4},{7,5},{8,14},{9,15},{10,... | collective-permute-start | bytes 1179656 | tf_op jit(solution)/shard_map/ppermute | solution.py:703
  97.6 10.8 %copy-start = (f32[128,1536]{1,0:T(8,128)S(1)}, f32[128,1536]{1,0:T(8,128)}, u32[]{:S(2)}) copy-start(f32[128,1536]{1,0:T(8,128)} %get-tuple-element.40) | copy-start | bytes 2359300

commit v6 on v5

--- a/solution.py
+++ b/solution.py
@@ -97,13 +97,6 @@
         ag(x_all, 0, i).start()
     own_dy.wait()
 
-    @pl.loop(0, chips * two // 64)
-    def _(r):
-        q = r // (two // 64)
-        o = pl.multiple_of(lax.rem(r, two // 64) * 64, 64)
-        ypart[q, pl.ds(o, 64)] = jnp.zeros((64, width), F32)
-        dxpart[q, pl.ds(o, 64)] = jnp.zeros((64, width), F32)
-
     for d in range(1, group):
         for cpy in meta_copies(d):
             cpy.wait_recv()
@@ -152,7 +145,7 @@
         hit = column(q, e) == lax.broadcasted_iota(jnp.int32, (two, cp), 1).astype(F32)
         return jnp.where(hit, 1.0, 0.0).astype(BF16)
 
-    def forward(m, src, dst, s, aoff, on, emit):
+    def forward(m, src, dst, s, aoff, on, emit, used):
         for j in range(hid // 256):
             cs = slice(j * 256, (j + 1) * 256)
             a = dot_nn(src[...], w1[s, :, cs])
@@ -167,6 +160,7 @@
             act2[pl.ds(aoff, m), cs] = ga
             dst[:, cs] = u.astype(BF16)
 
+        used(0)
         for j in range(width // 256):
             cs = slice(j * 256, (j + 1) * 256)
             emit(cs, dot_nn(dst[...], w2[s, :, cs]).astype(BF16))
@@ -184,18 +178,18 @@
     def act_off(e):
         return pl.multiple_of(jnp.where(e == 0, 0, hot_rows + (e - 1) * n_rows), 64)
 
-    def add_out(q, e, first):
+    def add_out(q, e, first, fresh):
         gate = column(q, e + 8)
         put = put_rows(q, e)
         for j in range(width // 256):
             cs = slice(j * 256, (j + 1) * 256)
-            ypart[q, :, cs] += gate * dot_nn(put, orow[first:first + cp, cs])
+            ypart[q, :, cs] = jnp.where(fresh, 0.0, ypart[q, :, cs]) + gate * dot_nn(put, orow[first:first + cp, cs])
 
     def add_dx_one(q, p, e):
         put = put_rows(q, e)
         for j in range(width // 256):
             cs = slice(j * 256, (j + 1) * 256)
-            dxpart[q, :, cs] += dot_nn(put, orow[p * cp:(p + 1) * cp, cs])
+            dxpart[q, :, cs] = dot_nn(put, orow[p * cp:(p + 1) * cp, cs])
 
     def add_dx_two(q, p, e):
         now, before = column(q, e), column(q, e - 1)
@@ -211,27 +205,30 @@
         m = mc[q, pl.ds(r, n), :]
         return jnp.sum(jnp.where(lax.broadcasted_iota(jnp.int32, (n, 128), 1) == lane, m, 0.0), axis=1, keepdims=True)
 
-    def hot_forward(p, q, s):
+    def hot_forward(p, q, s, fresh):
         o = pl.multiple_of(p * two, 64)
         gate = column(q, 8)
 
         def emit(cs, out):
-            ypart[q, :, cs] += gate * out.astype(F32)
-
-        forward(two, x_all.at[q], uhot.at[pl.ds(o, two)], s, o, column(q, 0) >= 0.0, emit)
-
-    def cold_forward(e, s, r0, r1):
+            ypart[q, :, cs] = jnp.where(fresh, 0.0, ypart[q, :, cs]) + gate * out.astype(F32)
+
+        forward(two, x_all.at[q], uhot.at[pl.ds(o, two)], s, o, column(q, 0) >= 0.0, emit, lambda part: None)
+
+    def load_next(i, e, step, parts):
+        @pl.when(i < last - 1)
+        def _():
+            for n in parts:
+                w_copies(e + 2 * step)[n].start()
+
+    def cold_forward(i, e, step, s, r0, r1):
         def emit(cs, out):
             orow[0:r1 - r0, cs] = out
 
-        forward(r1 - r0, erows.at[e, r0:r1], urow.at[e, r0:r1], s, pl.multiple_of(act_off(e) + r0, 16), None, emit)
-
-    def turn(i, e, step, first):
-        @pl.when(jnp.logical_and(i >= 1, i < last))
-        def _():
-            for cpy in w_copies(e + step):
-                cpy.start()
-
+        forward(r1 - r0, erows.at[e, r0:r1], urow.at[e, r0:r1], s, pl.multiple_of(act_off(e) + r0, 16), None, emit,
+                lambda part: load_next(i, e, step, (0, 1)))
+        load_next(i, e, step, (2,))
+
+    def weights_here(i, e, first):
         @pl.when(i >= (0 if first else 2))
         def _():
             for cpy in w_copies(e):
@@ -269,7 +266,7 @@
         e = last - i
         s = lax.rem(e, 2)
         hot = jnp.logical_and(is_owner, e == 0)
-        turn(i, e, -1, True)
+        weights_here(i, e, True)
 
         @pl.when(i == 3)
         def _():
@@ -282,12 +279,12 @@
 
         @pl.when(jnp.logical_not(hot))
         def _():
-            cold_forward(e, s, 0, cp)
-            add_out(c, e, 0)
+            cold_forward(i, e, -1, s, 0, cp)
+            add_out(c, e, 0, i == 0)
 
         @pl.when(hot)
         def _():
-            hot_forward(0, c, s)
+            hot_forward(0, c, s, False)
 
     ag(x_all, 0, 1).wait_recv()
     ag(x_all, 0, 7).start()
@@ -303,7 +300,7 @@
     def _(e):
         s = lax.rem(e, 2)
         hot = jnp.logical_and(is_owner, e == 0)
-        turn(e, e, 1, False)
+        weights_here(e, e, False)
 
         @pl.when(e == 2)
         def _():
@@ -321,9 +318,9 @@
 
         @pl.when(jnp.logical_not(hot))
         def _():
-            cold_forward(e, s, cp, 3 * cp)
+            cold_forward(e, e, 1, s, cp, 3 * cp)
             for j, p in ((1, 2), (2, 1)):
-                add_out(near[p], e, (p - 1) * cp)
+                add_out(near[p], e, (p - 1) * cp, e == 0)
 
                 @pl.when(e == last)
                 def _():
@@ -333,7 +330,9 @@
         def _():
             @pl.loop(1, 3)
             def _(p):
-                hot_forward(p, jnp.where(p == 1, c_l, c_r), s)
+                hot_forward(p, jnp.where(p == 1, c_l, c_r), s, True)
+
+            load_next(e, e, 1, (0, 1, 2))
 
     rs(0, 3).wait_recv()
     add_rows(ypart, c, k * tok, cbuf.at[c], tok)
@@ -345,6 +344,9 @@
         return (pltpu.make_async_copy(erows.at[e], xr_hbm.at[e], st_sem.at[0, e]),
                 pltpu.make_async_copy(urow.at[e], ur_hbm.at[e], st_sem.at[1, e]))
 
+    for e in range(n_loc):
+        st_fwd(e)[0].start()
+
     def st_hot():
         return [pltpu.make_async_copy(uhot, uh_hbm, hst_sem.at[0])] + [
             pltpu.make_async_copy(x_all.at[q], xh_hbm.at[p * two:(p + 1) * two], hst_sem.at[1 + p]) for p, q in enumerate(near)]
@@ -354,7 +356,7 @@
         e = last - i
         s = lax.rem(e, 2)
         hot = jnp.logical_and(is_owner, e == 0)
-        turn(i, e, -1, False)
+        weights_here(i, e, False)
 
         @pl.when(i == 1)
         def _():
@@ -373,26 +375,20 @@
 
         @pl.when(jnp.logical_not(hot))
         def _():
-            cold_forward(e, s, 3 * cp, n_rows)
-            add_out(c_o, e, 0)
-            for cpy in st_fwd(e):
-                cpy.start()
+            cold_forward(i, e, -1, s, 3 * cp, n_rows)
+            add_out(c_o, e, 0, i == 0)
+            st_fwd(e)[1].start()
 
         @pl.when(hot)
         def _():
-            hot_forward(3, c_o, s)
+            hot_forward(3, c_o, s, False)
             for cpy in st_hot():
                 cpy.start()
 
     rs(0, 0).start()
 
-    @pl.loop(0, n_loc)
-    def _(e):
-        @pl.when(jnp.logical_not(jnp.logical_and(is_owner, e == 0)))
-        def _():
-            for cpy in st_fwd(e):
-                cpy.wait()
-
+    for e in range(n_loc):
+        st_fwd(e)[0].wait()
     pick(0, c, dy_all, True)
     rs(0, 0).wait_recv()
     add_rows(ypart, c_o, k * tok, cbuf.at[c_o], tok)
@@ -411,6 +407,12 @@
     ag(dy_all, 1, 10).wait_recv()
     pick(3, c_o, dy_all, True)
 
+    @pl.loop(0, n_loc)
+    def _(e):
+        @pl.when(jnp.logical_not(jnp.logical_and(is_owner, e == 0)))
+        def _():
+            st_fwd(e)[1].wait()
+
     @pl.when(is_owner)
     def _():
         for cpy in st_hot():
@@ -439,7 +441,7 @@
         s = lax.rem(e, 2)
         hot = jnp.logical_and(is_owner, e == 0)
 
-        turn(e, e, 1, False)
+        weights_here(e, e, False)
 
         @pl.when(jnp.logical_not(hot))
         def _():
@@ -449,6 +451,7 @@
                 orow[pl.ds(ooff, n_rows), cs] = out
 
             backward(n_rows, erows.at[e], s, act_off(e), emit)
+            load_next(e, e, 1, (0, 1, 2))
 
             @pl.when(e == last - 1)
             def _():
@@ -490,7 +493,7 @@
 
                 def emit(cs, out):
                     for n, q in enumerate(pair):
-                        dxpart[q, :, cs] += out[n * two:(n + 1) * two].astype(F32)
+                        dxpart[q, :, cs] = out[n * two:(n + 1) * two].astype(F32)
 
                 backward(2 * two, hrows, s, o, emit)
                 sa = pltpu.make_async_copy(darow.at[s], dah_hbm.at[pl.ds(o, 2 * two)], hst_sem.at[1])
@@ -500,6 +503,8 @@
                 sd.wait()
                 sa.wait()
                 sb.wait()
+
+            load_next(e, e, 1, (0, 1, 2))
 
         @pl.when(jnp.logical_and(e >= 1, jnp.logical_not(jnp.logical_and(is_owner, e == 1))))
         def _():

time: 109 us -> 108 us (level)
  starting transfers between devices: 8.77 us -> 7.07 us
  waiting for transfers between devices: 2.99 us -> 4.17 us
where the time goes in v6:
time: 108 us
  Pallas kernels  95.4 us (88%)
  starting transfers between devices  7.07 us (7%)
  waiting for transfers between devices  4.17 us (4%)
    pallas_call x1, Pallas kernels, device_fn(): pl.pallas_call(functools.partial(layer_kernel, cfg), out_shape=(sds((tok,...  71.3 us
    pallas_call x1, Pallas kernels, device_fn(): pl.pallas_call(functools.partial(first_grads_kernel, owner), grid=(n_firs...  15.1 us
    pallas_call x1, Pallas kernels, device_fn(): pl.pallas_call(later_grads_kernel, grid=(n_loc - n_first,), out_shape=g_s...  8.93 us
    ppermute x1, starting transfers between devices, device_fn(): from_l = lax.ppermute(go_r, 'ep', to_right)  3.77 us
    ppermute x1, starting transfers between devices, device_fn(): fl_lo = lax.ppermute(sr + from_l[:half], 'ep', to_right)  2.19 us
  transfers between devices with their start and end apart: 4, of which 4 were waited for; matrix products, arithmetic and copies ran while one was open for 0% of the time, Pallas kernels for 22%

profile of v6, /device:TPU:112, one launch (start us, length us, event | category | flops | bytes accessed | tf_op | source)
XLA Modules:
  0.0 108.3 jit_solution(3148881497448464370)
XLA Ops:
  0.6 71.3 %moe_layer.1 = (bf16[128,1536]{1,0:T(8,128)(2,1)}, f32[128,1536]{1,0:T(8,128)}, f32[128,1536]{1,0:T(8,128)}, f32[64,1536]{1,0:T(8,128)}, f32[64,1536]{1,0:T(8,12...) custom-call(bf16[128,1536]{1,0:T(8,128)(2,1)} %x_hbm.1, ...), custom_call_target="tpu_custom_call" | custom-call | tf_op jit(solution)/shard_map/moe_layer/pallas_call | solution.py:632
  72.0 3.8 %collective-permute-start = (f32[128,1536]{1,0:T(8,128)}, f32[128,1536]{1,0:T(8,128)S(1)}, u32[]{:S(2)}, u32[]{:S(2)}) collective-permute-start(f32[128,1536]{1,0:T(8,128)} %get-tuple-element.42), channel_id=1, source_target_pairs={{0,2},{1,3},{2,4},{3,5},{4,6},{5,7},{6,0},{7,1},{8,10},{9,11},{10,... | collective-permute-start | bytes 2359304 | tf_op jit(solution)/shard_map/ppermute | solution.py:671
  75.7 0.6 collective-permute-start.2
  76.4 0.0 copy-start.2
  76.4 0.0 copy-start.1
  76.4 15.1 %first_grads.1 = (bf16[5,1536,512]{2,1,0:T(8,128)(2,1)}, bf16[5,1536,512]{2,1,0:T(8,128)(2,1)}, bf16[5,512,1536]{2,1,0:T(8,128)(2,1)}, bf16[128,1536]{1,0:T(8,128)(2,1)}) custom-call(bf16[5,448,1536]{2,1,0:T(8,128)(2,1)} %get-tuple-element.28.x_ref, bf16[5,448,1536]{2,1,0:T(8,128)(2,1)} %get-tuple-element.29.d_ref, ...), custom_call_target="tpu_custom_call" | custom-call | flops 6341787648 | bytes 26542080 | tf_op jit(solution)/shard_map/first_grads/pallas_call | solution.py:697
  91.5 1.0 collective-permute-done
  92.5 0.0 copy-done.2
  92.5 0.1 slice_add_fusion.1
  92.6 2.2 %collective-permute-start.1 = (f32[64,1536]{1,0:T(8,128)S(1)}, f32[64,1536]{1,0:T(8,128)S(1)}, u32[]{:S(2)}, u32[]{:S(2)}) collective-permute-start(f32[64,1536]{1,0:T(8,128)S(1)} %get-tuple-element.53), channel_id=1, source_target_pairs={{0,2},{1,3},{2,4},{3,5},{4,6},{5,7},{6,0},{7,1},{8,10},{9,11},{10,... | collective-permute-start | bytes 1179656 | tf_op jit(solution)/shard_map/ppermute | solution.py:707
  94.8 1.4 %collective-permute-done.2 = f32[128,1536]{1,0:T(8,128)S(1)} collective-permute-done((f32[128,1536]{1,0:T(8,128)}, f32[128,1536]{1,0:T(8,128)S(1)}, u32[]{:S(2)}, u32[]{:S(2)}) %collective-permute-start.2) | collective-permute-done | bytes 786464 | tf_op jit(solution)/shard_map/ppermute | solution.py:672
  96.1 0.0 copy-done.1
  96.1 0.1 fusion.2
  96.2 0.5 collective-permute-start.3
  96.7 0.0 copy-start
  96.7 8.9 %later_grads.1 = (bf16[5,1536,512]{2,1,0:T(8,128)(2,1)}, bf16[5,1536,512]{2,1,0:T(8,128)(2,1)}, bf16[5,512,1536]{2,1,0:T(8,128)(2,1)}) custom-call(bf16[5,448,1536]{2,1,0:T(8,128)(2,1)} %get-tuple-element.28.x_ref, bf16[5,448,1536]{2,1,0:T(8,128)(2,1)} %get-tuple-element.29.d_ref, ...), custom_call_target="tpu_custom_call", output_to_operand_aliasing={{0}: (5, {}), {1}: (6, {}), {2}: (7, {})} | custom-call | flops 4227858432 | bytes 17694720 | tf_op jit(solution)/shard_map/later_grads/pallas_call | solution.py:709
  105.6 0.4 collective-permute-done.1
  106.0 1.5 %collective-permute-done.3 = f32[64,1536]{1,0:T(8,128)S(1)} collective-permute-done((f32[64,1536]{1,0:T(8,128)S(1)}, f32[64,1536]{1,0:T(8,128)S(1)}, u32[]{:S(2)}, u32[]{:S(2)}) %collective-permute-start.3) | collective-permute-done | bytes 393248 | tf_op jit(solution)/shard_map/ppermute | solution.py:708
  107.4 0.0 copy-done
  107.4 0.9 fusion.1
Async XLA Ops:
  72.0 20.5 %collective-permute-start = (f32[128,1536]{1,0:T(8,128)}, f32[128,1536]{1,0:T(8,128)S(1)}, u32[]{:S(2)}, u32[]{:S(2)}) collective-permute-start(f32[128,1536]{1,0:T(8,128)} %get-tuple-element.42), channel_id=1, source_target_pairs={{0,2},{1,3},{2,4},{3,5},{4,6},{5,7},{6,0},{7,1},{8,10},{9,11},{10,... | collective-permute-start | bytes 2359304 | tf_op jit(solution)/shard_map/ppermute | solution.py:671
  75.7 20.4 %collective-permute-start.2 = (f32[128,1536]{1,0:T(8,128)}, f32[128,1536]{1,0:T(8,128)S(1)}, u32[]{:S(2)}, u32[]{:S(2)}) collective-permute-start(f32[128,1536]{1,0:T(8,128)} %get-tuple-element.43), channel_id=1, source_target_pairs={{0,6},{1,7},{2,0},{3,1},{4,2},{5,3},{6,4},{7,5},{8,14},{9,15},{10,... | collective-permute-start | bytes 2359304 | tf_op jit(solution)/shard_map/ppermute | solution.py:672
  76.4 16.1 %copy-start.2 = (f32[64,1536]{1,0:T(8,128)S(1)}, f32[64,1536]{1,0:T(8,128)}, u32[]{:S(2)}) copy-start(f32[64,1536]{1,0:T(8,128)} %get-tuple-element.41) | copy-start | bytes 1179652
  76.4 19.8 %copy-start.1 = (f32[64,1536]{1,0:T(8,128)S(1)}, f32[64,1536]{1,0:T(8,128)}, u32[]{:S(2)}) copy-start(f32[64,1536]{1,0:T(8,128)} %get-tuple-element.44) | copy-start | bytes 1179652
  92.6 13.4 %collective-permute-start.1 = (f32[64,1536]{1,0:T(8,128)S(1)}, f32[64,1536]{1,0:T(8,128)S(1)}, u32[]{:S(2)}, u32[]{:S(2)}) collective-permute-start(f32[64,1536]{1,0:T(8,128)S(1)} %get-tuple-element.53), channel_id=1, source_target_pairs={{0,2},{1,3},{2,4},{3,5},{4,6},{5,7},{6,0},{7,1},{8,10},{9,11},{10,... | collective-permute-start | bytes 1179656 | tf_op jit(solution)/shard_map/ppermute | solution.py:707
  96.2 11.2 %collective-permute-start.3 = (f32[64,1536]{1,0:T(8,128)S(1)}, f32[64,1536]{1,0:T(8,128)S(1)}, u32[]{:S(2)}, u32[]{:S(2)}) collective-permute-start(f32[64,1536]{1,0:T(8,128)S(1)} %get-tuple-element.52), channel_id=1, source_target_pairs={{0,6},{1,7},{2,0},{3,1},{4,2},{5,3},{6,4},{7,5},{8,14},{9,15},{10,... | collective-permute-start | bytes 1179656 | tf_op jit(solution)/shard_map/ppermute | solution.py:708
  96.7 10.8 %copy-start = (f32[128,1536]{1,0:T(8,128)S(1)}, f32[128,1536]{1,0:T(8,128)}, u32[]{:S(2)}) copy-start(f32[128,1536]{1,0:T(8,128)} %get-tuple-element.40) | copy-start | bytes 2359300

commit v7 on v6

--- a/solution.py
+++ b/solution.py
@@ -60,7 +60,7 @@
                 pltpu.make_async_copy(w3_hbm.at[e], w3.at[s], w_sem.at[1, s]),
                 pltpu.make_async_copy(w2_hbm.at[e], w2.at[s], w_sem.at[2, s]))
 
-    for e in (last, last - 1):
+    for e in (0, 1):
         for cpy in w_copies(e):
             cpy.start()
     ids_all[me] = ids_ref[...]
@@ -262,13 +262,12 @@
     pick(0, c, x_all, False)
 
     @pl.loop(0, n_loc)
-    def _(i):
-        e = last - i
+    def _(e):
         s = lax.rem(e, 2)
         hot = jnp.logical_and(is_owner, e == 0)
-        weights_here(i, e, True)
-
-        @pl.when(i == 3)
+        weights_here(e, e, True)
+
+        @pl.when(e == 2)
         def _():
             ag(x_all, 0, 0).wait_recv()
             ag(x_all, 0, 5).start()
@@ -279,12 +278,13 @@
 
         @pl.when(jnp.logical_not(hot))
         def _():
-            cold_forward(i, e, -1, s, 0, cp)
-            add_out(c, e, 0, i == 0)
+            cold_forward(e, e, 1, s, 0, cp)
+            add_out(c, e, 0, e == 0)
 
         @pl.when(hot)
         def _():
-            hot_forward(0, c, s, False)
+            hot_forward(0, c, s, True)
+            load_next(e, e, 1, (0, 1, 2))
 
     ag(x_all, 0, 1).wait_recv()
     ag(x_all, 0, 7).start()
@@ -293,47 +293,12 @@
     rs(0, 3).start()
     ag(x_all, 0, 7).wait_recv()
     pick(1, c_l, x_all, False)
+    ag(x_all, 0, 5).wait_recv()
+    ag(x_all, 0, 9).start()
+    ag(x_all, 0, 6).wait_recv()
+    ag(x_all, 0, 10).start()
     ag(x_all, 0, 8).wait_recv()
     pick(2, c_r, x_all, False)
-
-    @pl.loop(0, n_loc)
-    def _(e):
-        s = lax.rem(e, 2)
-        hot = jnp.logical_and(is_owner, e == 0)
-        weights_here(e, e, False)
-
-        @pl.when(e == 2)
-        def _():
-            ag(x_all, 0, 5).wait_recv()
-            ag(x_all, 0, 9).start()
-            ag(x_all, 0, 6).wait_recv()
-            ag(x_all, 0, 10).start()
-
-        @pl.when(e == last)
-        def _():
-            ag(dy_all, 1, 0).wait_recv()
-            ag(dy_all, 1, 5).start()
-            ag(dy_all, 1, 2).wait_recv()
-            ag(dy_all, 1, 6).start()
-
-        @pl.when(jnp.logical_not(hot))
-        def _():
-            cold_forward(e, e, 1, s, cp, 3 * cp)
-            for j, p in ((1, 2), (2, 1)):
-                add_out(near[p], e, (p - 1) * cp, e == 0)
-
-                @pl.when(e == last)
-                def _():
-                    rs(0, j).start()
-
-        @pl.when(hot)
-        def _():
-            @pl.loop(1, 3)
-            def _(p):
-                hot_forward(p, jnp.where(p == 1, c_l, c_r), s, True)
-
-            load_next(e, e, 1, (0, 1, 2))
-
     rs(0, 3).wait_recv()
     add_rows(ypart, c, k * tok, cbuf.at[c], tok)
     ag(x_all, 0, 9).wait_recv()
@@ -360,10 +325,10 @@
 
         @pl.when(i == 1)
         def _():
-            for j, q in ((1, c_r), (2, c_l)):
-                rs(0, j).wait_recv()
-                add_rows(ypart, q, k * tok, cbuf.at[q], tok)
-                rs(0, 5 + j).start()
+            ag(dy_all, 1, 0).wait_recv()
+            ag(dy_all, 1, 5).start()
+            ag(dy_all, 1, 2).wait_recv()
+            ag(dy_all, 1, 6).start()
 
         @pl.when(i == 3)
         def _():
@@ -375,32 +340,48 @@
 
         @pl.when(jnp.logical_not(hot))
         def _():
-            cold_forward(i, e, -1, s, 3 * cp, n_rows)
-            add_out(c_o, e, 0, i == 0)
+            cold_forward(i, e, -1, s, cp, n_rows)
+            for j, p in enumerate((3, 2, 1)):
+                add_out(near[p], e, (p - 1) * cp, i == 0)
+
+                @pl.when(i == last)
+                def _():
+                    rs(0, j).start()
+
             st_fwd(e)[1].start()
 
         @pl.when(hot)
         def _():
-            hot_forward(3, c_o, s, False)
+            @pl.loop(0, 3)
+            def _(n):
+                p = 3 - n
+                hot_forward(p, jnp.where(p == 1, c_l, jnp.where(p == 2, c_r, c_o)), s, False)
+                for j in range(3):
+                    @pl.when(n == j)
+                    def _():
+                        rs(0, j).start()
+
             for cpy in st_hot():
                 cpy.start()
 
-    rs(0, 0).start()
-
     for e in range(n_loc):
         st_fwd(e)[0].wait()
-    pick(0, c, dy_all, True)
     rs(0, 0).wait_recv()
     add_rows(ypart, c_o, k * tok, cbuf.at[c_o], tok)
     rs(0, 4).start()
     rs(0, 5).start()
-    pl.semaphore_signal(free_sem, inc=1, device_id={"ep": partner}, device_id_type=MESH)
-    ag(dy_all, 1, 7).wait_recv()
-    pick(1, c_l, dy_all, True)
     ag(dy_all, 1, 5).wait_recv()
     ag(dy_all, 1, 9).start()
     ag(dy_all, 1, 6).wait_recv()
     ag(dy_all, 1, 10).start()
+    pick(0, c, dy_all, True)
+    for j, q in ((1, c_r), (2, c_l)):
+        rs(0, j).wait_recv()
+        add_rows(ypart, q, k * tok, cbuf.at[q], tok)
+        rs(0, 5 + j).start()
+    pl.semaphore_signal(free_sem, inc=1, device_id={"ep": partner}, device_id_type=MESH)
+    ag(dy_all, 1, 7).wait_recv()
+    pick(1, c_l, dy_all, True)
     ag(dy_all, 1, 8).wait_recv()
     pick(2, c_r, dy_all, True)
     ag(dy_all, 1, 9).wait_recv()
@@ -453,7 +434,7 @@
             backward(n_rows, erows.at[e], s, act_off(e), emit)
             load_next(e, e, 1, (0, 1, 2))
 
-            @pl.when(e == last - 1)
+            @pl.when(e == last - 2)
             def _():
                 rs_relay_y()
 

time: 108 us -> 105 us (0.972)
  Pallas kernels: 95.4 us -> 93.4 us
  waiting for transfers between devices: 4.17 us -> 2.9 us
    ppermute x1, starting transfers between devices: 3.77 us -> 1.24 us  [device_fn(): from_l = lax.ppermute(go_r, 'ep', to_right)]
    pallas_call x1, Pallas kernels: 71.3 us -> 69.3 us  [device_fn(): pl.pallas_call(functools.partial(layer_kernel, cfg), out_shape=(sds((tok,...]
    ppermute x1, starting transfers between devices: 0.65 us -> 2.07 us  [device_fn(): from_r = lax.ppermute(go_l, 'ep', to_left)]
  transfers between devices with their start and end apart: 4 -> 4, of which waited for: 4 -> 3; matrix products, arithmetic and copies ran while one was open for 0% -> 0% of each run, Pallas kernels for 22% -> 23%
where the time goes in v7:
time: 105 us; the launch traced here: 104 us
  Pallas kernels  93.4 us (89%)
  starting transfers between devices  6.39 us (6%)
  waiting for transfers between devices  2.9 us (3%)
    pallas_call x1, Pallas kernels, device_fn(): pl.pallas_call(functools.partial(layer_kernel, cfg), out_shape=(sds((tok,...  69.3 us
    pallas_call x1, Pallas kernels, device_fn(): pl.pallas_call(functools.partial(first_grads_kernel, owner), grid=(n_firs...  15.1 us
    pallas_call x1, Pallas kernels, device_fn(): pl.pallas_call(later_grads_kernel, grid=(n_loc - n_first,), out_shape=g_s...  8.93 us
  transfers between devices with their start and end apart: 4, of which 3 were waited for; matrix products, arithmetic and copies ran while one was open for 0% of the time, Pallas kernels for 23%

profile of v7, /device:TPU:112, one launch (start us, length us, event | category | flops | bytes accessed | tf_op | source)
XLA Modules:
  0.0 104.4 jit_solution(7649599453679170092)
XLA Ops:
  0.6 69.3 %moe_layer.1 = (bf16[128,1536]{1,0:T(8,128)(2,1)}, f32[128,1536]{1,0:T(8,128)}, f32[128,1536]{1,0:T(8,128)}, f32[64,1536]{1,0:T(8,128)}, f32[64,1536]{1,0:T(8,12...) custom-call(bf16[128,1536]{1,0:T(8,128)(2,1)} %x_hbm.1, ...), custom_call_target="tpu_custom_call" | custom-call | tf_op jit(solution)/shard_map/moe_layer/pallas_call | solution.py:613
  70.0 1.2 %collective-permute-start = (f32[128,1536]{1,0:T(8,128)}, f32[128,1536]{1,0:T(8,128)S(1)}, u32[]{:S(2)}, u32[]{:S(2)}) collective-permute-start(f32[128,1536]{1,0:T(8,128)} %get-tuple-element.42), channel_id=1, source_target_pairs={{0,2},{1,3},{2,4},{3,5},{4,6},{5,7},{6,0},{7,1},{8,10},{9,11},{10,... | collective-permute-start | bytes 2359304 | tf_op jit(solution)/shard_map/ppermute | solution.py:652
  71.2 2.1 %collective-permute-start.2 = (f32[128,1536]{1,0:T(8,128)}, f32[128,1536]{1,0:T(8,128)S(1)}, u32[]{:S(2)}, u32[]{:S(2)}) collective-permute-start(f32[128,1536]{1,0:T(8,128)} %get-tuple-element.43), channel_id=1, source_target_pairs={{0,6},{1,7},{2,0},{3,1},{4,2},{5,3},{6,4},{7,5},{8,14},{9,15},{10,... | collective-permute-start | bytes 2359304 | tf_op jit(solution)/shard_map/ppermute | solution.py:653
  73.3 0.0 copy-start.2
  73.3 0.0 copy-start.1
  73.3 15.1 %first_grads.1 = (bf16[5,1536,512]{2,1,0:T(8,128)(2,1)}, bf16[5,1536,512]{2,1,0:T(8,128)(2,1)}, bf16[5,512,1536]{2,1,0:T(8,128)(2,1)}, bf16[128,1536]{1,0:T(8,128)(2,1)}) custom-call(bf16[5,448,1536]{2,1,0:T(8,128)(2,1)} %get-tuple-element.28.x_ref, bf16[5,448,1536]{2,1,0:T(8,128)(2,1)} %get-tuple-element.29.d_ref, ...), custom_call_target="tpu_custom_call" | custom-call | flops 6341787648 | bytes 26542080 | tf_op jit(solution)/shard_map/first_grads/pallas_call | solution.py:678
  88.4 1.3 %collective-permute-done = f32[128,1536]{1,0:T(8,128)S(1)} collective-permute-done((f32[128,1536]{1,0:T(8,128)}, f32[128,1536]{1,0:T(8,128)S(1)}, u32[]{:S(2)}, u32[]{:S(2)}) %collective-permute-start) | collective-permute-done | bytes 786464 | tf_op jit(solution)/shard_map/ppermute | solution.py:652
  89.7 0.0 copy-done.2
  89.7 0.1 slice_add_fusion.1
  89.8 1.5 %collective-permute-start.1 = (f32[64,1536]{1,0:T(8,128)S(1)}, f32[64,1536]{1,0:T(8,128)S(1)}, u32[]{:S(2)}, u32[]{:S(2)}) collective-permute-start(f32[64,1536]{1,0:T(8,128)S(1)} %get-tuple-element.53), channel_id=1, source_target_pairs={{0,2},{1,3},{2,4},{3,5},{4,6},{5,7},{6,0},{7,1},{8,10},{9,11},{10,... | collective-permute-start | bytes 1179656 | tf_op jit(solution)/shard_map/ppermute | solution.py:688
  91.3 0.3 collective-permute-done.2
  91.6 0.0 copy-done.1
  91.6 0.1 fusion.2
  91.7 1.5 %collective-permute-start.3 = (f32[64,1536]{1,0:T(8,128)S(1)}, f32[64,1536]{1,0:T(8,128)S(1)}, u32[]{:S(2)}, u32[]{:S(2)}) collective-permute-start(f32[64,1536]{1,0:T(8,128)S(1)} %get-tuple-element.52), channel_id=1, source_target_pairs={{0,6},{1,7},{2,0},{3,1},{4,2},{5,3},{6,4},{7,5},{8,14},{9,15},{10,... | collective-permute-start | bytes 1179656 | tf_op jit(solution)/shard_map/ppermute | solution.py:689
  93.2 0.0 copy-start
  93.2 8.9 %later_grads.1 = (bf16[5,1536,512]{2,1,0:T(8,128)(2,1)}, bf16[5,1536,512]{2,1,0:T(8,128)(2,1)}, bf16[5,512,1536]{2,1,0:T(8,128)(2,1)}) custom-call(bf16[5,448,1536]{2,1,0:T(8,128)(2,1)} %get-tuple-element.28.x_ref, bf16[5,448,1536]{2,1,0:T(8,128)(2,1)} %get-tuple-element.29.d_ref, ...), custom_call_target="tpu_custom_call", output_to_operand_aliasing={{0}: (5, {}), {1}: (6, {}), {2}: (7, {})} | custom-call | flops 4227858432 | bytes 17694720 | tf_op jit(solution)/shard_map/later_grads/pallas_call | solution.py:690
  102.2 0.0 collective-permute-done.1
  102.2 1.3 %collective-permute-done.3 = f32[64,1536]{1,0:T(8,128)S(1)} collective-permute-done((f32[64,1536]{1,0:T(8,128)S(1)}, f32[64,1536]{1,0:T(8,128)S(1)}, u32[]{:S(2)}, u32[]{:S(2)}) %collective-permute-start.3) | collective-permute-done | bytes 393248 | tf_op jit(solution)/shard_map/ppermute | solution.py:689
  103.5 0.0 copy-done
  103.5 0.9 fusion.1
Async XLA Ops:
  70.0 19.7 %collective-permute-start = (f32[128,1536]{1,0:T(8,128)}, f32[128,1536]{1,0:T(8,128)S(1)}, u32[]{:S(2)}, u32[]{:S(2)}) collective-permute-start(f32[128,1536]{1,0:T(8,128)} %get-tuple-element.42), channel_id=1, source_target_pairs={{0,2},{1,3},{2,4},{3,5},{4,6},{5,7},{6,0},{7,1},{8,10},{9,11},{10,... | collective-permute-start | bytes 2359304 | tf_op jit(solution)/shard_map/ppermute | solution.py:652
  71.2 20.4 %collective-permute-start.2 = (f32[128,1536]{1,0:T(8,128)}, f32[128,1536]{1,0:T(8,128)S(1)}, u32[]{:S(2)}, u32[]{:S(2)}) collective-permute-start(f32[128,1536]{1,0:T(8,128)} %get-tuple-element.43), channel_id=1, source_target_pairs={{0,6},{1,7},{2,0},{3,1},{4,2},{5,3},{6,4},{7,5},{8,14},{9,15},{10,... | collective-permute-start | bytes 2359304 | tf_op jit(solution)/shard_map/ppermute | solution.py:653
  73.3 16.4 %copy-start.2 = (f32[64,1536]{1,0:T(8,128)S(1)}, f32[64,1536]{1,0:T(8,128)}, u32[]{:S(2)}) copy-start(f32[64,1536]{1,0:T(8,128)} %get-tuple-element.41) | copy-start | bytes 1179652
  73.3 18.3 %copy-start.1 = (f32[64,1536]{1,0:T(8,128)S(1)}, f32[64,1536]{1,0:T(8,128)}, u32[]{:S(2)}) copy-start(f32[64,1536]{1,0:T(8,128)} %get-tuple-element.44) | copy-start | bytes 1179652
  89.8 12.4 %collective-permute-start.1 = (f32[64,1536]{1,0:T(8,128)S(1)}, f32[64,1536]{1,0:T(8,128)S(1)}, u32[]{:S(2)}, u32[]{:S(2)}) collective-permute-start(f32[64,1536]{1,0:T(8,128)S(1)} %get-tuple-element.53), channel_id=1, source_target_pairs={{0,2},{1,3},{2,4},{3,5},{4,6},{5,7},{6,0},{7,1},{8,10},{9,11},{10,... | collective-permute-start | bytes 1179656 | tf_op jit(solution)/shard_map/ppermute | solution.py:688
  91.7 11.8 %collective-permute-start.3 = (f32[64,1536]{1,0:T(8,128)S(1)}, f32[64,1536]{1,0:T(8,128)S(1)}, u32[]{:S(2)}, u32[]{:S(2)}) collective-permute-start(f32[64,1536]{1,0:T(8,128)S(1)} %get-tuple-element.52), channel_id=1, source_target_pairs={{0,6},{1,7},{2,0},{3,1},{4,2},{5,3},{6,4},{7,5},{8,14},{9,15},{10,... | collective-permute-start | bytes 1179656 | tf_op jit(solution)/shard_map/ppermute | solution.py:689
  93.2 10.3 %copy-start = (f32[128,1536]{1,0:T(8,128)S(1)}, f32[128,1536]{1,0:T(8,128)}, u32[]{:S(2)}) copy-start(f32[128,1536]{1,0:T(8,128)} %get-tuple-element.40) | copy-start | bytes 2359300

commit v8 on v7

--- a/solution.py
+++ b/solution.py
@@ -165,15 +165,20 @@
             cs = slice(j * 256, (j + 1) * 256)
             emit(cs, dot_nn(dst[...], w2[s, :, cs]).astype(BF16))
 
-    def backward(m, src, s, aoff, emit):
+    all_tiles = range(width // 256)
+
+    def backward_du(m, src, s, aoff, ab=None):
+        ab = s if ab is None else ab
         for j in range(hid // 256):
             cs = slice(j * 256, (j + 1) * 256)
             du = dot_nt(src[...], w2[s, cs, :])
-            darow[s, 0:m, cs] = (du * act1[pl.ds(aoff, m), cs]).astype(BF16)
-            dbrow[s, 0:m, cs] = (du * act2[pl.ds(aoff, m), cs]).astype(BF16)
-        for j in range(width // 256):
+            darow[ab, 0:m, cs] = (du * act1[pl.ds(aoff, m), cs]).astype(BF16)
+            dbrow[ab, 0:m, cs] = (du * act2[pl.ds(aoff, m), cs]).astype(BF16)
+    def backward_dx(m, s, tiles, emit, ab=None):
+        ab = s if ab is None else ab
+        for j in tiles:
             cs = slice(j * 256, (j + 1) * 256)
-            emit(cs, (dot_nt(darow[s, 0:m, :], w1[s, cs, :]) + dot_nt(dbrow[s, 0:m, :], w3[s, cs, :])).astype(BF16))
+            emit(cs, (dot_nt(darow[ab, 0:m, :], w1[s, cs, :]) + dot_nt(dbrow[ab, 0:m, :], w3[s, cs, :])).astype(BF16))
 
     def act_off(e):
         return pl.multiple_of(jnp.where(e == 0, 0, hot_rows + (e - 1) * n_rows), 64)
@@ -191,12 +196,12 @@
             cs = slice(j * 256, (j + 1) * 256)
             dxpart[q, :, cs] = dot_nn(put, orow[p * cp:(p + 1) * cp, cs])
 
-    def add_dx_two(q, p, e):
+    def add_dx_two(q, p, e, tiles):
         now, before = column(q, e), column(q, e - 1)
         now = jnp.where(now >= 0.0, now + float(cp), -1.0)
         lane = lax.broadcasted_iota(jnp.int32, (two, 2 * cp), 1).astype(F32)
         put = jnp.where(jnp.logical_or(before == lane, now == lane), 1.0, 0.0).astype(BF16)
-        for j in range(width // 256):
+        for j in tiles:
             cs = slice(j * 256, (j + 1) * 256)
             both = jnp.concatenate([orow[2 * two + p * cp:2 * two + (p + 1) * cp, cs], orow[p * cp:(p + 1) * cp, cs]], axis=0)
             dxpart[q, :, cs] += dot_nn(put, both)
@@ -240,6 +245,11 @@
         if j < 4:
             q = (c_o, c_r, c_l, c)[j]
             src, dst, dev = part.at[q, pl.ds((1 - k) * tok, tok)], cbuf.at[q], partner
+            if t == 1:
+                src, dst = part.at[q, pl.ds((1 - k) * tok, tok), 0:width // 2], cbuf.at[q, :, 0:width // 2]
+        elif j >= 10:
+            q = (c_o, c_r, c_l, c)[j - 10]
+            src, dst, dev = part.at[q, pl.ds((1 - k) * tok, tok), width // 2:width], cbuf.at[q, :, width // 2:width], partner
         else:
             src, dst, dev = (
                 (part.at[c_o, pl.ds(o, half)], yra, right),
@@ -409,6 +419,11 @@
     for e in range(n_loc):
         st_d(e).start()
 
+    def st_hot_ab(h):
+        at = pl.multiple_of(h * 2 * two, 64)
+        return (pltpu.make_async_copy(darow.at[h], dah_hbm.at[pl.ds(at, 2 * two)], hst_sem.at[1 + h]),
+                pltpu.make_async_copy(dbrow.at[h], dbh_hbm.at[pl.ds(at, 2 * two)], hst_sem.at[3 + h]))
+
     def rs_relay_y():
         rs(0, 4).wait_recv()
         add_rows(ypart, c_r, k * tok, yra, half)
@@ -424,6 +439,12 @@
 
         weights_here(e, e, False)
 
+        @pl.when(jnp.logical_and(is_owner, e == 1))
+        def _():
+            for h in range(2):
+                for cpy in st_hot_ab(h):
+                    cpy.wait()
+
         @pl.when(jnp.logical_not(hot))
         def _():
             ooff = pl.multiple_of(s * 2 * two, 64)
@@ -431,30 +452,37 @@
             def emit(cs, out):
                 orow[pl.ds(ooff, n_rows), cs] = out
 
-            backward(n_rows, erows.at[e], s, act_off(e), emit)
-            load_next(e, e, 1, (0, 1, 2))
-
-            @pl.when(e == last - 2)
+            backward_du(n_rows, erows.at[e], s, act_off(e))
+
+            @pl.when(e < last)
             def _():
-                rs_relay_y()
-
-            @pl.when(e == 0)
-            def _():
-                for p in range(chips):
-                    add_dx_one(near[p], p, e)
+                backward_dx(n_rows, s, all_tiles, emit)
+                load_next(e, e, 1, (0, 1, 2))
+
+                @pl.when(e == last - 2)
+                def _():
+                    rs_relay_y()
+
+                @pl.when(e == 0)
+                def _():
+                    for p in range(chips):
+                        add_dx_one(near[p], p, e)
+
+                @pl.when(jnp.logical_and(e > 0, s == 0))
+                def _():
+                    for p in (3, 2, 1, 0):
+                        add_dx_two(near[p], p, e, all_tiles)
 
             @pl.when(e == last)
             def _():
-                pl.semaphore_wait(free_sem, 1)
-
-            @pl.when(jnp.logical_and(e > 0, s == 0))
-            def _():
-                for j, p in enumerate((3, 2, 1, 0)):
-                    add_dx_two(near[p], p, e)
-
-                    @pl.when(e == last)
-                    def _():
-                        rs(1, j).start()
+                for h in range(2):
+                    tiles = all_tiles[h * len(all_tiles) // 2:(h + 1) * len(all_tiles) // 2]
+                    backward_dx(n_rows, s, tiles, emit)
+                    if h == 0:
+                        pl.semaphore_wait(free_sem, 1)
+                    for j, p in enumerate((3, 2, 1, 0)):
+                        add_dx_two(near[p], p, e, tiles)
+                        rs(1, j + 10 * h).start()
 
         @pl.when(hot)
         def _():
@@ -476,14 +504,11 @@
                     for n, q in enumerate(pair):
                         dxpart[q, :, cs] = out[n * two:(n + 1) * two].astype(F32)
 
-                backward(2 * two, hrows, s, o, emit)
-                sa = pltpu.make_async_copy(darow.at[s], dah_hbm.at[pl.ds(o, 2 * two)], hst_sem.at[1])
-                sb = pltpu.make_async_copy(dbrow.at[s], dbh_hbm.at[pl.ds(o, 2 * two)], hst_sem.at[2])
-                sa.start()
-                sb.start()
+                backward_du(2 * two, hrows, s, o, h)
+                backward_dx(2 * two, s, all_tiles, emit, h)
+                for cpy in st_hot_ab(h):
+                    cpy.start()
                 sd.wait()
-                sa.wait()
-                sb.wait()
 
             load_next(e, e, 1, (0, 1, 2))
 
@@ -520,6 +545,7 @@
 
     for j, q in enumerate((c_o, c_r, c_l, c)):
         rs(1, j).wait_recv()
+        rs(1, j + 10).wait_recv()
         add_rows(dxpart, q, k * tok, cbuf.at[q], tok)
         for cpy in chip_sums_out(j):
             cpy.start()
@@ -540,6 +566,7 @@
         rs(0, j).wait_send()
     for j in range(4):
         rs(1, j).wait_send()
+        rs(1, j + 10).wait_send()
         for cpy in chip_sums_out(j):
             cpy.wait()
     y_out.wait()
@@ -638,7 +665,7 @@
                     pltpu.VMEM((tok, width), BF16),
                     pltpu.SemaphoreType.DMA((2, group)), pltpu.SemaphoreType.DMA((2, group)),
                     pltpu.SemaphoreType.DMA((2, 11)), pltpu.SemaphoreType.DMA((2, 11)),
-                    pltpu.SemaphoreType.DMA((2, 10)), pltpu.SemaphoreType.DMA((2, 10)),
+                    pltpu.SemaphoreType.DMA((2, 14)), pltpu.SemaphoreType.DMA((2, 14)),
                     pltpu.SemaphoreType.DMA((3, 2)), pltpu.SemaphoreType.DMA((2, n_loc)), pltpu.SemaphoreType.DMA((5,)),
                     pltpu.SemaphoreType.DMA((2,)), pltpu.SemaphoreType.DMA((7,)), pltpu.SemaphoreType.REGULAR,
                 ],

time: 105 us -> 104 us (level)
  no operation moved by 1% of the time
where the time goes in v8:
time: 104 us
  Pallas kernels  93.5 us (90%)
  starting transfers between devices  5.56 us (5%)
  waiting for transfers between devices  2.94 us (3%)
    pallas_call x1, Pallas kernels, device_fn(): pl.pallas_call(functools.partial(layer_kernel, cfg), out_shape=(sds((tok,...  69.5 us
    pallas_call x1, Pallas kernels, device_fn(): pl.pallas_call(functools.partial(first_grads_kernel, owner), grid=(n_firs...  15.1 us
    pallas_call x1, Pallas kernels, device_fn(): pl.pallas_call(later_grads_kernel, grid=(n_loc - n_first,), out_shape=g_s...  8.93 us
  transfers between devices with their start and end apart: 4, of which 3 were waited for; matrix products, arithmetic and copies ran while one was open for 0% of the time, Pallas kernels for 23%

profile of v8, /device:TPU:112, one launch (start us, length us, event | category | flops | bytes accessed | tf_op | source)
XLA Modules:
  0.0 103.7 jit_solution(15647627565366182784)
XLA Ops:
  0.6 69.5 %moe_layer.1 = (bf16[128,1536]{1,0:T(8,128)(2,1)}, f32[128,1536]{1,0:T(8,128)}, f32[128,1536]{1,0:T(8,128)}, f32[64,1536]{1,0:T(8,128)}, f32[64,1536]{1,0:T(8,12...) custom-call(bf16[128,1536]{1,0:T(8,128)(2,1)} %x_hbm.1, ...), custom_call_target="tpu_custom_call" | custom-call | tf_op jit(solution)/shard_map/moe_layer/pallas_call | solution.py:640
  70.1 1.2 %collective-permute-start = (f32[128,1536]{1,0:T(8,128)}, f32[128,1536]{1,0:T(8,128)S(1)}, u32[]{:S(2)}, u32[]{:S(2)}) collective-permute-start(f32[128,1536]{1,0:T(8,128)} %get-tuple-element.42), channel_id=1, source_target_pairs={{0,2},{1,3},{2,4},{3,5},{4,6},{5,7},{6,0},{7,1},{8,10},{9,11},{10,... | collective-permute-start | bytes 2359304 | tf_op jit(solution)/shard_map/ppermute | solution.py:679
  71.4 2.1 %collective-permute-start.2 = (f32[128,1536]{1,0:T(8,128)}, f32[128,1536]{1,0:T(8,128)S(1)}, u32[]{:S(2)}, u32[]{:S(2)}) collective-permute-start(f32[128,1536]{1,0:T(8,128)} %get-tuple-element.43), channel_id=1, source_target_pairs={{0,6},{1,7},{2,0},{3,1},{4,2},{5,3},{6,4},{7,5},{8,14},{9,15},{10,... | collective-permute-start | bytes 2359304 | tf_op jit(solution)/shard_map/ppermute | solution.py:680
  73.4 0.0 copy-start.2
  73.5 0.0 copy-start.1
  73.5 15.1 %first_grads.1 = (bf16[5,1536,512]{2,1,0:T(8,128)(2,1)}, bf16[5,1536,512]{2,1,0:T(8,128)(2,1)}, bf16[5,512,1536]{2,1,0:T(8,128)(2,1)}, bf16[128,1536]{1,0:T(8,128)(2,1)}) custom-call(bf16[5,448,1536]{2,1,0:T(8,128)(2,1)} %get-tuple-element.28.x_ref, bf16[5,448,1536]{2,1,0:T(8,128)(2,1)} %get-tuple-element.29.d_ref, ...), custom_call_target="tpu_custom_call" | custom-call | flops 6341787648 | bytes 26542080 | tf_op jit(solution)/shard_map/first_grads/pallas_call | solution.py:705
  88.6 1.3 %collective-permute-done = f32[128,1536]{1,0:T(8,128)S(1)} collective-permute-done((f32[128,1536]{1,0:T(8,128)}, f32[128,1536]{1,0:T(8,128)S(1)}, u32[]{:S(2)}, u32[]{:S(2)}) %collective-permute-start) | collective-permute-done | bytes 786464 | tf_op jit(solution)/shard_map/ppermute | solution.py:679
  89.9 0.0 copy-done.2
  89.9 0.1 slice_add_fusion.1
  90.0 0.6 collective-permute-start.1
  90.5 1.2 %collective-permute-done.2 = f32[128,1536]{1,0:T(8,128)S(1)} collective-permute-done((f32[128,1536]{1,0:T(8,128)}, f32[128,1536]{1,0:T(8,128)S(1)}, u32[]{:S(2)}, u32[]{:S(2)}) %collective-permute-start.2) | collective-permute-done | bytes 786464 | tf_op jit(solution)/shard_map/ppermute | solution.py:680
  91.7 0.0 copy-done.1
  91.7 0.1 fusion.2
  91.8 1.7 %collective-permute-start.3 = (f32[64,1536]{1,0:T(8,128)S(1)}, f32[64,1536]{1,0:T(8,128)S(1)}, u32[]{:S(2)}, u32[]{:S(2)}) collective-permute-start(f32[64,1536]{1,0:T(8,128)S(1)} %get-tuple-element.52), channel_id=1, source_target_pairs={{0,6},{1,7},{2,0},{3,1},{4,2},{5,3},{6,4},{7,5},{8,14},{9,15},{10,... | collective-permute-start | bytes 1179656 | tf_op jit(solution)/shard_map/ppermute | solution.py:716
  93.4 0.0 copy-start
  93.4 8.9 %later_grads.1 = (bf16[5,1536,512]{2,1,0:T(8,128)(2,1)}, bf16[5,1536,512]{2,1,0:T(8,128)(2,1)}, bf16[5,512,1536]{2,1,0:T(8,128)(2,1)}) custom-call(bf16[5,448,1536]{2,1,0:T(8,128)(2,1)} %get-tuple-element.28.x_ref, bf16[5,448,1536]{2,1,0:T(8,128)(2,1)} %get-tuple-element.29.d_ref, ...), custom_call_target="tpu_custom_call", output_to_operand_aliasing={{0}: (5, {}), {1}: (6, {}), {2}: (7, {})} | custom-call | flops 4227858432 | bytes 17694720 | tf_op jit(solution)/shard_map/later_grads/pallas_call | solution.py:717
  102.4 0.0 collective-permute-done.1
  102.4 0.5 collective-permute-done.3
  102.9 0.0 copy-done
  102.9 0.9 fusion.1
Async XLA Ops:
  70.1 19.8 %collective-permute-start = (f32[128,1536]{1,0:T(8,128)}, f32[128,1536]{1,0:T(8,128)S(1)}, u32[]{:S(2)}, u32[]{:S(2)}) collective-permute-start(f32[128,1536]{1,0:T(8,128)} %get-tuple-element.42), channel_id=1, source_target_pairs={{0,2},{1,3},{2,4},{3,5},{4,6},{5,7},{6,0},{7,1},{8,10},{9,11},{10,... | collective-permute-start | bytes 2359304 | tf_op jit(solution)/shard_map/ppermute | solution.py:679
  71.4 20.3 %collective-permute-start.2 = (f32[128,1536]{1,0:T(8,128)}, f32[128,1536]{1,0:T(8,128)S(1)}, u32[]{:S(2)}, u32[]{:S(2)}) collective-permute-start(f32[128,1536]{1,0:T(8,128)} %get-tuple-element.43), channel_id=1, source_target_pairs={{0,6},{1,7},{2,0},{3,1},{4,2},{5,3},{6,4},{7,5},{8,14},{9,15},{10,... | collective-permute-start | bytes 2359304 | tf_op jit(solution)/shard_map/ppermute | solution.py:680
  73.4 16.4 %copy-start.2 = (f32[64,1536]{1,0:T(8,128)S(1)}, f32[64,1536]{1,0:T(8,128)}, u32[]{:S(2)}) copy-start(f32[64,1536]{1,0:T(8,128)} %get-tuple-element.41) | copy-start | bytes 1179652
  73.5 18.2 %copy-start.1 = (f32[64,1536]{1,0:T(8,128)S(1)}, f32[64,1536]{1,0:T(8,128)}, u32[]{:S(2)}) copy-start(f32[64,1536]{1,0:T(8,128)} %get-tuple-element.44) | copy-start | bytes 1179652
  90.0 12.4 %collective-permute-start.1 = (f32[64,1536]{1,0:T(8,128)S(1)}, f32[64,1536]{1,0:T(8,128)S(1)}, u32[]{:S(2)}, u32[]{:S(2)}) collective-permute-start(f32[64,1536]{1,0:T(8,128)S(1)} %get-tuple-element.53), channel_id=1, source_target_pairs={{0,2},{1,3},{2,4},{3,5},{4,6},{5,7},{6,0},{7,1},{8,10},{9,11},{10,... | collective-permute-start | bytes 1179656 | tf_op jit(solution)/shard_map/ppermute | solution.py:715
  91.8 11.1 %collective-permute-start.3 = (f32[64,1536]{1,0:T(8,128)S(1)}, f32[64,1536]{1,0:T(8,128)S(1)}, u32[]{:S(2)}, u32[]{:S(2)}) collective-permute-start(f32[64,1536]{1,0:T(8,128)S(1)} %get-tuple-element.52), channel_id=1, source_target_pairs={{0,6},{1,7},{2,0},{3,1},{4,2},{5,3},{6,4},{7,5},{8,14},{9,15},{10,... | collective-permute-start | bytes 1179656 | tf_op jit(solution)/shard_map/ppermute | solution.py:716
  93.4 9.4 %copy-start = (f32[128,1536]{1,0:T(8,128)S(1)}, f32[128,1536]{1,0:T(8,128)}, u32[]{:S(2)}) copy-start(f32[128,1536]{1,0:T(8,128)} %get-tuple-element.40) | copy-start | bytes 2359300

commit v9 on v8

--- a/solution.py
+++ b/solution.py
@@ -25,9 +25,9 @@
 
 
 def layer_kernel(cfg, x_hbm, dy_hbm, ids_ref, gates_ref, w1_hbm, w3_hbm, w2_hbm,
-                 y_hbm, go_r, go_l, sr_hbm, sl_hbm, sc_hbm, xr_hbm, dr_hbm, ur_hbm, da_hbm, db_hbm, xh_hbm, dh_hbm, uh_hbm, dah_hbm, dbh_hbm,
-                 x_all, dy_all, ids_all, gates_all, rt, gt, mc, ypart, dxpart, cbuf, yra, yrb, yfl, yfr,
-                 erows, hrows, urow, uhot, darow, dbrow, act1, act2, orow, pbuf, w1, w3, w2, outb,
+                 yown, yfl, yfr, go_r, go_l, sr_hbm, sl_hbm, sc_hbm, xr_hbm, dr_hbm, ur_hbm, da_hbm, db_hbm, xh_hbm, dh_hbm, uh_hbm, dah_hbm, dbh_hbm,
+                 x_all, dy_all, ids_all, gates_all, rt, gt, mc, ypart, dxpart, cbuf, yra, yrb,
+                 erows, hrows, urow, uhot, darow, dbrow, act1, act2, orow, pbuf, w1, w3, w2,
                  m_send, m_recv, ag_send, ag_recv, rs_send, rs_recv, w_sem, st_sem, hst_sem, io_sem, so_sem, free_sem):
     chips, tok, width, hid, n_loc, cap, owner = cfg
     group = 2 * chips
@@ -311,6 +311,8 @@
     pick(2, c_r, x_all, False)
     rs(0, 3).wait_recv()
     add_rows(ypart, c, k * tok, cbuf.at[c], tok)
+    own_out = pltpu.make_async_copy(ypart.at[c, pl.ds(k * tok, tok)], yown, io_sem.at[0])
+    own_out.start()
     ag(x_all, 0, 9).wait_recv()
     ag(x_all, 0, 10).wait_recv()
     pick(3, c_o, x_all, False)
@@ -522,18 +524,6 @@
             for cpy in st_ab(e, s):
                 cpy.start()
 
-    def rs_end_y():
-        for j in (6, 7, 8, 9):
-            rs(0, j).wait_recv()
-
-        @pl.loop(0, tok // 32)
-        def _(r):
-            o = pl.multiple_of(r * 32, 32)
-            total = ypart[c, pl.ds(pl.multiple_of(k * tok + r * 32, 32), 32)] + yfl[pl.ds(o, 32)] + yfr[pl.ds(o, 32)]
-            outb[pl.ds(o, 32)] = total.astype(BF16)
-
-        return pltpu.make_async_copy(outb, y_hbm, io_sem.at[0])
-
     def chip_sums_out(j):
         q = (c_o, c_r, c_l, c)[j]
         lo = dxpart.at[q, pl.ds(k * tok, half)]
@@ -549,8 +539,8 @@
         add_rows(dxpart, q, k * tok, cbuf.at[q], tok)
         for cpy in chip_sums_out(j):
             cpy.start()
-    y_out = rs_end_y()
-    y_out.start()
+    for j in (6, 7, 8, 9):
+        rs(0, j).wait_recv()
 
     for e in range(n_loc):
         st_d(e).wait()
@@ -569,7 +559,7 @@
         rs(1, j + 10).wait_send()
         for cpy in chip_sums_out(j):
             cpy.wait()
-    y_out.wait()
+    own_out.wait()
 
 
 def expert_grads(x_ref, d_ref, u_ref, da_ref, db_ref, g1, g3, g2):
@@ -578,14 +568,17 @@
     g2[0] = dot_tn(u_ref[0], d_ref[0]).astype(BF16)
 
 
-def first_grads_kernel(owner, x_ref, d_ref, u_ref, da_ref, db_ref, xh, dh, uh, dah, dbh, y_ref, g1, g3, g2, y_out, xb, dbuf, ub, dab, dbb, sem):
+def first_grads_kernel(owner, x_ref, d_ref, u_ref, da_ref, db_ref, xh, dh, uh, dah, dbh, own_ref, fl_ref, fr_ref, g1, g3, g2, y_out, xb, dbuf, ub, dab, dbb, sem):
     i = pl.program_id(0)
-    y_out[...] = y_ref[...]
     is_owner = lax.axis_index("ep") == owner
     hot = jnp.logical_and(is_owner, i == pl.num_programs(0) - 1)
 
     def copies():
         return [pltpu.make_async_copy(src, dst, sem.at[j]) for j, (src, dst) in enumerate(((xh, xb), (dah, dab), (dbh, dbb), (uh, ub), (dh, dbuf)))]
+
+    @pl.when(i == 0)
+    def _():
+        y_out[...] = (own_ref[...] + fl_ref[...] + fr_ref[...]).astype(BF16)
 
     @pl.when(jnp.logical_and(is_owner, i == 0))
     def _():
@@ -640,13 +633,13 @@
             outs = pl.pallas_call(
                 functools.partial(layer_kernel, cfg),
                 out_shape=(
-                    sds((tok, width), BF16), *[sds((tok, width), F32)] * 2, *[sds((half, width), F32)] * 2, sds((tok, width), F32),
+                    *[sds((tok, width), F32)] * 5, *[sds((half, width), F32)] * 2, sds((tok, width), F32),
                     sds((n_loc, n_rows, width), BF16), sds((n_loc, n_rows, width), BF16),
                     sds((n_loc, n_rows, hid), BF16), sds((n_loc, n_rows, hid), BF16), sds((n_loc, n_rows, hid), BF16),
                     sds((hot_rows, width), BF16), sds((hot_rows, width), BF16),
                     sds((hot_rows, hid), BF16), sds((hot_rows, hid), BF16), sds((hot_rows, hid), BF16)),
                 in_specs=[any_spec, any_spec, vmem_spec, vmem_spec, any_spec, any_spec, any_spec],
-                out_specs=[any_spec] * 16,
+                out_specs=[any_spec] * 18,
                 scratch_shapes=[
                     pltpu.VMEM((chips, 2 * tok, width), BF16), pltpu.VMEM((chips, 2 * tok, width), BF16),
                     pltpu.VMEM((group, top_k, tok), jnp.int32), pltpu.VMEM((group, top_k, tok), F32),
@@ -655,14 +648,12 @@
                     pltpu.VMEM((chips, 2 * tok, width), F32), pltpu.VMEM((chips, 2 * tok, width), F32),
                     pltpu.VMEM((chips, tok, width), F32),
                     pltpu.VMEM((half, width), F32), pltpu.VMEM((half, width), F32),
-                    pltpu.VMEM((tok, width), F32), pltpu.VMEM((tok, width), F32),
                     pltpu.VMEM((n_loc, n_rows, width), BF16), pltpu.VMEM((hb, width), BF16),
                     pltpu.VMEM((n_loc, n_rows, hid), BF16), pltpu.VMEM((hot_rows, hid), BF16),
                     pltpu.VMEM((2, hb, hid), BF16), pltpu.VMEM((2, hb, hid), BF16),
                     pltpu.VMEM((act_rows, hid), F32), pltpu.VMEM((act_rows, hid), F32),
                     pltpu.VMEM((hb + n_rows, width), BF16), pltpu.VMEM((n_loc * 2 * cap, 2 * tok), BF16),
                     pltpu.VMEM((2, width, hid), BF16), pltpu.VMEM((2, width, hid), BF16), pltpu.VMEM((2, hid, width), BF16),
-                    pltpu.VMEM((tok, width), BF16),
                     pltpu.SemaphoreType.DMA((2, group)), pltpu.SemaphoreType.DMA((2, group)),
                     pltpu.SemaphoreType.DMA((2, 11)), pltpu.SemaphoreType.DMA((2, 11)),
                     pltpu.SemaphoreType.DMA((2, 14)), pltpu.SemaphoreType.DMA((2, 14)),
@@ -672,7 +663,7 @@
                 compiler_params=pltpu.CompilerParams(collective_id=0, has_side_effects=True, vmem_limit_bytes=67043328),
                 name="moe_layer",
             )(x, dy, ids.T, gates.T, w1, w3, w2)
-            y, go_r, go_l, sr, sl, sc, xr, dr, ur, dar, dbr, xh, dh, uh, dah, dbh = outs
+            yown, yfl, yfr, go_r, go_l, sr, sl, sc, xr, dr, ur, dar, dbr, xh, dh, uh, dah, dbh = outs
 
             to_right = [(i, (i + 2) % group) for i in range(group)]
             to_left = [(i, (i + group - 2) % group) for i in range(group)]
@@ -705,12 +696,12 @@
             *grads, y = pl.pallas_call(
                 functools.partial(first_grads_kernel, owner),
                 grid=(n_first,), out_shape=g_shapes + (sds((tok, width), BF16),),
-                in_specs=row_specs(first_at) + [any_spec] * 5 + [y_spec], out_specs=out_blks(first_at) + [y_spec],
+                in_specs=row_specs(first_at) + [any_spec] * 5 + [y_spec] * 3, out_specs=out_blks(first_at) + [y_spec],
                 scratch_shapes=[pltpu.VMEM((hot_rows, width), BF16), pltpu.VMEM((hot_rows, width), BF16), pltpu.VMEM((hot_rows, hid), BF16),
                                 pltpu.VMEM((hot_rows, hid), BF16), pltpu.VMEM((hot_rows, hid), BF16), pltpu.SemaphoreType.DMA((5,))],
                 compiler_params=pltpu.CompilerParams(vmem_limit_bytes=60 << 20),
                 cost_estimate=cost(n_first), name="first_grads",
-            )(xr, dr, ur, dar, dbr, xh, dh, uh, dah, dbh, y)
+            )(xr, dr, ur, dar, dbr, xh, dh, uh, dah, dbh, yown, yfl, yfr)
 
             fl_lo = lax.ppermute(sr + from_l[:half], "ep", to_right)
             fr_hi = lax.ppermute(sl + from_r[:half], "ep", to_left)

time: 104 us -> 104 us (level)
  transfers between devices with their start and end apart: 4 -> 4, of which waited for: 3 -> 3; matrix products, arithmetic and copies ran while one was open for 0% -> 0% of each run, Pallas kernels for 23% -> 24%
where the time goes in v9:
time: 104 us
  Pallas kernels  93.4 us (90%)
  starting transfers between devices  6.39 us (6%)
  waiting for transfers between devices  2.49 us (2%)
    pallas_call x1, Pallas kernels, device_fn(): pl.pallas_call(functools.partial(layer_kernel, cfg), out_shape=(*[sds((to...  68.7 us
    pallas_call x1, Pallas kernels, device_fn(): pl.pallas_call(functools.partial(first_grads_kernel, owner), grid=(n_firs...  15.8 us
    pallas_call x1, Pallas kernels, device_fn(): pl.pallas_call(later_grads_kernel, grid=(n_loc - n_first,), out_shape=g_s...  8.93 us
  transfers between devices with their start and end apart: 4, of which 3 were waited for; matrix products, arithmetic and copies ran while one was open for 0% of the time, Pallas kernels for 24%

profile of v9, /device:TPU:112, one launch (start us, length us, event | category | flops | bytes accessed | tf_op | source)
XLA Modules:
  0.0 104.0 jit_solution(16571055703726034081)
XLA Ops:
  0.6 68.7 %moe_layer.1 = (f32[128,1536]{1,0:T(8,128)}, f32[128,1536]{1,0:T(8,128)}, f32[128,1536]{1,0:T(8,128)}, f32[128,1536]{1,0:T(8,128)}, f32[128,1536]{1,0:T(8,128)},...) custom-call(bf16[128,1536]{1,0:T(8,128)(2,1)} %x_hbm.1, ...), custom_call_target="tpu_custom_call" | custom-call | tf_op jit(solution)/shard_map/moe_layer/pallas_call | solution.py:633
  69.4 1.2 %collective-permute-start = (f32[128,1536]{1,0:T(8,128)}, f32[128,1536]{1,0:T(8,128)S(1)}, u32[]{:S(2)}, u32[]{:S(2)}) collective-permute-start(f32[128,1536]{1,0:T(8,128)} %get-tuple-element.46), channel_id=1, source_target_pairs={{0,2},{1,3},{2,4},{3,5},{4,6},{5,7},{6,0},{7,1},{8,10},{9,11},{10,... | collective-permute-start | bytes 2359304 | tf_op jit(solution)/shard_map/ppermute | solution.py:670
  70.6 2.1 %collective-permute-start.2 = (f32[128,1536]{1,0:T(8,128)}, f32[128,1536]{1,0:T(8,128)S(1)}, u32[]{:S(2)}, u32[]{:S(2)}) collective-permute-start(f32[128,1536]{1,0:T(8,128)} %get-tuple-element.47), channel_id=1, source_target_pairs={{0,6},{1,7},{2,0},{3,1},{4,2},{5,3},{6,4},{7,5},{8,14},{9,15},{10,... | collective-permute-start | bytes 2359304 | tf_op jit(solution)/shard_map/ppermute | solution.py:671
  72.7 0.0 copy-start.2
  72.7 0.0 copy-start.1
  72.7 15.8 %first_grads.1 = (bf16[5,1536,512]{2,1,0:T(8,128)(2,1)}, bf16[5,1536,512]{2,1,0:T(8,128)(2,1)}, bf16[5,512,1536]{2,1,0:T(8,128)(2,1)}, bf16[128,1536]{1,0:T(8,128)(2,1)}) custom-call(bf16[5,448,1536]{2,1,0:T(8,128)(2,1)} %get-tuple-element.30.x_ref, bf16[5,448,1536]{2,1,0:T(8,128)(2,1)} %get-tuple-element.31.d_ref, ...), custom_call_target="tpu_custom_call" | custom-call | flops 6341787648 | bytes 26542080 | tf_op jit(solution)/shard_map/first_grads/pallas_call | solution.py:696
  88.5 1.3 %collective-permute-done = f32[128,1536]{1,0:T(8,128)S(1)} collective-permute-done((f32[128,1536]{1,0:T(8,128)}, f32[128,1536]{1,0:T(8,128)S(1)}, u32[]{:S(2)}, u32[]{:S(2)}) %collective-permute-start) | collective-permute-done | bytes 786464 | tf_op jit(solution)/shard_map/ppermute | solution.py:670
  89.8 0.0 copy-done.2
  89.8 0.1 slice_add_fusion.1
  89.9 1.1 %collective-permute-start.1 = (f32[64,1536]{1,0:T(8,128)S(1)}, f32[64,1536]{1,0:T(8,128)S(1)}, u32[]{:S(2)}, u32[]{:S(2)}) collective-permute-start(f32[64,1536]{1,0:T(8,128)S(1)} %get-tuple-element.57), channel_id=1, source_target_pairs={{0,2},{1,3},{2,4},{3,5},{4,6},{5,7},{6,0},{7,1},{8,10},{9,11},{10,... | collective-permute-start | bytes 1179656 | tf_op jit(solution)/shard_map/ppermute | solution.py:706
  90.9 0.3 collective-permute-done.2
  91.3 0.0 copy-done.1
  91.3 0.1 fusion.2
  91.3 2.0 %collective-permute-start.3 = (f32[64,1536]{1,0:T(8,128)S(1)}, f32[64,1536]{1,0:T(8,128)S(1)}, u32[]{:S(2)}, u32[]{:S(2)}) collective-permute-start(f32[64,1536]{1,0:T(8,128)S(1)} %get-tuple-element.56), channel_id=1, source_target_pairs={{0,6},{1,7},{2,0},{3,1},{4,2},{5,3},{6,4},{7,5},{8,14},{9,15},{10,... | collective-permute-start | bytes 1179656 | tf_op jit(solution)/shard_map/ppermute | solution.py:707
  93.3 0.0 copy-start
  93.3 8.9 %later_grads.1 = (bf16[5,1536,512]{2,1,0:T(8,128)(2,1)}, bf16[5,1536,512]{2,1,0:T(8,128)(2,1)}, bf16[5,512,1536]{2,1,0:T(8,128)(2,1)}) custom-call(bf16[5,448,1536]{2,1,0:T(8,128)(2,1)} %get-tuple-element.30.x_ref, bf16[5,448,1536]{2,1,0:T(8,128)(2,1)} %get-tuple-element.31.d_ref, ...), custom_call_target="tpu_custom_call", output_to_operand_aliasing={{0}: (5, {}), {1}: (6, {}), {2}: (7, {})} | custom-call | flops 4227858432 | bytes 17694720 | tf_op jit(solution)/shard_map/later_grads/pallas_call | solution.py:708
  102.3 0.0 collective-permute-done.1
  102.3 0.9 collective-permute-done.3
  103.1 0.0 copy-done
  103.1 0.9 fusion.1
Async XLA Ops:
  69.4 20.4 %collective-permute-start = (f32[128,1536]{1,0:T(8,128)}, f32[128,1536]{1,0:T(8,128)S(1)}, u32[]{:S(2)}, u32[]{:S(2)}) collective-permute-start(f32[128,1536]{1,0:T(8,128)} %get-tuple-element.46), channel_id=1, source_target_pairs={{0,2},{1,3},{2,4},{3,5},{4,6},{5,7},{6,0},{7,1},{8,10},{9,11},{10,... | collective-permute-start | bytes 2359304 | tf_op jit(solution)/shard_map/ppermute | solution.py:670
  70.6 20.6 %collective-permute-start.2 = (f32[128,1536]{1,0:T(8,128)}, f32[128,1536]{1,0:T(8,128)S(1)}, u32[]{:S(2)}, u32[]{:S(2)}) collective-permute-start(f32[128,1536]{1,0:T(8,128)} %get-tuple-element.47), channel_id=1, source_target_pairs={{0,6},{1,7},{2,0},{3,1},{4,2},{5,3},{6,4},{7,5},{8,14},{9,15},{10,... | collective-permute-start | bytes 2359304 | tf_op jit(solution)/shard_map/ppermute | solution.py:671
  72.7 17.1 %copy-start.2 = (f32[64,1536]{1,0:T(8,128)S(1)}, f32[64,1536]{1,0:T(8,128)}, u32[]{:S(2)}) copy-start(f32[64,1536]{1,0:T(8,128)} %get-tuple-element.45) | copy-start | bytes 1179652
  72.7 18.6 %copy-start.1 = (f32[64,1536]{1,0:T(8,128)S(1)}, f32[64,1536]{1,0:T(8,128)}, u32[]{:S(2)}) copy-start(f32[64,1536]{1,0:T(8,128)} %get-tuple-element.48) | copy-start | bytes 1179652
  89.9 12.4 %collective-permute-start.1 = (f32[64,1536]{1,0:T(8,128)S(1)}, f32[64,1536]{1,0:T(8,128)S(1)}, u32[]{:S(2)}, u32[]{:S(2)}) collective-permute-start(f32[64,1536]{1,0:T(8,128)S(1)} %get-tuple-element.57), channel_id=1, source_target_pairs={{0,2},{1,3},{2,4},{3,5},{4,6},{5,7},{6,0},{7,1},{8,10},{9,11},{10,... | collective-permute-start | bytes 1179656 | tf_op jit(solution)/shard_map/ppermute | solution.py:706
  91.3 11.8 %collective-permute-start.3 = (f32[64,1536]{1,0:T(8,128)S(1)}, f32[64,1536]{1,0:T(8,128)S(1)}, u32[]{:S(2)}, u32[]{:S(2)}) collective-permute-start(f32[64,1536]{1,0:T(8,128)S(1)} %get-tuple-element.56), channel_id=1, source_target_pairs={{0,6},{1,7},{2,0},{3,1},{4,2},{5,3},{6,4},{7,5},{8,14},{9,15},{10,... | collective-permute-start | bytes 1179656 | tf_op jit(solution)/shard_map/ppermute | solution.py:707
  93.3 9.8 %copy-start = (f32[128,1536]{1,0:T(8,128)S(1)}, f32[128,1536]{1,0:T(8,128)}, u32[]{:S(2)}) copy-start(f32[128,1536]{1,0:T(8,128)} %get-tuple-element.44) | copy-start | bytes 2359300

commit v10 on v9

--- a/solution.py
+++ b/solution.py
@@ -568,7 +568,7 @@
     g2[0] = dot_tn(u_ref[0], d_ref[0]).astype(BF16)
 
 
-def first_grads_kernel(owner, x_ref, d_ref, u_ref, da_ref, db_ref, xh, dh, uh, dah, dbh, own_ref, fl_ref, fr_ref, g1, g3, g2, y_out, xb, dbuf, ub, dab, dbb, sem):
+def first_grads_kernel(owner, x_ref, d_ref, u_ref, da_ref, db_ref, xh, dh, uh, dah, dbh, own_hbm, fl_hbm, fr_hbm, g1, g3, g2, y_out, xb, dbuf, ub, dab, dbb, parts, sem, y_sem):
     i = pl.program_id(0)
     is_owner = lax.axis_index("ep") == owner
     hot = jnp.logical_and(is_owner, i == pl.num_programs(0) - 1)
@@ -576,9 +576,19 @@
     def copies():
         return [pltpu.make_async_copy(src, dst, sem.at[j]) for j, (src, dst) in enumerate(((xh, xb), (dah, dab), (dbh, dbb), (uh, ub), (dh, dbuf)))]
 
+    def y_copies():
+        return [pltpu.make_async_copy(src, parts.at[j], y_sem.at[j]) for j, src in enumerate((own_hbm, fl_hbm, fr_hbm))]
+
     @pl.when(i == 0)
     def _():
-        y_out[...] = (own_ref[...] + fl_ref[...] + fr_ref[...]).astype(BF16)
+        for cpy in y_copies():
+            cpy.start()
+
+    @pl.when(i == pl.num_programs(0) - 1)
+    def _():
+        for cpy in y_copies():
+            cpy.wait()
+        y_out[...] = (parts[0] + parts[1] + parts[2]).astype(BF16)
 
     @pl.when(jnp.logical_and(is_owner, i == 0))
     def _():
@@ -696,9 +706,10 @@
             *grads, y = pl.pallas_call(
                 functools.partial(first_grads_kernel, owner),
                 grid=(n_first,), out_shape=g_shapes + (sds((tok, width), BF16),),
-                in_specs=row_specs(first_at) + [any_spec] * 5 + [y_spec] * 3, out_specs=out_blks(first_at) + [y_spec],
+                in_specs=row_specs(first_at) + [any_spec] * 8, out_specs=out_blks(first_at) + [y_spec],
                 scratch_shapes=[pltpu.VMEM((hot_rows, width), BF16), pltpu.VMEM((hot_rows, width), BF16), pltpu.VMEM((hot_rows, hid), BF16),
-                                pltpu.VMEM((hot_rows, hid), BF16), pltpu.VMEM((hot_rows, hid), BF16), pltpu.SemaphoreType.DMA((5,))],
+                                pltpu.VMEM((hot_rows, hid), BF16), pltpu.VMEM((hot_rows, hid), BF16), pltpu.VMEM((3, tok, width), F32),
+                                pltpu.SemaphoreType.DMA((5,)), pltpu.SemaphoreType.DMA((3,))],
                 compiler_params=pltpu.CompilerParams(vmem_limit_bytes=60 << 20),
                 cost_estimate=cost(n_first), name="first_grads",
             )(xr, dr, ur, dar, dbr, xh, dh, uh, dah, dbh, yown, yfl, yfr)

time: 104 us -> 104 us (level)
  Pallas kernels: 93.4 us -> 92.2 us
  waiting for transfers between devices: 2.49 us -> 3.69 us
    ppermute x1, waiting for transfers between devices: 1.31 us -> 2.51 us  [device_fn(): from_l = lax.ppermute(go_r, 'ep', to_right)]
    pallas_call x1, Pallas kernels: 15.8 us -> 14.6 us  [device_fn(): pl.pallas_call(functools.partial(first_grads_kernel, owner), grid=(n_firs...]
  transfers between devices with their start and end apart: 4 -> 4, of which waited for: 3 -> 3; matrix products, arithmetic and copies ran while one was open for 0% -> 0% of each run, Pallas kernels for 24% -> 23%
where the time goes in v10:
time: 104 us
  Pallas kernels  92.2 us (89%)
  starting transfers between devices  6.39 us (6%)
  waiting for transfers between devices  3.69 us (4%)
    pallas_call x1, Pallas kernels, device_fn(): pl.pallas_call(functools.partial(layer_kernel, cfg), out_shape=(*[sds((to...  68.7 us
    pallas_call x1, Pallas kernels, device_fn(): pl.pallas_call(functools.partial(first_grads_kernel, owner), grid=(n_firs...  14.6 us
    pallas_call x1, Pallas kernels, device_fn(): pl.pallas_call(later_grads_kernel, grid=(n_loc - n_first,), out_shape=g_s...  8.93 us
    ppermute x1, waiting for transfers between devices, device_fn(): from_l = lax.ppermute(go_r, 'ep', to_right)  2.51 us
  transfers between devices with their start and end apart: 4, of which 3 were waited for; matrix products, arithmetic and copies ran while one was open for 0% of the time, Pallas kernels for 23%

profile of v10, /device:TPU:112, one launch (start us, length us, event | category | flops | bytes accessed | tf_op | source)
XLA Modules:
  0.0 104.0 jit_solution(18216729776528319821)
XLA Ops:
  0.6 68.7 %moe_layer.1 = (f32[128,1536]{1,0:T(8,128)}, f32[128,1536]{1,0:T(8,128)}, f32[128,1536]{1,0:T(8,128)}, f32[128,1536]{1,0:T(8,128)}, f32[128,1536]{1,0:T(8,128)},...) custom-call(bf16[128,1536]{1,0:T(8,128)(2,1)} %x_hbm.1, ...), custom_call_target="tpu_custom_call" | custom-call | tf_op jit(solution)/shard_map/moe_layer/pallas_call | solution.py:643
  69.4 1.2 %collective-permute-start = (f32[128,1536]{1,0:T(8,128)}, f32[128,1536]{1,0:T(8,128)S(1)}, u32[]{:S(2)}, u32[]{:S(2)}) collective-permute-start(f32[128,1536]{1,0:T(8,128)} %get-tuple-element.46), channel_id=1, source_target_pairs={{0,2},{1,3},{2,4},{3,5},{4,6},{5,7},{6,0},{7,1},{8,10},{9,11},{10,... | collective-permute-start | bytes 2359304 | tf_op jit(solution)/shard_map/ppermute | solution.py:680
  70.6 2.1 %collective-permute-start.2 = (f32[128,1536]{1,0:T(8,128)}, f32[128,1536]{1,0:T(8,128)S(1)}, u32[]{:S(2)}, u32[]{:S(2)}) collective-permute-start(f32[128,1536]{1,0:T(8,128)} %get-tuple-element.47), channel_id=1, source_target_pairs={{0,6},{1,7},{2,0},{3,1},{4,2},{5,3},{6,4},{7,5},{8,14},{9,15},{10,... | collective-permute-start | bytes 2359304 | tf_op jit(solution)/shard_map/ppermute | solution.py:681
  72.7 0.0 copy-start.2
  72.7 0.0 copy-start.1
  72.7 14.6 %first_grads.1 = (bf16[5,1536,512]{2,1,0:T(8,128)(2,1)}, bf16[5,1536,512]{2,1,0:T(8,128)(2,1)}, bf16[5,512,1536]{2,1,0:T(8,128)(2,1)}, bf16[128,1536]{1,0:T(8,128)(2,1)}) custom-call(bf16[5,448,1536]{2,1,0:T(8,128)(2,1)} %get-tuple-element.30.x_ref, bf16[5,448,1536]{2,1,0:T(8,128)(2,1)} %get-tuple-element.31.d_ref, ...), custom_call_target="tpu_custom_call" | custom-call | flops 6341787648 | bytes 26542080 | tf_op jit(solution)/shard_map/first_grads/pallas_call | solution.py:706
  87.3 2.5 %collective-permute-done = f32[128,1536]{1,0:T(8,128)S(1)} collective-permute-done((f32[128,1536]{1,0:T(8,128)}, f32[128,1536]{1,0:T(8,128)S(1)}, u32[]{:S(2)}, u32[]{:S(2)}) %collective-permute-start) | collective-permute-done | bytes 786464 | tf_op jit(solution)/shard_map/ppermute | solution.py:680
  89.8 0.0 copy-done.2
  89.8 0.1 slice_add_fusion.1
  89.9 1.1 %collective-permute-start.1 = (f32[64,1536]{1,0:T(8,128)S(1)}, f32[64,1536]{1,0:T(8,128)S(1)}, u32[]{:S(2)}, u32[]{:S(2)}) collective-permute-start(f32[64,1536]{1,0:T(8,128)S(1)} %get-tuple-element.57), channel_id=1, source_target_pairs={{0,2},{1,3},{2,4},{3,5},{4,6},{5,7},{6,0},{7,1},{8,10},{9,11},{10,... | collective-permute-start | bytes 1179656 | tf_op jit(solution)/shard_map/ppermute | solution.py:717
  90.9 0.3 collective-permute-done.2
  91.3 0.0 copy-done.1
  91.3 0.1 fusion.2
  91.3 2.0 %collective-permute-start.3 = (f32[64,1536]{1,0:T(8,128)S(1)}, f32[64,1536]{1,0:T(8,128)S(1)}, u32[]{:S(2)}, u32[]{:S(2)}) collective-permute-start(f32[64,1536]{1,0:T(8,128)S(1)} %get-tuple-element.56), channel_id=1, source_target_pairs={{0,6},{1,7},{2,0},{3,1},{4,2},{5,3},{6,4},{7,5},{8,14},{9,15},{10,... | collective-permute-start | bytes 1179656 | tf_op jit(solution)/shard_map/ppermute | solution.py:718
  93.3 0.0 copy-start
  93.3 8.9 %later_grads.1 = (bf16[5,1536,512]{2,1,0:T(8,128)(2,1)}, bf16[5,1536,512]{2,1,0:T(8,128)(2,1)}, bf16[5,512,1536]{2,1,0:T(8,128)(2,1)}) custom-call(bf16[5,448,1536]{2,1,0:T(8,128)(2,1)} %get-tuple-element.30.x_ref, bf16[5,448,1536]{2,1,0:T(8,128)(2,1)} %get-tuple-element.31.d_ref, ...), custom_call_target="tpu_custom_call", output_to_operand_aliasing={{0}: (5, {}), {1}: (6, {}), {2}: (7, {})} | custom-call | flops 4227858432 | bytes 17694720 | tf_op jit(solution)/shard_map/later_grads/pallas_call | solution.py:719
  102.3 0.0 collective-permute-done.1
  102.3 0.9 collective-permute-done.3
  103.1 0.0 copy-done
  103.1 0.9 fusion.1
Async XLA Ops:
  69.4 20.4 %collective-permute-start = (f32[128,1536]{1,0:T(8,128)}, f32[128,1536]{1,0:T(8,128)S(1)}, u32[]{:S(2)}, u32[]{:S(2)}) collective-permute-start(f32[128,1536]{1,0:T(8,128)} %get-tuple-element.46), channel_id=1, source_target_pairs={{0,2},{1,3},{2,4},{3,5},{4,6},{5,7},{6,0},{7,1},{8,10},{9,11},{10,... | collective-permute-start | bytes 2359304 | tf_op jit(solution)/shard_map/ppermute | solution.py:680
  70.6 20.6 %collective-permute-start.2 = (f32[128,1536]{1,0:T(8,128)}, f32[128,1536]{1,0:T(8,128)S(1)}, u32[]{:S(2)}, u32[]{:S(2)}) collective-permute-start(f32[128,1536]{1,0:T(8,128)} %get-tuple-element.47), channel_id=1, source_target_pairs={{0,6},{1,7},{2,0},{3,1},{4,2},{5,3},{6,4},{7,5},{8,14},{9,15},{10,... | collective-permute-start | bytes 2359304 | tf_op jit(solution)/shard_map/ppermute | solution.py:681
  72.7 17.1 %copy-start.2 = (f32[64,1536]{1,0:T(8,128)S(1)}, f32[64,1536]{1,0:T(8,128)}, u32[]{:S(2)}) copy-start(f32[64,1536]{1,0:T(8,128)} %get-tuple-element.45) | copy-start | bytes 1179652
  72.7 18.6 %copy-start.1 = (f32[64,1536]{1,0:T(8,128)S(1)}, f32[64,1536]{1,0:T(8,128)}, u32[]{:S(2)}) copy-start(f32[64,1536]{1,0:T(8,128)} %get-tuple-element.48) | copy-start | bytes 1179652
  89.9 12.4 %collective-permute-start.1 = (f32[64,1536]{1,0:T(8,128)S(1)}, f32[64,1536]{1,0:T(8,128)S(1)}, u32[]{:S(2)}, u32[]{:S(2)}) collective-permute-start(f32[64,1536]{1,0:T(8,128)S(1)} %get-tuple-element.57), channel_id=1, source_target_pairs={{0,2},{1,3},{2,4},{3,5},{4,6},{5,7},{6,0},{7,1},{8,10},{9,11},{10,... | collective-permute-start | bytes 1179656 | tf_op jit(solution)/shard_map/ppermute | solution.py:717
  91.3 11.8 %collective-permute-start.3 = (f32[64,1536]{1,0:T(8,128)S(1)}, f32[64,1536]{1,0:T(8,128)S(1)}, u32[]{:S(2)}, u32[]{:S(2)}) collective-permute-start(f32[64,1536]{1,0:T(8,128)S(1)} %get-tuple-element.56), channel_id=1, source_target_pairs={{0,6},{1,7},{2,0},{3,1},{4,2},{5,3},{6,4},{7,5},{8,14},{9,15},{10,... | collective-permute-start | bytes 1179656 | tf_op jit(solution)/shard_map/ppermute | solution.py:718
  93.3 9.8 %copy-start = (f32[128,1536]{1,0:T(8,128)S(1)}, f32[128,1536]{1,0:T(8,128)}, u32[]{:S(2)}) copy-start(f32[128,1536]{1,0:T(8,128)} %get-tuple-element.44) | copy-start | bytes 2359300
